TPU v7x, 512 devices: a whole 4x4x16 slice. The times are simulated.
512 devices in a mesh: rows: 32 (over z, core), ch: 16 (over y, x).
Axes of the slice: x: 4, y: 4, z: 16, core: 2. Of those that a mesh axis runs over, the one named last changes fastest.
Arguments:
- features: bfloat16 [128, 256, 8192], P('rows', None, 'ch'), may hold values from -6 to 6
- conv_weight: bfloat16 [3, 3, 256, 256], P(None, None, 'ch'), may hold values from -0.125 to 0.125
- cotangent: bfloat16 [128, 256, 8192], P('rows', None, 'ch'), may hold values from -6 to 6
- valid_rows: int32 [64], replicated, may hold values from 64 to 128
Outputs:
- input_grad: bfloat16 [128, 256, 8192], P('rows', None, 'ch')
- weight_grad: float32 [3, 3, 256, 256], P(None, None, 'ch')
All inputs are finite; a program needn't handle non-finite values.
Results may differ from a plain program's by a relative error of at most 0.0049.
Values may be sent and summed in bfloat16 or wider, within the bound.
No kernel may reach another device: no remote copies, remote signals or barrier semaphores. Data moves between devices by JAX's collectives and lax.ppermute only.
A program may use at most 64 MiB of HBM per device.

v0:
```python
import jax
import jax.numpy as jnp
from jax import lax
from jax.sharding import Mesh
from jax.sharding import PartitionSpec as P

COLS = 128
CH = ("ch_0", "ch_1")
ROWS = ("rows_0", "rows_1")


def laid_out(parts, dim):
    parts = jnp.moveaxis(parts, 0, dim)
    shape = parts.shape
    return parts.reshape(*shape[:dim], shape[dim] * shape[dim + 1], *shape[dim + 2 :])


def from_everyone(array, axis):
    peers = lax.axis_size(axis)
    return lax.all_to_all(
        jnp.broadcast_to(array[None], (peers, *array.shape)), axis, 0, 0, tiled=True
    )


def collect(array, axis, dim):
    return laid_out(from_everyone(array, axis), dim)


def padded_2(block, sides, width):
    for axis, dim in sides:
        count = lax.axis_size(axis)
        forward = [(i, i + 1) for i in range(count - 1)]
        backward = [(target, source) for source, target in forward]
        low = lax.ppermute(
            lax.slice_in_dim(block, block.shape[dim] - width, None, axis=dim), axis, forward
        )
        high = lax.ppermute(lax.slice_in_dim(block, 0, width, axis=dim), axis, backward)
        block = jnp.concatenate([low, block, high], axis=dim)
    return block


def filled_up(lines, peers):
    spare = -lines.shape[0] % peers
    if not spare:
        return lines
    return jnp.concatenate([lines, jnp.zeros((spare, *lines.shape[1:]), lines.dtype)])


def whole_of(array, axes, dim):
    far, near = axes
    parts = from_everyone(from_everyone(array, far), near)
    return laid_out(parts.swapaxes(0, 1).reshape(-1, *array.shape), dim)


def cut_along(array, dim, peers):
    shape = array.shape
    parts = array.reshape(*shape[:dim], peers, shape[dim] // peers, *shape[dim + 1 :])
    return jnp.moveaxis(parts, dim, 0)


def sent_and_summed(array, axis, dim):
    parts = cut_along(array, dim, lax.axis_size(axis))
    arrived = lax.all_to_all(parts, axis, split_axis=0, concat_axis=0, tiled=True)
    return arrived.sum(axis=0)


def sum_in_two_steps(array, axes, dim):
    far, near = axes
    parts = cut_along(array, dim, lax.axis_size(far))
    nearer = sent_and_summed(parts, near, dim + 1)
    arrived = lax.all_to_all(nearer, far, split_axis=0, concat_axis=0, tiled=True)
    return arrived.sum(axis=0)


def total_of(array, axes):
    lines = array.reshape(-1)
    padded = filled_up(lines, lax.axis_size(axes[0]) * lax.axis_size(axes[1]))
    whole = whole_of(sum_in_two_steps(padded, axes, 0), axes, 0)
    return lax.slice_in_dim(whole, 0, len(lines)).reshape(array.shape)


def shift_cols(field, across, columns):
    if across == 0:
        return field
    length = field.shape[-1]
    widths = [(0, 0)] * (field.ndim - 1) + [(1, 1)]
    padded = jnp.pad(field, widths)
    moved = padded[..., 1 + across : 1 + across + length]
    position = jnp.arange(length).astype(jnp.int32) % columns + across
    inside = (position >= 0) & (position < columns)
    return jnp.where(inside, moved, jnp.zeros_like(moved))


def body(features, conv_weight, cotangent, valid_rows):
    band = features.shape[0]
    total_ch = features.shape[1]
    cells = features.shape[2]
    columns = COLS
    img_count = cells // columns
    local_out = conv_weight.shape[2]
    kernel = collect(conv_weight, CH, 2)
    padded = padded_2(features, ((ROWS, 0),), 1)
    summed = jnp.zeros(features.shape, jnp.float32)
    for offset_row in range(3):
        for offset_col in range(3):
            window = shift_cols(padded[offset_row : offset_row + band], offset_col - 1, columns)
            summed = summed + jnp.einsum(
                "hik,oi->hok",
                window,
                kernel[offset_row, offset_col],
                preferred_element_type=jnp.float32,
            )
    center = jnp.sum(summed, 1) / total_ch
    inverse = lax.rsqrt(jnp.sum(summed * summed, 1) / total_ch - center * center + 1e-06)
    normed = (summed - center[:, None, :]) * inverse[:, None, :]
    row_ids = lax.axis_index(ROWS) * band + jnp.arange(band)
    local_limits = lax.dynamic_slice_in_dim(
        valid_rows, lax.axis_index(CH) * img_count, img_count, 0
    )
    limits = jnp.repeat(local_limits, columns, total_repeat_length=cells)
    keep = (row_ids[:, None] < limits[None, :]).astype(jnp.float32)
    masked = cotangent.astype(jnp.float32) * keep[:, None, :]
    grad_total = jnp.sum(masked, 1)
    grad_cross = jnp.sum(masked * normed, 1)
    grad_pre = (
        inverse[:, None, :]
        * (
            masked
            - (grad_total / total_ch)[:, None, :]
            - normed * (grad_cross / total_ch)[:, None, :]
        )
    ).astype(jnp.bfloat16)
    taps = []
    for offset_row in range(3):
        for offset_col in range(3):
            window = shift_cols(padded[offset_row : offset_row + band], offset_col - 1, columns)
            taps.append(
                jnp.einsum("hik,hok->oi", window, grad_pre, preferred_element_type=jnp.float32)
            )
    weight_part = jnp.stack(taps).reshape((3, 3, total_ch, total_ch))
    summed_all = total_of(weight_part, (("rows_0", "rows_1"), ("ch_0", "ch_1")))
    weight_grad = lax.dynamic_slice_in_dim(summed_all, lax.axis_index(CH) * local_out, local_out, 2)
    grad_padded = padded_2(grad_pre, ((ROWS, 0),), 1)
    input_sum = jnp.zeros(features.shape, jnp.float32)
    for offset_row in range(3):
        for offset_col in range(3):
            window = shift_cols(
                grad_padded[2 - offset_row : 2 - offset_row + band], 1 - offset_col, columns
            )
            input_sum = input_sum + jnp.einsum(
                "hok,oi->hik",
                window,
                kernel[offset_row, offset_col],
                preferred_element_type=jnp.float32,
            )
    return (input_sum.astype(jnp.bfloat16), weight_grad)


def solution(mesh):
    split = Mesh(mesh.devices.reshape(16, 2, 4, 4), ("rows_0", "rows_1", "ch_0", "ch_1"))
    placed = (P(ROWS, None, CH), P(None, None, CH, None), P(ROWS, None, CH), P())
    return jax.shard_map(
        body,
        mesh=split,
        in_specs=placed,
        out_specs=(P(ROWS, None, CH), P(None, None, CH, None)),
        check_vma=False,
    )
```

profile of v0, /device:TPU:64, one launch (start us, length us, event | category | flops | bytes accessed | tf_op | source)
XLA Modules:
  0.0 207.8 jit_solution(9543383644601922551)
XLA Ops:
  0.6 1.5 copy.58
  2.2 2.1 collective-permute-start
  4.3 3.6 %collective-permute-start.1 = (bf16[1,256,512]{1,2,0:T(8,128)(2,1)S(1)}, bf16[1,256,512]{1,2,0:T(8,128)(2,1)S(1)}, u32[]{:S(2)}, u32[]{:S(2)}) collective-permute-start(bf16[1,256,512]{1,2,0:T(8,128)(2,1)S(1)} %get-tuple-element.31), channel_id=1, source_target_pairs={{16,0},{32,16},{48,32},{64,48},{80,64},{96,80},{112,96},{128,112},... | collective-permute-start | bytes 786440 | tf_op jit(solution)/shard_map/ppermute | solution.py:37
  9.0 7.1 %all-to-all-start = ((bf16[16,3,3,16,256]{4,3,2,1,0:T(8,128)(2,1)}), bf16[16,3,3,16,256]{4,3,2,1,0:T(8,128)(2,1)}, u32[]{:S(2)}, u32[]{:S(2)}) async-start(bf16[16,3,3,16,256]{4,3,2,1,0:T(8,128)(2,1)} %broadcast_in_dim.80), calls=%async_computation | async-start | bytes 2359296 | tf_op jit(solution)/shard_map/all_to_all | solution.py:20
  17.0 2.6 %compare_select_fusion.1 = s32[512,1]{0,1:T(1,128)S(1)} fusion(s32[512,1]{0,1:T(1,128)S(1)} %bitcast.183, s32[512,1]{0,1:T(1,128)S(1)} %bitcast.182, s32[]{:T(128)} %bitcast.30, s32[]{:T(128)} %bitcast.31, s32[]{:T(128)} %bitcast.33, s32[]{:T(128)} %bitcast.32), kind=kLoop, calls=%fused_computation.109 | loop fusion | flops 4096 | bytes 6160 | tf_op jit(solution)/shard_map/jit(_take)/gather | solution.py:120
  22.9 13.3 %all-to-all-done = bf16[16,3,3,16,256]{4,3,2,1,0:T(8,128)(2,1)} async-done(((bf16[16,3,3,16,256]{4,3,2,1,0:T(8,128)(2,1)}), bf16[16,3,3,16,256]{4,3,2,1,0:T(8,128)(2,1)}, u32[]{:S(2)}, u32[]{:S(2)}) %all-to-all-start) | async-done | bytes 1179680 | tf_op jit(solution)/shard_map/all_to_all | solution.py:20
  36.2 1.4 copy.60
  44.1 1.6 fusion.1
  45.7 1.7 multiply_convert_fusion
  58.7 2.5 %reshape_reshape_reshape_reshape.3 = f32[32,16,1152]{2,1,0:T(8,128)S(1)} reshape(f32[9,256,256]{2,1,0:T(8,128)} %fusion.17) | data formatting | bytes 4718592 | tf_op jit(solution)/shard_map/reshape;reshape;reshape;reshape | solution.py:57
  61.2 2.2 %copy.107 = f32[32,16,1152]{2,0,1:T(8,128)} copy(f32[32,16,1152]{2,1,0:T(8,128)S(1)} %reshape_reshape_reshape_reshape.3) | data formatting | bytes 4718592 | tf_op jit(solution)/shard_map/reshape;reshape;reshape;reshape | solution.py:57
  63.4 3.7 %all-to-all-start.1 = ((f32[16,32,1152]{2,1,0:T(8,128)}), f32[16,32,1152]{2,1,0:T(8,128)S(1)}, u32[]{:S(2)}, u32[]{:S(2)}) async-start(f32[16,32,1152]{2,1,0:T(8,128)} %bitcast.162), calls=%async_computation.1 | async-start | bytes 4718592 | tf_op jit(solution)/shard_map/all_to_all | solution.py:63
  67.1 34.6 %all-to-all-done.1 = f32[16,32,1152]{2,1,0:T(8,128)S(1)} async-done(((f32[16,32,1152]{2,1,0:T(8,128)}), f32[16,32,1152]{2,1,0:T(8,128)S(1)}, u32[]{:S(2)}, u32[]{:S(2)}) %all-to-all-start.1) | async-done | bytes 2359328 | tf_op jit(solution)/shard_map/all_to_all | solution.py:63
  102.6 17.8 %all-to-all-start.2 = ((f32[32,1,1152]{2,1,0:T(1,128)}), f32[32,1,1152]{2,1,0:T(1,128)S(1)}, u32[]{:S(2)}, u32[]{:S(2)}) async-start(f32[32,1,1152]{2,1,0:T(1,128)} %all_to_all.21), calls=%async_computation.2 | async-start | bytes 294912 | tf_op jit(solution)/shard_map/all_to_all | solution.py:71
  120.4 2.7 %fusion.33 = f32[4,512,256]{2,1,0:T(8,128)} fusion(pred[512]{0:T(512)(128)(4,1)} %copy-done.15, bf16[4,256,512]{1,2,0:T(8,128)(2,1)S(1)} %multiply_convert_fusion, bf16[3,3,256,256]{3,2,1,0:T(8,128)(2,1)} %bitcast.172), kind=kOutput, calls=%fused_computation.63 | convolution fusion | flops 268959744 | bytes 3277312 | tf_op jit(solution)/shard_map/hok,oi->hik/dot_general | solution.py:150
  123.2 2.7 %fusion.59 = f32[4,512,256]{2,1,0:T(8,128)} fusion(bf16[4,256,512]{1,2,0:T(8,128)(2,1)S(1)} %multiply_convert_fusion, bf16[3,3,256,256]{3,2,1,0:T(8,128)(2,1)} %bitcast.173), kind=kOutput, calls=%fused_computation.105 | convolution fusion | flops 268435456 | bytes 3276800 | tf_op jit(solution)/shard_map/hok,oi->hik/dot_general | solution.py:150
  125.9 9.3 %all-to-all-done.2 = f32[32,1,1152]{2,1,0:T(1,128)S(1)} async-done(((f32[32,1,1152]{2,1,0:T(1,128)}), f32[32,1,1152]{2,1,0:T(1,128)S(1)}, u32[]{:S(2)}, u32[]{:S(2)}) %all-to-all-start.2) | async-done | bytes 147488 | tf_op jit(solution)/shard_map/all_to_all | solution.py:71
  136.1 6.8 %all-to-all-start.3 = ((f32[32,1,1152]{2,1,0:T(1,128)}), f32[32,1,1152]{2,1,0:T(1,128)S(1)}, u32[]{:S(2)}, u32[]{:S(2)}) async-start(f32[32,1,1152]{2,1,0:T(1,128)} %broadcast_in_dim.82), calls=%async_computation.3 | async-start | bytes 294912 | tf_op jit(solution)/shard_map/all_to_all | solution.py:20
  143.7 2.2 %collective-permute-start.2 = (bf16[1,256,512]{1,2,0:T(8,128)(2,1)S(1)}, bf16[1,256,512]{1,2,0:T(8,128)(2,1)S(1)}, u32[]{:S(2)}, u32[]{:S(2)}) collective-permute-start(bf16[1,256,512]{1,2,0:T(8,128)(2,1)S(1)} %get-tuple-element.26), channel_id=1, source_target_pairs={{16,0},{32,16},{48,32},{64,48},{80,64},{96,80},{112,96},{128,112},... | collective-permute-start | bytes 786440 | tf_op jit(solution)/shard_map/ppermute | solution.py:37
  145.8 2.1 %collective-permute-start.3 = (bf16[1,256,512]{1,2,0:T(8,128)(2,1)}, bf16[1,256,512]{1,2,0:T(8,128)(2,1)}, u32[]{:S(2)}, u32[]{:S(2)}) collective-permute-start(bf16[1,256,512]{1,2,0:T(8,128)(2,1)} %get-tuple-element.27), channel_id=1, source_target_pairs={{0,16},{16,32},{32,48},{48,64},{64,80},{80,96},{96,112},{112,128},... | collective-permute-start | bytes 786440 | tf_op jit(solution)/shard_map/ppermute | solution.py:34
  148.0 2.8 %fusion.36 = f32[4,512,256]{2,1,0:T(8,128)} fusion(pred[512]{0:T(512)(128)(4,1)S(1)} %copy-done.18, bf16[4,256,512]{1,2,0:T(8,128)(2,1)S(1)} %multiply_convert_fusion, bf16[3,3,256,256]{3,2,1,0:T(8,128)(2,1)} %bitcast.174), kind=kOutput, calls=%fused_computation.66 | convolution fusion | flops 268959744 | bytes 3277312 | tf_op jit(solution)/shard_map/hok,oi->hik/dot_general | solution.py:150
  150.8 1.9 collective-permute-done.2
  153.4 2.7 %fusion.10 = f32[4,512,256]{2,1,0:T(8,128)} fusion(bf16[1,256,512]{1,2,0:T(8,128)(2,1)S(1)} %collective-permute-done.2, bf16[4,256,512]{1,2,0:T(8,128)(2,1)S(1)} %multiply_convert_fusion, bf16[3,3,256,256]{3,2,1,0:T(8,128)(2,1)} %bitcast.175), kind=kOutput, calls=%fused_computation.24 | convolution fusion | flops 271056896 | bytes 3538944 | tf_op jit(solution)/shard_map/hok,oi->hik/dot_general | solution.py:150
  156.1 1.6 all-to-all-done.3
  157.8 1.7 broadcast_in_dim.84
  159.4 3.9 %all-to-all-start.4 = ((f32[16,32,1152]{2,1,0:T(8,128)}), f32[16,32,1152]{2,1,0:T(8,128)S(1)}, u32[]{:S(2)}, u32[]{:S(2)}) async-start(f32[16,32,1152]{2,1,0:T(8,128)} %broadcast_in_dim.84), calls=%async_computation.4 | async-start | bytes 4718592 | tf_op jit(solution)/shard_map/all_to_all | solution.py:20
  163.4 1.5 fusion.28
  169.1 3.0 %fusion.2 = bf16[4,256,512]{1,2,0:T(8,128)(2,1)} fusion(f32[4,512,256]{2,1,0:T(8,128)S(1)} %fusion.29, f32[4,512,256]{2,1,0:T(8,128)S(1)} %fusion.30, f32[4,512,256]{2,1,0:T(8,128)S(1)} %copy-done.7, f32[4,512,256]{2,1,0:T(8,128)S(1)} %copy-done.8, f32[4,512,256]{2,1,0:T(8,128)S(1)} %copy-done.9, f32[4,512,256]{2,1,0:T(8,128)S(1)} %fusion.31, ...), kind=kOutput, calls=%fused_computation.16 | convolution fusion | flops 275775488 | bytes 19267584 | tf_op jit(solution)/shard_map/hok,oi->hik/dot_general | solution.py:150
  172.0 2.3 %copy.85 = bf16[4,256,512]{2,1,0:T(8,128)(2,1)} copy(bf16[4,256,512]{1,2,0:T(8,128)(2,1)} %fusion.2) | data formatting | bytes 2097152
  174.3 27.4 %all-to-all-done.4 = f32[16,32,1152]{2,1,0:T(8,128)S(1)} async-done(((f32[16,32,1152]{2,1,0:T(8,128)}), f32[16,32,1152]{2,1,0:T(8,128)S(1)}, u32[]{:S(2)}, u32[]{:S(2)}) %all-to-all-start.4) | async-done | bytes 2359328 | tf_op jit(solution)/shard_map/all_to_all | solution.py:20
  201.7 2.8 %copy.84 = f32[32,16,1152]{2,1,0:T(8,128)} copy(f32[32,16,1152]{2,0,1:T(8,128)S(1)} %bitcast.161) | data formatting | bytes 4718592 | tf_op jit(solution)/shard_map/transpose | solution.py:52
  204.5 2.5 %reshape_reshape_reshape.3 = f32[3,3,256,256]{3,2,1,0:T(8,128)S(1)} reshape(f32[32,16,1152]{2,1,0:T(8,128)} %copy.84) | data formatting | bytes 4718592 | tf_op jit(solution)/shard_map/reshape;reshape;reshape | solution.py:79
  (87 shorter events, 30.9 us)
Async XLA Ops:
  0.6 7.3 %copy-start.14 = (bf16[3,3,16,256]{3,2,1,0:T(8,128)(2,1)S(1)}, bf16[3,3,16,256]{3,2,1,0:T(8,128)(2,1)}, u32[]{:S(2)}) copy-start(bf16[3,3,16,256]{3,2,1,0:T(8,128)(2,1)} %param.7) | copy-start | bytes 221188
  2.2 14.0 %copy-start.19 = (s32[64]{0:T(128)S(1)}, s32[64]{0:T(128)}, u32[]{:S(2)}) copy-start(s32[64]{0:T(128)} %param.9) | copy-start | bytes 772
  2.2 17.4 %copy-start.13 = (bf16[4,256,512]{2,1,0:T(8,128)(2,1)S(1)}, bf16[4,256,512]{2,1,0:T(8,128)(2,1)}, u32[]{:S(2)}) copy-start(bf16[4,256,512]{2,1,0:T(8,128)(2,1)} %param.8) | copy-start | bytes 3145732
  2.2 18.8 %collective-permute-start = (bf16[1,256,512]{1,2,0:T(8,128)(2,1)S(1)}, bf16[1,256,512]{1,2,0:T(8,128)(2,1)S(1)}, u32[]{:S(2)}, u32[]{:S(2)}) collective-permute-start(bf16[1,256,512]{1,2,0:T(8,128)(2,1)S(1)} %get-tuple-element.30), channel_id=1, source_target_pairs={{0,16},{16,32},{32,48},{48,64},{64,80},{80,96},{96,112},{112,128},... | collective-permute-start | bytes 786440 | tf_op jit(solution)/shard_map/ppermute | solution.py:34
  4.3 17.4 %collective-permute-start.1 = (bf16[1,256,512]{1,2,0:T(8,128)(2,1)S(1)}, bf16[1,256,512]{1,2,0:T(8,128)(2,1)S(1)}, u32[]{:S(2)}, u32[]{:S(2)}) collective-permute-start(bf16[1,256,512]{1,2,0:T(8,128)(2,1)S(1)} %get-tuple-element.31), channel_id=1, source_target_pairs={{16,0},{32,16},{48,32},{64,48},{80,64},{96,80},{112,96},{128,112},... | collective-permute-start | bytes 786440 | tf_op jit(solution)/shard_map/ppermute | solution.py:37
  9.0 27.2 %all-to-all-start = ((bf16[16,3,3,16,256]{4,3,2,1,0:T(8,128)(2,1)}), bf16[16,3,3,16,256]{4,3,2,1,0:T(8,128)(2,1)}, u32[]{:S(2)}, u32[]{:S(2)}) async-start(bf16[16,3,3,16,256]{4,3,2,1,0:T(8,128)(2,1)} %broadcast_in_dim.80), calls=%async_computation | async-start | bytes 2359296 | tf_op jit(solution)/shard_map/all_to_all | solution.py:20
  16.1 38.8 %copy-start.15 = (pred[512]{0:T(512)(128)(4,1)}, pred[512]{0:T(512)(128)(4,1)S(1)}, u32[]{:S(2)}) copy-start(pred[512]{0:T(512)(128)(4,1)S(1)} %compare_and_fusion) | copy-start | bytes 1540
  16.2 41.2 %copy-start.17 = (pred[512]{0:T(512)(128)(4,1)}, pred[512]{0:T(512)(128)(4,1)S(1)}, u32[]{:S(2)}) copy-start(pred[512]{0:T(512)(128)(4,1)S(1)} %compare_and_fusion.1) | copy-start | bytes 1540
  21.0 0.7 copy-start.11
  22.8 15.2 %copy-start = (bf16[4,256,512]{1,2,0:T(8,128)(2,1)}, bf16[4,256,512]{1,2,0:T(8,128)(2,1)S(1)}, u32[]{:S(2)}) copy-start(bf16[4,256,512]{1,2,0:T(8,128)(2,1)S(1)} %get-tuple-element.28) | copy-start | bytes 3145732
  37.6 5.1 %copy-start.4 = (bf16[3,3,16,16,256]{4,3,2,1,0:T(8,128)(2,1)}, bf16[3,3,16,16,256]{4,3,2,1,0:T(8,128)(2,1)S(1)}, u32[]{:S(2)}) copy-start(bf16[3,3,16,16,256]{4,3,2,1,0:T(8,128)(2,1)S(1)} %copy.60) | copy-start | bytes 3538948
  40.1 1.2 copy-start.2
  41.3 0.9 copy-start.12
  42.7 1.4 copy-start.3
  45.7 1.7 copy-start.1
  63.4 38.4 %all-to-all-start.1 = ((f32[16,32,1152]{2,1,0:T(8,128)}), f32[16,32,1152]{2,1,0:T(8,128)S(1)}, u32[]{:S(2)}, u32[]{:S(2)}) async-start(f32[16,32,1152]{2,1,0:T(8,128)} %bitcast.162), calls=%async_computation.1 | async-start | bytes 4718592 | tf_op jit(solution)/shard_map/all_to_all | solution.py:63
  102.6 32.6 %all-to-all-start.2 = ((f32[32,1,1152]{2,1,0:T(1,128)}), f32[32,1,1152]{2,1,0:T(1,128)S(1)}, u32[]{:S(2)}, u32[]{:S(2)}) async-start(f32[32,1,1152]{2,1,0:T(1,128)} %all_to_all.21), calls=%async_computation.2 | async-start | bytes 294912 | tf_op jit(solution)/shard_map/all_to_all | solution.py:71
  123.2 24.8 %copy-start.18 = (pred[512]{0:T(512)(128)(4,1)S(1)}, pred[512]{0:T(512)(128)(4,1)}, u32[]{:S(2)}) copy-start(pred[512]{0:T(512)(128)(4,1)} %copy-done.17) | copy-start | bytes 1540
  136.1 21.7 %all-to-all-start.3 = ((f32[32,1,1152]{2,1,0:T(1,128)}), f32[32,1,1152]{2,1,0:T(1,128)S(1)}, u32[]{:S(2)}, u32[]{:S(2)}) async-start(f32[32,1,1152]{2,1,0:T(1,128)} %broadcast_in_dim.82), calls=%async_computation.3 | async-start | bytes 294912 | tf_op jit(solution)/shard_map/all_to_all | solution.py:20
  143.7 9.0 %collective-permute-start.2 = (bf16[1,256,512]{1,2,0:T(8,128)(2,1)S(1)}, bf16[1,256,512]{1,2,0:T(8,128)(2,1)S(1)}, u32[]{:S(2)}, u32[]{:S(2)}) collective-permute-start(bf16[1,256,512]{1,2,0:T(8,128)(2,1)S(1)} %get-tuple-element.26), channel_id=1, source_target_pairs={{16,0},{32,16},{48,32},{64,48},{80,64},{96,80},{112,96},{128,112},... | collective-permute-start | bytes 786440 | tf_op jit(solution)/shard_map/ppermute | solution.py:37
  145.8 17.5 %collective-permute-start.3 = (bf16[1,256,512]{1,2,0:T(8,128)(2,1)}, bf16[1,256,512]{1,2,0:T(8,128)(2,1)}, u32[]{:S(2)}, u32[]{:S(2)}) collective-permute-start(bf16[1,256,512]{1,2,0:T(8,128)(2,1)} %get-tuple-element.27), channel_id=1, source_target_pairs={{0,16},{16,32},{32,48},{48,64},{64,80},{80,96},{96,112},{112,128},... | collective-permute-start | bytes 786440 | tf_op jit(solution)/shard_map/ppermute | solution.py:34
  152.7 0.7 copy-start.10
  159.4 42.3 %all-to-all-start.4 = ((f32[16,32,1152]{2,1,0:T(8,128)}), f32[16,32,1152]{2,1,0:T(8,128)S(1)}, u32[]{:S(2)}, u32[]{:S(2)}) async-start(f32[16,32,1152]{2,1,0:T(8,128)} %broadcast_in_dim.84), calls=%async_computation.4 | async-start | bytes 4718592 | tf_op jit(solution)/shard_map/all_to_all | solution.py:20
  163.4 1.5 copy-start.5
  163.4 1.5 copy-start.16
  165.4 1.6 copy-start.9
  165.9 1.8 copy-start.7
  166.0 2.4 %copy-start.8 = (f32[4,512,256]{2,1,0:T(8,128)S(1)}, f32[4,512,256]{2,1,0:T(8,128)}, u32[]{:S(2)}) copy-start(f32[4,512,256]{2,1,0:T(8,128)} %fusion.59) | copy-start | bytes 6291460
  166.5 2.6 %copy-start.6 = (f32[4,512,256]{2,1,0:T(8,128)S(1)}, f32[4,512,256]{2,1,0:T(8,128)}, u32[]{:S(2)}) copy-start(f32[4,512,256]{2,1,0:T(8,128)} %fusion.10) | copy-start | bytes 6291460
where the time goes:
time: 209 us; the launch traced here: 208 us
  waiting for transfers between devices  88.3 us (42%)
  starting transfers between devices  49.4 us (24%)
  matrix products  32.6 us (16%)
  local copies, waits for them, and re-layouts  27.6 us (13%)
  other arithmetic  8.84 us (4%)
    all_to_all x3, waiting for transfers between devices, from_everyone(): lax.all_to_all(jnp.broadcast_to(array[None], (peers, *array.shape)), axis...  42.4 us
    all_to_all x1, waiting for transfers between devices, sent_and_summed(): lax.all_to_all(parts, axis, split_axis=0, concat_axis=0, tiled=True)  34.6 us
    all_to_all x3, starting transfers between devices, from_everyone(): lax.all_to_all(jnp.broadcast_to(array[None], (peers, *array.shape)), axis...  17.9 us
    all_to_all x1, starting transfers between devices, sum_in_two_steps(): lax.all_to_all(nearer, far, split_axis=0, concat_axis=0, tiled=True)  17.8 us
    dot_general x9, matrix products, body(): jnp.einsum('hok,oi->hik', window, kernel[offset_row, offset_col], preferr...  16 us
    dot_general x9, matrix products, body(): jnp.einsum('hik,hok->oi', window, grad_pre, preferred_element_type=jnp.fl...  11.2 us
    unnamed x44, local copies, waits for them, and re-layouts  9.78 us
    all_to_all x1, waiting for transfers between devices, sum_in_two_steps(): lax.all_to_all(nearer, far, split_axis=0, concat_axis=0, tiled=True)  9.35 us
  transfers between devices with their start and end apart: 9, of which 6 were waited for; matrix products, arithmetic and copies ran while one was open for 14% of the time, Pallas kernels for 0%

commit v1 on v0

v1 whole, which is shorter than its diff:
```python
import jax
import jax.numpy as jnp
from jax import lax
from jax.experimental import pallas as pl
from jax.experimental.pallas import tpu as pltpu
from jax.sharding import Mesh
from jax.sharding import PartitionSpec as P

COLS = 128
CH = ("ch_0", "ch_1")
ROWS = ("rows_0", "rows_1")
BF16 = jnp.bfloat16
F32 = jnp.float32


def dot(a, b, dims):
    return lax.dot_general(a, b, (dims, ((), ())), preferred_element_type=F32)


def side_shift(tile, across):
    lane = lax.broadcasted_iota(jnp.int32, tile.shape, 1)
    wide = tile.astype(F32)
    moved = pltpu.roll(wide, -across % COLS, 1)
    edge = COLS - 1 if across > 0 else 0
    return jnp.where(lane == edge, 0.0, moved).astype(tile.dtype)


def fill_shifted(out_ref, row, source):
    cells = source.shape[1]
    base = row * cells
    out_ref[1, :, pl.ds(base, cells)] = source
    for image in range(cells // COLS):
        tile = source[:, image * COLS : (image + 1) * COLS]
        for side in (0, 2):
            out_ref[side, :, pl.ds(base + image * COLS, COLS)] = side_shift(tile, side - 1)


def grad_kernel(limits_ref, core_ref, low_ref, feat_ref, high_ref, w_ref, cot_ref,
                grad_ref, own_ref, other_ref, shifted_ref, flat_ref):
    band, ch, cells = feat_ref.shape
    images = cells // COLS
    fill_shifted(shifted_ref, 0, low_ref[0])
    for h in range(band):
        fill_shifted(shifted_ref, h + 1, feat_ref[h])
    fill_shifted(shifted_ref, band + 1, high_ref[0])
    for h in range(band):
        summed = None
        for r in range(3):
            for c in range(3):
                w = w_ref[:, 3 * r + c].reshape(ch, ch)
                x = shifted_ref[c, :, pl.ds((h + r) * cells, cells)]
                term = dot(w, x, ((1,), (0,)))
                summed = term if summed is None else summed + term
        center = jnp.sum(summed, 0, keepdims=True) / ch
        spread = jnp.sum(summed * summed, 0, keepdims=True) / ch - center * center
        inverse = lax.rsqrt(spread + 1e-06)
        normed = (summed - center) * inverse
        keep = jnp.concatenate(
            [jnp.full((1, COLS), jnp.where(h < limits_ref[n], 1.0, 0.0), F32) for n in range(images)], 1
        )
        masked = cot_ref[h].astype(F32) * keep
        total = jnp.sum(masked, 0, keepdims=True) / ch
        cross = jnp.sum(masked * normed, 0, keepdims=True) / ch
        grad = (inverse * (masked - total - normed * cross)).astype(BF16)
        grad_ref[h] = grad
        flat_ref[:, pl.ds(h * cells, cells)] = grad
    half = ch // 2
    first = core_ref[0] == 0
    for r in range(3):
        for c in range(3):
            tap = dot(
                flat_ref[...], shifted_ref[c, :, pl.ds(r * cells, band * cells)], ((1,), (1,))
            )
            left, right = tap[:, :half], tap[:, half:]
            parts = own_ref.shape[0], own_ref.shape[2], half
            own_ref[:, 3 * r + c] = jnp.where(first, left, right).reshape(parts)
            other_ref[:, 3 * r + c] = jnp.where(first, right, left).astype(BF16).reshape(parts)


def input_kernel(low_ref, grad_ref, high_ref, w_ref, out_ref, shifted_ref, wt_ref):
    band, ch, cells = grad_ref.shape
    fill_shifted(shifted_ref, 0, low_ref[0])
    for h in range(band):
        fill_shifted(shifted_ref, h + 1, grad_ref[h])
    fill_shifted(shifted_ref, band + 1, high_ref[0])
    for t in range(9):
        wt_ref[t] = w_ref[:, t].reshape(ch, ch).T
    for h in range(band):
        summed = None
        for r in range(3):
            for c in range(3):
                x = shifted_ref[2 - c, :, pl.ds((h + 2 - r) * cells, cells)]
                term = dot(wt_ref[3 * r + c], x, ((1,), (0,)))
                summed = term if summed is None else summed + term
        out_ref[h] = summed.astype(BF16)


def exchange(block, axis):
    return lax.ppermute(block, axis, [(0, 1), (1, 0)])


def band_edges(block):
    count = lax.axis_size(ROWS)
    forward = [(i, i + 1) for i in range(count - 1)]
    backward = [(target, source) for source, target in forward]
    low = lax.ppermute(block[-1:], ROWS, forward)
    high = lax.ppermute(block[:1], ROWS, backward)
    return low, high


def to_all(block, axis):
    peers = lax.axis_size(axis)
    return lax.all_to_all(jnp.broadcast_to(block[None], (peers, *block.shape)), axis, 0, 0, tiled=True)


def vmem(count):
    return [pl.BlockSpec(memory_space=pltpu.VMEM)] * count


def work(block, convs):
    band, ch, cells = block.shape
    return pl.CostEstimate(
        flops=convs * 18 * ch * ch * band * cells, bytes_accessed=convs << 22, transcendentals=0
    )


def call_grad(limits, core, low, features, high, kernel, cotangent):
    band, ch, cells = features.shape
    halved = (*kernel.shape[:3], ch // 2)
    return pl.pallas_call(
        grad_kernel,
        in_specs=[pl.BlockSpec(memory_space=pltpu.SMEM)] * 2 + vmem(5),
        out_specs=vmem(3),
        out_shape=[
            jax.ShapeDtypeStruct(features.shape, BF16),
            jax.ShapeDtypeStruct(halved, F32),
            jax.ShapeDtypeStruct(halved, BF16),
        ],
        scratch_shapes=[
            pltpu.VMEM((3, ch, (band + 2) * cells), BF16),
            pltpu.VMEM((ch, band * cells), BF16),
        ],
        cost_estimate=work(features, 2),
        compiler_params=pltpu.CompilerParams(vmem_limit_bytes=24 << 20),
        name="grad",
    )(limits, core, low, features, high, kernel, cotangent)


def call_input(low, grad, high, kernel):
    band, ch, cells = grad.shape
    return pl.pallas_call(
        input_kernel,
        in_specs=vmem(4),
        out_specs=vmem(1)[0],
        out_shape=jax.ShapeDtypeStruct(grad.shape, BF16),
        scratch_shapes=[
            pltpu.VMEM((3, ch, (band + 2) * cells), BF16),
            pltpu.VMEM((9, ch, ch), BF16),
        ],
        cost_estimate=work(grad, 1),
        compiler_params=pltpu.CompilerParams(vmem_limit_bytes=20 << 20),
        name="input",
    )(low, grad, high, kernel)


def body(features, conv_weight, cotangent, valid_rows):
    band, ch, cells = features.shape
    images = cells // COLS
    near = conv_weight.shape[2]
    half = ch // 2
    core = lax.axis_index("rows_1").astype(jnp.int32).reshape(1)
    limits = lax.dynamic_slice_in_dim(valid_rows, lax.axis_index(CH) * images, images, 0)
    limits = limits - lax.axis_index(ROWS) * band
    kernel = to_all(conv_weight.reshape(9, near, ch), CH)
    low, high = band_edges(features)
    grad_pre, own, other = call_grad(limits, core, low, features, high, kernel, cotangent)
    pair = (own + exchange(other, "rows_1").astype(F32)).astype(BF16)
    plane = lax.all_to_all(pair, CH, 0, 0, tiled=True).astype(F32).sum(0)
    lines = plane.transpose(1, 0, 2)
    share = lax.all_to_all(lines, "rows_0", 0, 0, tiled=True).reshape(near, 9, half).sum(0)
    mine = to_all(share, "rows_0")
    theirs = exchange(mine, "rows_1")
    first = core[0] == 0
    weight_grad = jnp.concatenate(
        [jnp.where(first, mine, theirs), jnp.where(first, theirs, mine)], 2
    ).transpose(1, 0, 2)
    grad_low, grad_high = band_edges(grad_pre)
    input_grad = call_input(grad_low, grad_pre, grad_high, kernel)
    return input_grad, weight_grad.reshape(3, 3, near, ch)


def solution(mesh):
    split = Mesh(mesh.devices.reshape(16, 2, 4, 4), ("rows_0", "rows_1", "ch_0", "ch_1"))
    placed = (P(ROWS, None, CH), P(None, None, CH, None), P(ROWS, None, CH), P())
    return jax.shard_map(
        body,
        mesh=split,
        in_specs=placed,
        out_specs=(P(ROWS, None, CH), P(None, None, CH, None)),
        check_vma=False,
    )
```

time: 209 us -> 114 us (0.55)
  the two profiles are of different devices: /device:TPU:64 before, /device:TPU:1 now
where the time goes in v1:
time: 114 us; the launch traced here: 113 us
  blocking collectives  40.9 us (36%)
  starting transfers between devices  39.3 us (34%)
  waiting for transfers between devices  14.9 us (13%)
  Pallas kernels  10.5 us (9%)
  local copies, waits for them, and re-layouts  5.67 us (5%)
    all_to_all x1, blocking collectives, body(): lax.all_to_all(lines, 'rows_0', 0, 0, tiled=True).reshape(near, 9, half)  26.8 us
    all_to_all x1, blocking collectives, body(): plane = lax.all_to_all(pair, CH, 0, 0, tiled=True).astype(F32).sum(0)  14.1 us
    all_to_all x2, starting transfers between devices, to_all(): lax.all_to_all(jnp.broadcast_to(block[None], (peers, *block.shape)), axis...  13 us
    ppermute x2, starting transfers between devices, exchange(): return lax.ppermute(block, axis, [(0, 1), (1, 0)])  12.4 us
    ppermute x2, starting transfers between devices, band_edges(): low = lax.ppermute(block[-1:], ROWS, forward)  10 us
    all_to_all x2, waiting for transfers between devices, to_all(): lax.all_to_all(jnp.broadcast_to(block[None], (peers, *block.shape)), axis...  7.33 us
    pallas_call x1, Pallas kernels, call_grad(): pl.pallas_call(grad_kernel, in_specs=[pl.BlockSpec(memory_space=pltpu.SME...  6.43 us
    ppermute x2, waiting for transfers between devices, band_edges(): high = lax.ppermute(block[:1], ROWS, backward)  4.69 us
  transfers between devices with their start and end apart: 8, of which 5 were waited for; matrix products, arithmetic and copies ran while one was open for 0% of the time, Pallas kernels for 4%

profile of v1, /device:TPU:1, one launch (start us, length us, event | category | flops | bytes accessed | tf_op | source)
XLA Modules:
  0.0 113.1 jit_solution(5028243323337933832)
XLA Ops:
  0.6 2.0 %broadcast_in_dim.14 = bf16[16,9,16,256]{3,2,1,0:T(8,128)(2,1)} broadcast(bf16[9,16,256]{2,1,0:T(8,128)(2,1)} %bitcast.8), dimensions={1,2,3} | broadcast | bytes 1253376 | tf_op jit(solution)/shard_map/broadcast_in_dim | solution.py:113
  2.6 0.0 copy-start
  2.6 7.7 %all-to-all-start = ((bf16[16,9,16,256]{3,2,1,0:T(8,128)(2,1)}), bf16[16,9,16,256]{3,2,1,0:T(8,128)(2,1)S(1)}, u32[]{:S(2)}, u32[]{:S(2)}) async-start(bf16[16,9,16,256]{3,2,1,0:T(8,128)(2,1)} %broadcast_in_dim.14), calls=%async_computation | async-start | bytes 2359296 | tf_op jit(solution)/shard_map/all_to_all | solution.py:113
  10.3 0.0 copy-done
  10.4 4.4 %collective-permute-start = (bf16[1,256,512]{2,1,0:T(8,128)(2,1)S(1)}, bf16[1,256,512]{2,1,0:T(8,128)(2,1)S(1)}, u32[]{:S(2)}, u32[]{:S(2)}) collective-permute-start(bf16[1,256,512]{2,1,0:T(8,128)(2,1)S(1)} %get-tuple-element.13), channel_id=1, source_target_pairs={{0,16},{16,32},{32,48},{48,64},{64,80},{80,96},{96,112},{112,128},... | collective-permute-start | bytes 786440 | tf_op jit(solution)/shard_map/ppermute | solution.py:106
  14.8 1.9 %collective-permute-start.1 = (bf16[1,256,512]{2,1,0:T(8,128)(2,1)S(1)}, bf16[1,256,512]{2,1,0:T(8,128)(2,1)S(1)}, u32[]{:S(2)}, u32[]{:S(2)}) collective-permute-start(bf16[1,256,512]{2,1,0:T(8,128)(2,1)S(1)} %get-tuple-element.12), channel_id=1, source_target_pairs={{16,0},{32,16},{48,32},{64,48},{80,64},{96,80},{112,96},{128,112},... | collective-permute-start | bytes 786440 | tf_op jit(solution)/shard_map/ppermute | solution.py:107
  16.7 0.0 copy-done.4
  16.7 0.1 dynamic-slice_subtract_fusion.limits_ref
  16.8 1.3 %collective-permute-done.low_ref = bf16[1,256,512]{2,1,0:T(8,128)(2,1)S(1)} collective-permute-done((bf16[1,256,512]{2,1,0:T(8,128)(2,1)S(1)}, bf16[1,256,512]{2,1,0:T(8,128)(2,1)S(1)}, u32[]{:S(2)}, u32[]{:S(2)}) %collective-permute-start) | collective-permute-done | bytes 262176 | tf_op jit(solution)/shard_map/ppermute | solution.py:106
  18.1 4.7 %collective-permute-done.1.high_ref = bf16[1,256,512]{2,1,0:T(8,128)(2,1)S(1)} collective-permute-done((bf16[1,256,512]{2,1,0:T(8,128)(2,1)S(1)}, bf16[1,256,512]{2,1,0:T(8,128)(2,1)S(1)}, u32[]{:S(2)}, u32[]{:S(2)}) %collective-permute-start.1) | collective-permute-done | bytes 262176 | tf_op jit(solution)/shard_map/ppermute | solution.py:107
  22.8 0.7 copy-done.2
  23.5 2.9 %all-to-all-done.w_ref = bf16[16,9,16,256]{3,2,1,0:T(8,128)(2,1)S(1)} async-done(((bf16[16,9,16,256]{3,2,1,0:T(8,128)(2,1)}), bf16[16,9,16,256]{3,2,1,0:T(8,128)(2,1)S(1)}, u32[]{:S(2)}, u32[]{:S(2)}) %all-to-all-start) | async-done | bytes 1179680 | tf_op jit(solution)/shard_map/all_to_all | solution.py:113
  26.4 1.2 %copy-done.1 = bf16[4,256,512]{2,1,0:T(8,128)(2,1)S(1)} copy-done((bf16[4,256,512]{2,1,0:T(8,128)(2,1)S(1)}, bf16[4,256,512]{2,1,0:T(8,128)(2,1)}, u32[]{:S(2)}) %copy-start.1) | copy-done | bytes 1048600
  27.6 0.9 copy-done.3
  28.6 6.4 %grad.1 = (bf16[4,256,512]{2,1,0:T(8,128)(2,1)S(1)}, f32[16,9,16,128]{3,2,1,0:T(8,128)S(1)}, bf16[16,9,16,128]{3,2,1,0:T(8,128)(2,1)S(1)}) custom-call(s32[4]{0:T(128)S(1)} %dynamic-slice_subtract_fusion.limits_ref, s32[1]{0:T(128)} %bitcast.core_ref, bf16[1,256,512]{2,1,0:T(8,128)(2,1)S(1)} %collective-permute-done.low_ref, ...), custom_call_target="tpu_custom_call" | custom-call | flops 4831838208 | bytes 8388608 | tf_op jit(solution)/shard_map/grad/pallas_call | solution.py:130
  35.0 5.9 %collective-permute-start.4 = (bf16[16,9,16,128]{3,2,1,0:T(8,128)(2,1)S(1)}, bf16[16,9,16,128]{3,2,1,0:T(8,128)(2,1)S(1)}, u32[]{:S(2)}, u32[]{:S(2)}) collective-permute-start(bf16[16,9,16,128]{3,2,1,0:T(8,128)(2,1)S(1)} %get-tuple-element.7), channel_id=1, source_target_pairs={{0,16},{16,0},{1,17},{17,1},{2,18},{18,2},{3,19},{19,3},{4,20},{20... | collective-permute-start | bytes 1769480 | tf_op jit(solution)/shard_map/ppermute | solution.py:99
  40.9 1.6 %collective-permute-done.4 = bf16[16,9,16,128]{3,2,1,0:T(8,128)(2,1)S(1)} collective-permute-done((bf16[16,9,16,128]{3,2,1,0:T(8,128)(2,1)S(1)}, bf16[16,9,16,128]{3,2,1,0:T(8,128)(2,1)S(1)}, u32[]{:S(2)}, u32[]{:S(2)}) %collective-permute-start.4) | collective-permute-done | bytes 589856 | tf_op jit(solution)/shard_map/ppermute | solution.py:99
  42.5 0.1 add_convert_fusion
  42.7 14.1 %all_to_all.20 = bf16[16,9,16,128]{3,2,1,0:T(8,128)(2,1)S(1)} all-to-all(bf16[16,9,16,128]{3,2,1,0:T(8,128)(2,1)S(1)} %add_convert_fusion), channel_id=1, replica_groups=mesh['rows_0'=16,'rows_1'=2,'ch_0'=4,'ch_1'=4] {'ch_0','ch_1'}, dimensions={0} | all-to-all | bytes 1179648 | tf_op jit(solution)/shard_map/all_to_all | solution.py:178
  56.8 0.1 convert_reduce_fusion
  56.9 26.8 %all_to_all.21 = f32[16,9,128]{2,1,0:T(8,128)S(1)} all-to-all(f32[16,9,128]{2,1,0:T(8,128)S(1)} %copy.10), channel_id=1, replica_groups=mesh['rows_0'=16,'rows_1'=2,'ch_0'=4,'ch_1'=4] {'rows_0'}, dimensions={0} | all-to-all | bytes 147456 | tf_op jit(solution)/shard_map/all_to_all | solution.py:180
  83.7 0.7 broadcast_in_dim.15
  84.4 5.3 %all-to-all-start.3 = ((f32[16,9,128]{2,1,0:T(8,128)}), f32[16,9,128]{2,1,0:T(8,128)S(1)}, u32[]{:S(2)}, u32[]{:S(2)}) async-start(f32[16,9,128]{2,1,0:T(8,128)} %broadcast_in_dim.15), calls=%async_computation.3 | async-start | bytes 262144 | tf_op jit(solution)/shard_map/all_to_all | solution.py:113
  89.8 5.6 %collective-permute-start.2 = (bf16[1,256,512]{2,1,0:T(8,128)(2,1)S(1)}, bf16[1,256,512]{2,1,0:T(8,128)(2,1)S(1)}, u32[]{:S(2)}, u32[]{:S(2)}) collective-permute-start(bf16[1,256,512]{2,1,0:T(8,128)(2,1)S(1)} %get-tuple-element.11), channel_id=1, source_target_pairs={{0,16},{16,32},{32,48},{48,64},{64,80},{80,96},{96,112},{112,128},... | collective-permute-start | bytes 786440 | tf_op jit(solution)/shard_map/ppermute | solution.py:106
  95.4 1.9 %collective-permute-start.3 = (bf16[1,256,512]{2,1,0:T(8,128)(2,1)S(1)}, bf16[1,256,512]{2,1,0:T(8,128)(2,1)S(1)}, u32[]{:S(2)}, u32[]{:S(2)}) collective-permute-start(bf16[1,256,512]{2,1,0:T(8,128)(2,1)S(1)} %get-tuple-element.10), channel_id=1, source_target_pairs={{16,0},{32,16},{48,32},{64,48},{80,64},{96,80},{112,96},{128,112},... | collective-permute-start | bytes 786440 | tf_op jit(solution)/shard_map/ppermute | solution.py:107
  97.3 4.4 %all-to-all-done.3 = f32[16,9,128]{2,1,0:T(8,128)S(1)} async-done(((f32[16,9,128]{2,1,0:T(8,128)}), f32[16,9,128]{2,1,0:T(8,128)S(1)}, u32[]{:S(2)}, u32[]{:S(2)}) %all-to-all-start.3) | async-done | bytes 73760 | tf_op jit(solution)/shard_map/all_to_all | solution.py:113
  101.7 6.5 %collective-permute-start.5 = (f32[16,9,128]{2,0,1:T(8,128)S(1)}, f32[16,9,128]{2,0,1:T(8,128)S(1)}, u32[]{:S(2)}, u32[]{:S(2)}) collective-permute-start(f32[16,9,128]{2,0,1:T(8,128)S(1)} %copy.12), channel_id=1, source_target_pairs={{0,16},{16,0},{1,17},{17,1},{2,18},{18,2},{3,19},{19,3},{4,20},{20... | collective-permute-start | bytes 221192 | tf_op jit(solution)/shard_map/ppermute | solution.py:99
  108.3 0.0 collective-permute-done.2.low_ref
  108.3 0.0 collective-permute-done.3.high_ref
  108.3 4.1 %input.1 = bf16[4,256,512]{2,1,0:T(8,128)(2,1)} custom-call(bf16[1,256,512]{2,1,0:T(8,128)(2,1)S(1)} %collective-permute-done.2.low_ref, bf16[4,256,512]{2,1,0:T(8,128)(2,1)S(1)} %get-tuple-element.5.grad_ref, bf16[1,256,512]{2,1,0:T(8,128)(2,1)S(1)} %collective-permute-done.3.high_ref, bf16[16,9,16,256]{3,2,1,0:T(8,128)(2,1)S(1)} %all-to-all-done.w_ref), custom_call_target="tpu_custom_call" | custom-call | flops 2415919104 | bytes 4194304 | tf_op jit(solution)/shard_map/input/pallas_call | solution.py:151
  112.4 0.0 collective-permute-done.5
  112.4 0.7 pad_maximum_fusion
  (10 shorter events, 0.2 us)
Async XLA Ops:
  2.6 7.7 %copy-start = (bf16[4,256,512]{2,1,0:T(8,128)(2,1)S(1)}, bf16[4,256,512]{2,1,0:T(8,128)(2,1)}, u32[]{:S(2)}) copy-start(bf16[4,256,512]{2,1,0:T(8,128)(2,1)} %feat_ref.1) | copy-start | bytes 3145732
  2.6 14.1 %copy-start.4 = (s32[64]{0:T(128)S(1)}, s32[64]{0:T(128)}, u32[]{:S(2)}) copy-start(s32[64]{0:T(128)} %param.7) | copy-start | bytes 772
  2.6 23.8 %all-to-all-start = ((bf16[16,9,16,256]{3,2,1,0:T(8,128)(2,1)}), bf16[16,9,16,256]{3,2,1,0:T(8,128)(2,1)S(1)}, u32[]{:S(2)}, u32[]{:S(2)}) async-start(bf16[16,9,16,256]{3,2,1,0:T(8,128)(2,1)} %broadcast_in_dim.14), calls=%async_computation | async-start | bytes 2359296 | tf_op jit(solution)/shard_map/all_to_all | solution.py:113
  10.4 7.7 %collective-permute-start = (bf16[1,256,512]{2,1,0:T(8,128)(2,1)S(1)}, bf16[1,256,512]{2,1,0:T(8,128)(2,1)S(1)}, u32[]{:S(2)}, u32[]{:S(2)}) collective-permute-start(bf16[1,256,512]{2,1,0:T(8,128)(2,1)S(1)} %get-tuple-element.13), channel_id=1, source_target_pairs={{0,16},{16,32},{32,48},{48,64},{64,80},{80,96},{96,112},{112,128},... | collective-permute-start | bytes 786440 | tf_op jit(solution)/shard_map/ppermute | solution.py:106
  14.8 8.0 %collective-permute-start.1 = (bf16[1,256,512]{2,1,0:T(8,128)(2,1)S(1)}, bf16[1,256,512]{2,1,0:T(8,128)(2,1)S(1)}, u32[]{:S(2)}, u32[]{:S(2)}) collective-permute-start(bf16[1,256,512]{2,1,0:T(8,128)(2,1)S(1)} %get-tuple-element.12), channel_id=1, source_target_pairs={{16,0},{32,16},{48,32},{64,48},{80,64},{96,80},{112,96},{128,112},... | collective-permute-start | bytes 786440 | tf_op jit(solution)/shard_map/ppermute | solution.py:107
  22.8 0.7 copy-start.2
  26.4 1.2 %copy-start.1 = (bf16[4,256,512]{2,1,0:T(8,128)(2,1)S(1)}, bf16[4,256,512]{2,1,0:T(8,128)(2,1)}, u32[]{:S(2)}) copy-start(bf16[4,256,512]{2,1,0:T(8,128)(2,1)} %cot_ref.1) | copy-start | bytes 3145732
  27.6 0.9 copy-start.3
  35.0 7.5 %collective-permute-start.4 = (bf16[16,9,16,128]{3,2,1,0:T(8,128)(2,1)S(1)}, bf16[16,9,16,128]{3,2,1,0:T(8,128)(2,1)S(1)}, u32[]{:S(2)}, u32[]{:S(2)}) collective-permute-start(bf16[16,9,16,128]{3,2,1,0:T(8,128)(2,1)S(1)} %get-tuple-element.7), channel_id=1, source_target_pairs={{0,16},{16,0},{1,17},{17,1},{2,18},{18,2},{3,19},{19,3},{4,20},{20... | collective-permute-start | bytes 1769480 | tf_op jit(solution)/shard_map/ppermute | solution.py:99
  84.4 17.3 %all-to-all-start.3 = ((f32[16,9,128]{2,1,0:T(8,128)}), f32[16,9,128]{2,1,0:T(8,128)S(1)}, u32[]{:S(2)}, u32[]{:S(2)}) async-start(f32[16,9,128]{2,1,0:T(8,128)} %broadcast_in_dim.15), calls=%async_computation.3 | async-start | bytes 262144 | tf_op jit(solution)/shard_map/all_to_all | solution.py:113
  89.8 18.5 %collective-permute-start.2 = (bf16[1,256,512]{2,1,0:T(8,128)(2,1)S(1)}, bf16[1,256,512]{2,1,0:T(8,128)(2,1)S(1)}, u32[]{:S(2)}, u32[]{:S(2)}) collective-permute-start(bf16[1,256,512]{2,1,0:T(8,128)(2,1)S(1)} %get-tuple-element.11), channel_id=1, source_target_pairs={{0,16},{16,32},{32,48},{48,64},{64,80},{80,96},{96,112},{112,128},... | collective-permute-start | bytes 786440 | tf_op jit(solution)/shard_map/ppermute | solution.py:106
  95.4 12.9 %collective-permute-start.3 = (bf16[1,256,512]{2,1,0:T(8,128)(2,1)S(1)}, bf16[1,256,512]{2,1,0:T(8,128)(2,1)S(1)}, u32[]{:S(2)}, u32[]{:S(2)}) collective-permute-start(bf16[1,256,512]{2,1,0:T(8,128)(2,1)S(1)} %get-tuple-element.10), channel_id=1, source_target_pairs={{16,0},{32,16},{48,32},{64,48},{80,64},{96,80},{112,96},{128,112},... | collective-permute-start | bytes 786440 | tf_op jit(solution)/shard_map/ppermute | solution.py:107
  101.7 10.7 %collective-permute-start.5 = (f32[16,9,128]{2,0,1:T(8,128)S(1)}, f32[16,9,128]{2,0,1:T(8,128)S(1)}, u32[]{:S(2)}, u32[]{:S(2)}) collective-permute-start(f32[16,9,128]{2,0,1:T(8,128)S(1)} %copy.12), channel_id=1, source_target_pairs={{0,16},{16,0},{1,17},{17,1},{2,18},{18,2},{3,19},{19,3},{4,20},{20... | collective-permute-start | bytes 221192 | tf_op jit(solution)/shard_map/ppermute | solution.py:99

commit v2 on v1

v2 whole, which is shorter than its diff:
```python
import jax
import jax.numpy as jnp
from jax import lax
from jax.experimental import pallas as pl
from jax.experimental.pallas import tpu as pltpu
from jax.sharding import Mesh
from jax.sharding import PartitionSpec as P

COLS = 128
CH = ("ch_0", "ch_1")
ROWS = ("z_far", "z_near", "core")
BF16 = jnp.bfloat16
F32 = jnp.float32


def dot(a, b, dims):
    return lax.dot_general(a, b, (dims, ((), ())), preferred_element_type=F32)


def side_shift(tile, across):
    lane = lax.broadcasted_iota(jnp.int32, tile.shape, 1)
    moved = pltpu.roll(tile.astype(F32), -across % COLS, 1)
    edge = COLS - 1 if across > 0 else 0
    return jnp.where(lane == edge, 0.0, moved).astype(tile.dtype)


def fill_shifted(out_ref, row, halves):
    half, cells = halves[0].shape
    for k, source in enumerate(halves):
        rows = slice(k * half, (k + 1) * half)
        out_ref[1, rows, pl.ds(row * cells, cells)] = source
        for image in range(cells // COLS):
            tile = source[:, image * COLS : (image + 1) * COLS]
            for side in (0, 2):
                out_ref[side, rows, pl.ds(row * cells + image * COLS, COLS)] = side_shift(tile, side - 1)


def grad_kernel(limits_ref, core_ref, low_hbm, feat_hbm, high_hbm, mine_ref, theirs_ref, cot_hbm,
                grad_ref, own_ref, other_ref, feat_ref, cot_ref, shifted_ref, flat_ref, sems):
    band, ch, cells = cot_ref.shape
    images = cells // COLS
    half = ch // 2
    sources = [low_hbm.at[0]] + [feat_hbm.at[h] for h in range(band)] + [high_hbm.at[0]]
    loads = [pltpu.make_async_copy(s, feat_ref.at[h], sems.at[h]) for h, s in enumerate(sources)]
    masks = [
        pltpu.make_async_copy(cot_hbm.at[h], cot_ref.at[h], sems.at[band + 2 + h]) for h in range(band)
    ]
    for load in loads + masks:
        load.start()
    near = pl.ds(pl.multiple_of(core_ref[0] * half, half), half)
    far = pl.ds(pl.multiple_of((1 - core_ref[0]) * half, half), half)
    for h in range(band + 2):
        loads[h].wait()
        fill_shifted(shifted_ref, h, [feat_ref[h, near], feat_ref[h, far]])
    for h in range(band):
        summed = None
        for r in range(3):
            for c in range(3):
                t = 3 * r + c
                w = jnp.concatenate(
                    [mine_ref[:, t].reshape(ch, half), theirs_ref[:, t].reshape(ch, half)], 1
                )
                x = shifted_ref[c, :, pl.ds((h + r) * cells, cells)]
                term = dot(w, x, ((1,), (0,)))
                summed = term if summed is None else summed + term
        center = jnp.sum(summed, 0, keepdims=True) / ch
        spread = jnp.sum(summed * summed, 0, keepdims=True) / ch - center * center
        inverse = lax.rsqrt(spread + 1e-06)
        normed = (summed - center) * inverse
        keep = jnp.concatenate(
            [jnp.full((1, COLS), jnp.where(h < limits_ref[n], 1.0, 0.0), F32) for n in range(images)], 1
        )
        masks[h].wait()
        masked = cot_ref[h].astype(F32) * keep
        total = jnp.sum(masked, 0, keepdims=True) / ch
        cross = jnp.sum(masked * normed, 0, keepdims=True) / ch
        grad = (inverse * (masked - total - normed * cross)).astype(BF16)
        grad_ref[h] = grad
        flat_ref[:, pl.ds(h * cells, cells)] = grad
    parts = own_ref.shape[0], own_ref.shape[2], half
    for r in range(3):
        for c in range(3):
            t = 3 * r + c
            tap = dot(flat_ref[...], shifted_ref[c, :, pl.ds(r * cells, band * cells)], ((1,), (1,)))
            own_ref[:, t] = tap[:, :half].reshape(parts)
            other_ref[:, t] = tap[:, half:].astype(BF16).reshape(parts)


def input_kernel(core_ref, low_ref, grad_ref, high_ref, mine_ref, theirs_ref, out_ref, shifted_ref, wt_ref):
    band, ch, cells = grad_ref.shape
    half = ch // 2
    near = pl.ds(pl.multiple_of(core_ref[0] * half, half), half)
    far = pl.ds(pl.multiple_of((1 - core_ref[0]) * half, half), half)
    fill_shifted(shifted_ref, 0, [low_ref[0]])
    for h in range(band):
        fill_shifted(shifted_ref, h + 1, [grad_ref[h]])
    fill_shifted(shifted_ref, band + 1, [high_ref[0]])
    for t in range(9):
        wt_ref[t, :half] = mine_ref[:, t].reshape(ch, half).T
        wt_ref[t, half:] = theirs_ref[:, t].reshape(ch, half).T
    for h in range(band):
        summed = None
        for r in range(3):
            for c in range(3):
                x = shifted_ref[2 - c, :, pl.ds((h + 2 - r) * cells, cells)]
                term = dot(wt_ref[3 * r + c], x, ((1,), (0,)))
                summed = term if summed is None else summed + term
        out_ref[h, near] = summed[:half].astype(BF16)
        out_ref[h, far] = summed[half:].astype(BF16)


def vmem(count):
    return [pl.BlockSpec(memory_space=pltpu.VMEM)] * count


def smem(count):
    return [pl.BlockSpec(memory_space=pltpu.SMEM)] * count


def in_hbm(block):
    return pltpu.with_memory_space_constraint(block, pltpu.HBM)


HBM = pl.BlockSpec(memory_space=pltpu.HBM)


def work(block, convs):
    band, ch, cells = block.shape
    return pl.CostEstimate(
        flops=convs * 18 * ch * ch * band * cells, bytes_accessed=convs << 22, transcendentals=0
    )


def call_grad(limits, core, low, features, high, mine, theirs, cotangent):
    band, ch, cells = features.shape
    return pl.pallas_call(
        grad_kernel,
        in_specs=smem(2) + [HBM] * 3 + vmem(2) + [HBM],
        out_specs=vmem(3),
        out_shape=[
            jax.ShapeDtypeStruct(features.shape, BF16),
            jax.ShapeDtypeStruct(mine.shape, F32),
            jax.ShapeDtypeStruct(mine.shape, BF16),
        ],
        scratch_shapes=[
            pltpu.VMEM((band + 2, ch, cells), BF16),
            pltpu.VMEM(features.shape, BF16),
            pltpu.VMEM((3, ch, (band + 2) * cells), BF16),
            pltpu.VMEM((ch, band * cells), BF16),
            pltpu.SemaphoreType.DMA((2 * band + 2,)),
        ],
        cost_estimate=work(features, 2),
        compiler_params=pltpu.CompilerParams(vmem_limit_bytes=24 << 20),
        name="grad",
    )(limits, core, *map(in_hbm, (low, features, high)), mine, theirs, in_hbm(cotangent))


def call_input(core, low, grad, high, mine, theirs):
    band, ch, cells = grad.shape
    return pl.pallas_call(
        input_kernel,
        in_specs=smem(1) + vmem(5),
        out_specs=vmem(1)[0],
        out_shape=jax.ShapeDtypeStruct(grad.shape, BF16),
        scratch_shapes=[
            pltpu.VMEM((3, ch, (band + 2) * cells), BF16),
            pltpu.VMEM((9, ch, ch), BF16),
        ],
        cost_estimate=work(grad, 1),
        compiler_params=pltpu.CompilerParams(vmem_limit_bytes=20 << 20),
        name="input",
    )(core, low, grad, high, mine, theirs)


def exchange(block):
    return lax.ppermute(block, "core", [(0, 1), (1, 0)])


def band_edges(block):
    count = lax.axis_size(ROWS)
    forward = [(i, i + 1) for i in range(count - 1)]
    backward = [(target, source) for source, target in forward]
    low = lax.ppermute(block[-1:], ROWS, forward)
    high = lax.ppermute(block[:1], ROWS, backward)
    return low, high


def to_all(block, axis):
    peers = lax.axis_size(axis)
    return lax.all_to_all(jnp.broadcast_to(block[None], (peers, *block.shape)), axis, 0, 0, tiled=True)


def body(features, conv_weight, cotangent, valid_rows):
    band, ch, cells = features.shape
    images = cells // COLS
    near = conv_weight.shape[2]
    half = ch // 2
    core = lax.axis_index("core").astype(jnp.int32)
    limits = lax.dynamic_slice_in_dim(valid_rows, lax.axis_index(CH) * images, images, 0)
    limits = limits - lax.axis_index(ROWS) * band
    share = lax.dynamic_slice_in_dim(conv_weight, core * half, half, 3).reshape(9, near, half)
    mine = to_all(share, CH)
    low, high = band_edges(features)
    mine, low, high = lax.optimization_barrier((mine, low, high))
    theirs = exchange(mine)
    core = core.reshape(1)
    grad_pre, own, other = call_grad(limits, core, low, features, high, mine, theirs, cotangent)
    grad_low, grad_high = band_edges(grad_pre)
    pair = (own + exchange(other).astype(F32)).astype(BF16)
    plane = lax.all_to_all(pair, CH, 0, 0, tiled=True)
    plane, grad_low, grad_high = lax.optimization_barrier((plane, grad_low, grad_high))
    input_grad = call_input(core, grad_low, grad_pre, grad_high, mine, theirs)
    plane = plane.astype(F32).sum(0)
    lines = plane.reshape(lax.axis_size("z_near"), -1, half)
    block = lax.all_to_all(lines, "z_near", 0, 0, tiled=True).sum(0)
    block, input_grad = lax.optimization_barrier((to_all(block, "z_far"), input_grad))
    block = block.sum(0)
    whole = to_all(block, ("z_near", "core")).reshape(-1, 2, *block.shape)
    weight_grad = whole.swapaxes(1, 2).reshape(3, 3, near, ch)
    return input_grad, weight_grad


def solution(mesh):
    names = ("z_far", "z_near", "core", "ch_0", "ch_1")
    split = Mesh(mesh.devices.reshape(4, 4, 2, 4, 4), names)
    placed = (P(ROWS, None, CH), P(None, None, CH, None), P(ROWS, None, CH), P())
    return jax.shard_map(
        body,
        mesh=split,
        in_specs=placed,
        out_specs=(P(ROWS, None, CH), P(None, None, CH, None)),
        check_vma=False,
    )
```

time: 114 us -> 110 us (0.965)
  blocking collectives: 40.9 us -> 26 us
  waiting for transfers between devices: 14.9 us -> 22.9 us
  Pallas kernels: 10.5 us -> 14.4 us
  local copies, waits for them, and re-layouts: 5.67 us -> 3.38 us
  starting transfers between devices: 39.3 us -> 40.7 us
    all_to_all x2, blocking collectives: 40.9 us -> 26 us  [the longest x1 13.5 us: to_all(): lax.all_to_all(jnp.broadcast_to(block[None], (peers, *block.shape)), axis...]
    ppermute x2, starting transfers between devices: 12.4 us -> 5 us  [exchange(): return lax.ppermute(block, 'core', [(0, 1), (1, 0)])]
    all_to_all x0 -> x1, starting transfers between devices: none -> 6.18 us  [body(): plane = lax.all_to_all(pair, CH, 0, 0, tiled=True)]
    ppermute x2, waiting for transfers between devices: 4.69 us -> 9.38 us  [band_edges(): high = lax.ppermute(block[:1], ROWS, backward)]
    all_to_all x2, starting transfers between devices: 13 us -> 17.4 us  [to_all(): lax.all_to_all(jnp.broadcast_to(block[None], (peers, *block.shape)), axis...]
    pallas_call x2, Pallas kernels: 10.5 us -> 14.4 us  [the longest x1 10.2 us: call_grad(): pl.pallas_call(grad_kernel, in_specs=smem(2) + [HBM] * 3 + vmem(2) + [HBM...]
    unnamed x10, local copies, waits for them, and re-layouts: 2.88 us -> 0.88 us
    ppermute x2, starting transfers between devices: 10 us -> 8.25 us  [band_edges(): low = lax.ppermute(block[-1:], ROWS, forward)]
  transfers between devices with their start and end apart: 8 -> 9, of which waited for: 5 -> 7; matrix products, arithmetic and copies ran while one was open for 0% -> 0% of each run, Pallas kernels for 4% -> 4%
where the time goes in v2:
time: 110 us; the launch traced here: 109 us
  starting transfers between devices  40.7 us (37%)
  blocking collectives  26 us (24%)
  waiting for transfers between devices  22.9 us (21%)
  Pallas kernels  14.4 us (13%)
  local copies, waits for them, and re-layouts  3.38 us (3%)
  other arithmetic  1.11 us (1%)
    all_to_all x2, starting transfers between devices, to_all(): lax.all_to_all(jnp.broadcast_to(block[None], (peers, *block.shape)), axis...  17.4 us
    all_to_all x1, blocking collectives, to_all(): lax.all_to_all(jnp.broadcast_to(block[None], (peers, *block.shape)), axis...  13.5 us
    all_to_all x1, blocking collectives, body(): block = lax.all_to_all(lines, 'z_near', 0, 0, tiled=True).sum(0)  12.5 us
    pallas_call x1, Pallas kernels, call_grad(): pl.pallas_call(grad_kernel, in_specs=smem(2) + [HBM] * 3 + vmem(2) + [HBM...  10.2 us
    ppermute x2, waiting for transfers between devices, band_edges(): high = lax.ppermute(block[:1], ROWS, backward)  9.38 us
    ppermute x2, starting transfers between devices, band_edges(): low = lax.ppermute(block[-1:], ROWS, forward)  8.25 us
    all_to_all x2, waiting for transfers between devices, to_all(): lax.all_to_all(jnp.broadcast_to(block[None], (peers, *block.shape)), axis...  7.66 us
    all_to_all x1, starting transfers between devices, body(): plane = lax.all_to_all(pair, CH, 0, 0, tiled=True)  6.18 us
  transfers between devices with their start and end apart: 9, of which 7 were waited for; matrix products, arithmetic and copies ran while one was open for 0% of the time, Pallas kernels for 4%

profile of v2, /device:TPU:1, one launch (start us, length us, event | category | flops | bytes accessed | tf_op | source)
XLA Modules:
  0.0 109.3 jit_solution(9012723128144984440)
XLA Ops:
  0.6 0.0 copy-start
  0.6 0.0 copy-start.1
  0.7 0.9 copy-done
  1.5 0.9 broadcast_in_dim.9
  2.4 7.7 %all-to-all-start = ((bf16[16,9,16,128]{3,2,1,0:T(8,128)(2,1)}), bf16[16,9,16,128]{3,2,1,0:T(8,128)(2,1)S(1)}, u32[]{:S(2)}, u32[]{:S(2)}) async-start(bf16[16,9,16,128]{3,2,1,0:T(8,128)(2,1)} %broadcast_in_dim.9), calls=%async_computation | async-start | bytes 1179648 | tf_op jit(solution)/shard_map/all_to_all | solution.py:190
  10.2 4.4 %collective-permute-start = (bf16[1,256,512]{2,1,0:T(8,128)(2,1)S(1)}, bf16[1,256,512]{2,1,0:T(8,128)(2,1)S(1)}, u32[]{:S(2)}, u32[]{:S(2)}) collective-permute-start(bf16[1,256,512]{2,1,0:T(8,128)(2,1)S(1)} %get-tuple-element.27), channel_id=1, source_target_pairs={{0,16},{16,32},{32,48},{48,64},{64,80},{80,96},{96,112},{112,128},... | collective-permute-start | bytes 786440 | tf_op jit(solution)/shard_map/ppermute | solution.py:183
  14.6 1.9 %collective-permute-start.1 = (bf16[1,256,512]{2,1,0:T(8,128)(2,1)S(1)}, bf16[1,256,512]{2,1,0:T(8,128)(2,1)S(1)}, u32[]{:S(2)}, u32[]{:S(2)}) collective-permute-start(bf16[1,256,512]{2,1,0:T(8,128)(2,1)S(1)} %get-tuple-element.26), channel_id=1, source_target_pairs={{16,0},{32,16},{48,32},{64,48},{80,64},{96,80},{112,96},{128,112},... | collective-permute-start | bytes 786440 | tf_op jit(solution)/shard_map/ppermute | solution.py:184
  16.5 1.4 %collective-permute-done.low_hbm = bf16[1,256,512]{2,1,0:T(8,128)(2,1)S(1)} collective-permute-done((bf16[1,256,512]{2,1,0:T(8,128)(2,1)S(1)}, bf16[1,256,512]{2,1,0:T(8,128)(2,1)S(1)}, u32[]{:S(2)}, u32[]{:S(2)}) %collective-permute-start) | collective-permute-done | bytes 262176 | tf_op jit(solution)/shard_map/ppermute | solution.py:183
  17.9 4.7 %collective-permute-done.1.high_hbm = bf16[1,256,512]{2,1,0:T(8,128)(2,1)S(1)} collective-permute-done((bf16[1,256,512]{2,1,0:T(8,128)(2,1)S(1)}, bf16[1,256,512]{2,1,0:T(8,128)(2,1)S(1)}, u32[]{:S(2)}, u32[]{:S(2)}) %collective-permute-start.1) | collective-permute-done | bytes 262176 | tf_op jit(solution)/shard_map/ppermute | solution.py:184
  22.6 0.0 all-to-all-done.mine_ref
  22.6 2.7 %collective-permute-start.2 = (bf16[16,9,16,128]{3,2,1,0:T(8,128)(2,1)S(1)}, bf16[16,9,16,128]{3,2,1,0:T(8,128)(2,1)S(1)}, u32[]{:S(2)}, u32[]{:S(2)}) collective-permute-start(bf16[16,9,16,128]{3,2,1,0:T(8,128)(2,1)S(1)} %all-to-all-done.mine_ref), channel_id=1, source_target_pairs={{0,16},{16,0},{1,17},{17,1},{2,18},{18,2},{3,19},{19,3},{4,20},{20... | collective-permute-start | bytes 1769480 | tf_op jit(solution)/shard_map/ppermute | solution.py:176
  25.3 0.1 dynamic-slice_subtract_fusion.limits_ref
  25.4 1.5 %collective-permute-done.2.theirs_ref = bf16[16,9,16,128]{3,2,1,0:T(8,128)(2,1)S(1)} collective-permute-done((bf16[16,9,16,128]{3,2,1,0:T(8,128)(2,1)S(1)}, bf16[16,9,16,128]{3,2,1,0:T(8,128)(2,1)S(1)}, u32[]{:S(2)}, u32[]{:S(2)}) %collective-permute-start.2) | collective-permute-done | bytes 589856 | tf_op jit(solution)/shard_map/ppermute | solution.py:176
  26.9 10.2 %grad.1 = (bf16[4,256,512]{2,1,0:T(8,128)(2,1)S(1)}, f32[16,9,16,128]{3,2,1,0:T(8,128)S(1)}, bf16[16,9,16,128]{3,2,1,0:T(8,128)(2,1)S(1)}) custom-call(s32[4]{0:T(128)S(1)} %dynamic-slice_subtract_fusion.limits_ref, s32[1]{0:T(128)} %bitcast.core_ref, bf16[1,256,512]{2,1,0:T(8,128)(2,1)} %copy-done.3, bf16[4,256,512]{2,1,0:T(8,128)(2,1)} %feat_hbm.1, ...), custom_call_target="tpu_custom_call" | custom-call | flops 4831838208 | bytes 8388608 | tf_op jit(solution)/shard_map/grad/pallas_call | solution.py:136
  37.1 2.3 %collective-permute-start.3 = (bf16[16,9,16,128]{3,2,1,0:T(8,128)(2,1)S(1)}, bf16[16,9,16,128]{3,2,1,0:T(8,128)(2,1)S(1)}, u32[]{:S(2)}, u32[]{:S(2)}) collective-permute-start(bf16[16,9,16,128]{3,2,1,0:T(8,128)(2,1)S(1)} %get-tuple-element.17), channel_id=1, source_target_pairs={{0,16},{16,0},{1,17},{17,1},{2,18},{18,2},{3,19},{19,3},{4,20},{20... | collective-permute-start | bytes 1769480 | tf_op jit(solution)/shard_map/ppermute | solution.py:176
  39.4 1.6 %collective-permute-done.3 = bf16[16,9,16,128]{3,2,1,0:T(8,128)(2,1)S(1)} collective-permute-done((bf16[16,9,16,128]{3,2,1,0:T(8,128)(2,1)S(1)}, bf16[16,9,16,128]{3,2,1,0:T(8,128)(2,1)S(1)}, u32[]{:S(2)}, u32[]{:S(2)}) %collective-permute-start.3) | collective-permute-done | bytes 589856 | tf_op jit(solution)/shard_map/ppermute | solution.py:176
  41.0 0.9 add_convert_fusion
  42.0 6.2 %all-to-all-start.1 = ((bf16[16,9,16,128]{3,2,1,0:T(8,128)(2,1)}), bf16[16,9,16,128]{3,2,1,0:T(8,128)(2,1)S(1)}, u32[]{:S(2)}, u32[]{:S(2)}) async-start(bf16[16,9,16,128]{3,2,1,0:T(8,128)(2,1)} %add_convert_fusion), calls=%async_computation.1 | async-start | bytes 1179648 | tf_op jit(solution)/shard_map/all_to_all | solution.py:210
  48.2 3.9 %collective-permute-start.4 = (bf16[1,256,512]{2,1,0:T(8,128)(2,1)S(1)}, bf16[1,256,512]{2,1,0:T(8,128)(2,1)S(1)}, u32[]{:S(2)}, u32[]{:S(2)}) collective-permute-start(bf16[1,256,512]{2,1,0:T(8,128)(2,1)S(1)} %get-tuple-element.25), channel_id=1, source_target_pairs={{0,16},{16,32},{32,48},{48,64},{64,80},{80,96},{96,112},{112,128},... | collective-permute-start | bytes 786440 | tf_op jit(solution)/shard_map/ppermute | solution.py:183
  52.1 1.9 %collective-permute-start.5 = (bf16[1,256,512]{2,1,0:T(8,128)(2,1)S(1)}, bf16[1,256,512]{2,1,0:T(8,128)(2,1)S(1)}, u32[]{:S(2)}, u32[]{:S(2)}) collective-permute-start(bf16[1,256,512]{2,1,0:T(8,128)(2,1)S(1)} %get-tuple-element.24), channel_id=1, source_target_pairs={{16,0},{32,16},{48,32},{64,48},{80,64},{96,80},{112,96},{128,112},... | collective-permute-start | bytes 786440 | tf_op jit(solution)/shard_map/ppermute | solution.py:184
  54.0 1.4 %collective-permute-done.4.low_ref = bf16[1,256,512]{2,1,0:T(8,128)(2,1)S(1)} collective-permute-done((bf16[1,256,512]{2,1,0:T(8,128)(2,1)S(1)}, bf16[1,256,512]{2,1,0:T(8,128)(2,1)S(1)}, u32[]{:S(2)}, u32[]{:S(2)}) %collective-permute-start.4) | collective-permute-done | bytes 262176 | tf_op jit(solution)/shard_map/ppermute | solution.py:183
  55.4 4.7 %collective-permute-done.5.high_ref = bf16[1,256,512]{2,1,0:T(8,128)(2,1)S(1)} collective-permute-done((bf16[1,256,512]{2,1,0:T(8,128)(2,1)S(1)}, bf16[1,256,512]{2,1,0:T(8,128)(2,1)S(1)}, u32[]{:S(2)}, u32[]{:S(2)}) %collective-permute-start.5) | collective-permute-done | bytes 262176 | tf_op jit(solution)/shard_map/ppermute | solution.py:184
  60.1 0.0 all-to-all-done.1
  60.1 0.1 convert_reduce_fusion
  60.2 12.5 %all_to_all.25 = f32[4,36,128]{2,1,0:T(8,128)S(1)} all-to-all(f32[4,36,128]{2,1,0:T(8,128)S(1)} %reshape.20), channel_id=1, replica_groups=mesh['z_far'=4,'z_near'=4,'core'=2,'ch_0'=4,'ch_1'=4] {'z_near'}, dimensions={0} | all-to-all | bytes 147456 | tf_op jit(solution)/shard_map/all_to_all | solution.py:215
  72.7 0.6 broadcast_in_dim.10
  73.3 9.7 %all-to-all-start.3 = ((f32[4,36,128]{2,1,0:T(8,128)}), f32[4,36,128]{2,1,0:T(8,128)S(1)}, u32[]{:S(2)}, u32[]{:S(2)}) async-start(f32[4,36,128]{2,1,0:T(8,128)} %broadcast_in_dim.10), calls=%async_computation.3 | async-start | bytes 163840 | tf_op jit(solution)/shard_map/all_to_all | solution.py:190
  83.0 4.1 %input.1 = bf16[4,256,512]{2,1,0:T(8,128)(2,1)} custom-call(s32[1]{0:T(128)} %bitcast.core_ref, bf16[1,256,512]{2,1,0:T(8,128)(2,1)S(1)} %collective-permute-done.4.low_ref, bf16[4,256,512]{2,1,0:T(8,128)(2,1)S(1)} %get-tuple-element.18.grad_ref, bf16[1,256,512]{2,1,0:T(8,128)(2,1)S(1)} %collective-permute-done.5.high_ref, ...), custom_call_target="tpu_custom_call" | custom-call | flops 2415919104 | bytes 4194304 | tf_op jit(solution)/shard_map/input/pallas_call | solution.py:160
  87.2 7.7 %all-to-all-done.3 = f32[4,36,128]{2,1,0:T(8,128)S(1)} async-done(((f32[4,36,128]{2,1,0:T(8,128)}), f32[4,36,128]{2,1,0:T(8,128)S(1)}, u32[]{:S(2)}, u32[]{:S(2)}) %all-to-all-start.3) | async-done | bytes 73760 | tf_op jit(solution)/shard_map/all_to_all | solution.py:190
  94.9 13.5 %all_to_all.26 = f32[8,36,128]{2,1,0:T(8,128)S(1)} all-to-all(f32[8,36,128]{2,1,0:T(8,128)S(1)} %broadcast_in_dim.22), channel_id=1, replica_groups=mesh['z_far'=4,'z_near'=4,'core'=2,'ch_0'=4,'ch_1'=4] {'z_near','core'}, dimensions={0} | all-to-all | bytes 294912 | tf_op jit(solution)/shard_map/all_to_all | solution.py:190
  108.4 0.1 copy.8
  108.5 0.8 reshape.22
  (15 shorter events, 0.2 us)
Async XLA Ops:
  0.6 0.9 copy-start
  0.6 9.5 %copy-start.1 = (bf16[4,256,512]{2,1,0:T(8,128)(2,1)S(1)}, bf16[4,256,512]{2,1,0:T(8,128)(2,1)}, u32[]{:S(2)}) copy-start(bf16[4,256,512]{2,1,0:T(8,128)(2,1)} %feat_hbm.1) | copy-start | bytes 3145732
  2.4 22.9 %copy-start.2 = (s32[64]{0:T(128)S(1)}, s32[64]{0:T(128)}, u32[]{:S(2)}) copy-start(s32[64]{0:T(128)} %param.7) | copy-start | bytes 772
  2.4 20.2 %all-to-all-start = ((bf16[16,9,16,128]{3,2,1,0:T(8,128)(2,1)}), bf16[16,9,16,128]{3,2,1,0:T(8,128)(2,1)S(1)}, u32[]{:S(2)}, u32[]{:S(2)}) async-start(bf16[16,9,16,128]{3,2,1,0:T(8,128)(2,1)} %broadcast_in_dim.9), calls=%async_computation | async-start | bytes 1179648 | tf_op jit(solution)/shard_map/all_to_all | solution.py:190
  10.2 7.7 %collective-permute-start = (bf16[1,256,512]{2,1,0:T(8,128)(2,1)S(1)}, bf16[1,256,512]{2,1,0:T(8,128)(2,1)S(1)}, u32[]{:S(2)}, u32[]{:S(2)}) collective-permute-start(bf16[1,256,512]{2,1,0:T(8,128)(2,1)S(1)} %get-tuple-element.27), channel_id=1, source_target_pairs={{0,16},{16,32},{32,48},{48,64},{64,80},{80,96},{96,112},{112,128},... | collective-permute-start | bytes 786440 | tf_op jit(solution)/shard_map/ppermute | solution.py:183
  14.6 8.0 %collective-permute-start.1 = (bf16[1,256,512]{2,1,0:T(8,128)(2,1)S(1)}, bf16[1,256,512]{2,1,0:T(8,128)(2,1)S(1)}, u32[]{:S(2)}, u32[]{:S(2)}) collective-permute-start(bf16[1,256,512]{2,1,0:T(8,128)(2,1)S(1)} %get-tuple-element.26), channel_id=1, source_target_pairs={{16,0},{32,16},{48,32},{64,48},{80,64},{96,80},{112,96},{128,112},... | collective-permute-start | bytes 786440 | tf_op jit(solution)/shard_map/ppermute | solution.py:184
  17.9 9.0 %copy-start.3 = (bf16[1,256,512]{2,1,0:T(8,128)(2,1)}, bf16[1,256,512]{2,1,0:T(8,128)(2,1)S(1)}, u32[]{:S(2)}) copy-start(bf16[1,256,512]{2,1,0:T(8,128)(2,1)S(1)} %collective-permute-done.low_hbm) | copy-start | bytes 786436
  22.6 4.3 %copy-start.4 = (bf16[1,256,512]{2,1,0:T(8,128)(2,1)}, bf16[1,256,512]{2,1,0:T(8,128)(2,1)S(1)}, u32[]{:S(2)}) copy-start(bf16[1,256,512]{2,1,0:T(8,128)(2,1)S(1)} %collective-permute-done.1.high_hbm) | copy-start | bytes 786436
  22.6 4.3 %collective-permute-start.2 = (bf16[16,9,16,128]{3,2,1,0:T(8,128)(2,1)S(1)}, bf16[16,9,16,128]{3,2,1,0:T(8,128)(2,1)S(1)}, u32[]{:S(2)}, u32[]{:S(2)}) collective-permute-start(bf16[16,9,16,128]{3,2,1,0:T(8,128)(2,1)S(1)} %all-to-all-done.mine_ref), channel_id=1, source_target_pairs={{0,16},{16,0},{1,17},{17,1},{2,18},{18,2},{3,19},{19,3},{4,20},{20... | collective-permute-start | bytes 1769480 | tf_op jit(solution)/shard_map/ppermute | solution.py:176
  37.1 3.9 %collective-permute-start.3 = (bf16[16,9,16,128]{3,2,1,0:T(8,128)(2,1)S(1)}, bf16[16,9,16,128]{3,2,1,0:T(8,128)(2,1)S(1)}, u32[]{:S(2)}, u32[]{:S(2)}) collective-permute-start(bf16[16,9,16,128]{3,2,1,0:T(8,128)(2,1)S(1)} %get-tuple-element.17), channel_id=1, source_target_pairs={{0,16},{16,0},{1,17},{17,1},{2,18},{18,2},{3,19},{19,3},{4,20},{20... | collective-permute-start | bytes 1769480 | tf_op jit(solution)/shard_map/ppermute | solution.py:176
  42.0 18.1 %all-to-all-start.1 = ((bf16[16,9,16,128]{3,2,1,0:T(8,128)(2,1)}), bf16[16,9,16,128]{3,2,1,0:T(8,128)(2,1)S(1)}, u32[]{:S(2)}, u32[]{:S(2)}) async-start(bf16[16,9,16,128]{3,2,1,0:T(8,128)(2,1)} %add_convert_fusion), calls=%async_computation.1 | async-start | bytes 1179648 | tf_op jit(solution)/shard_map/all_to_all | solution.py:210
  48.2 7.2 %collective-permute-start.4 = (bf16[1,256,512]{2,1,0:T(8,128)(2,1)S(1)}, bf16[1,256,512]{2,1,0:T(8,128)(2,1)S(1)}, u32[]{:S(2)}, u32[]{:S(2)}) collective-permute-start(bf16[1,256,512]{2,1,0:T(8,128)(2,1)S(1)} %get-tuple-element.25), channel_id=1, source_target_pairs={{0,16},{16,32},{32,48},{48,64},{64,80},{80,96},{96,112},{112,128},... | collective-permute-start | bytes 786440 | tf_op jit(solution)/shard_map/ppermute | solution.py:183
  52.1 8.0 %collective-permute-start.5 = (bf16[1,256,512]{2,1,0:T(8,128)(2,1)S(1)}, bf16[1,256,512]{2,1,0:T(8,128)(2,1)S(1)}, u32[]{:S(2)}, u32[]{:S(2)}) collective-permute-start(bf16[1,256,512]{2,1,0:T(8,128)(2,1)S(1)} %get-tuple-element.24), channel_id=1, source_target_pairs={{16,0},{32,16},{48,32},{64,48},{80,64},{96,80},{112,96},{128,112},... | collective-permute-start | bytes 786440 | tf_op jit(solution)/shard_map/ppermute | solution.py:184
  73.3 21.5 %all-to-all-start.3 = ((f32[4,36,128]{2,1,0:T(8,128)}), f32[4,36,128]{2,1,0:T(8,128)S(1)}, u32[]{:S(2)}, u32[]{:S(2)}) async-start(f32[4,36,128]{2,1,0:T(8,128)} %broadcast_in_dim.10), calls=%async_computation.3 | async-start | bytes 163840 | tf_op jit(solution)/shard_map/all_to_all | solution.py:190

commit v3 on v2

--- a/solution.py
+++ b/solution.py
@@ -49,8 +49,9 @@
         load.start()
     near = pl.ds(pl.multiple_of(core_ref[0] * half, half), half)
     far = pl.ds(pl.multiple_of((1 - core_ref[0]) * half, half), half)
+    for load in loads + masks:
+        load.wait()
     for h in range(band + 2):
-        loads[h].wait()
         fill_shifted(shifted_ref, h, [feat_ref[h, near], feat_ref[h, far]])
     for h in range(band):
         summed = None
@@ -70,7 +71,6 @@
         keep = jnp.concatenate(
             [jnp.full((1, COLS), jnp.where(h < limits_ref[n], 1.0, 0.0), F32) for n in range(images)], 1
         )
-        masks[h].wait()
         masked = cot_ref[h].astype(F32) * keep
         total = jnp.sum(masked, 0, keepdims=True) / ch
         cross = jnp.sum(masked * normed, 0, keepdims=True) / ch
@@ -185,9 +185,12 @@
     return low, high
 
 
-def to_all(block, axis):
-    peers = lax.axis_size(axis)
-    return lax.all_to_all(jnp.broadcast_to(block[None], (peers, *block.shape)), axis, 0, 0, tiled=True)
+def copies(block, axis):
+    return jnp.broadcast_to(block[None], (lax.axis_size(axis), *block.shape))
+
+
+def swap(parts, axis):
+    return lax.all_to_all(parts, axis, 0, 0, tiled=True)
 
 
 def body(features, conv_weight, cotangent, valid_rows):
@@ -199,23 +202,23 @@
     limits = lax.dynamic_slice_in_dim(valid_rows, lax.axis_index(CH) * images, images, 0)
     limits = limits - lax.axis_index(ROWS) * band
     share = lax.dynamic_slice_in_dim(conv_weight, core * half, half, 3).reshape(9, near, half)
-    mine = to_all(share, CH)
     low, high = band_edges(features)
-    mine, low, high = lax.optimization_barrier((mine, low, high))
+    parts, low, high = lax.optimization_barrier((copies(share, CH), low, high))
+    mine = swap(parts, CH)
     theirs = exchange(mine)
     core = core.reshape(1)
     grad_pre, own, other = call_grad(limits, core, low, features, high, mine, theirs, cotangent)
+    pair = (own + exchange(other).astype(F32)).astype(BF16)
+    plane = swap(pair, CH).astype(F32).sum(0)
+    lines = plane.reshape(lax.axis_size("z_near"), -1, half)
+    block = copies(swap(lines, "z_near").sum(0), "z_far")
+    block, grad_pre = lax.optimization_barrier((block, grad_pre))
     grad_low, grad_high = band_edges(grad_pre)
-    pair = (own + exchange(other).astype(F32)).astype(BF16)
-    plane = lax.all_to_all(pair, CH, 0, 0, tiled=True)
-    plane, grad_low, grad_high = lax.optimization_barrier((plane, grad_low, grad_high))
     input_grad = call_input(core, grad_low, grad_pre, grad_high, mine, theirs)
-    plane = plane.astype(F32).sum(0)
-    lines = plane.reshape(lax.axis_size("z_near"), -1, half)
-    block = lax.all_to_all(lines, "z_near", 0, 0, tiled=True).sum(0)
-    block, input_grad = lax.optimization_barrier((to_all(block, "z_far"), input_grad))
-    block = block.sum(0)
-    whole = to_all(block, ("z_near", "core")).reshape(-1, 2, *block.shape)
+    block = swap(block, "z_far")
+    block, input_grad = lax.optimization_barrier((block, input_grad))
+    pieces = ("z_near", "core")
+    whole = swap(copies(block.sum(0), pieces), pieces).reshape(-1, 2, *block.shape[1:])
     weight_grad = whole.swapaxes(1, 2).reshape(3, 3, near, ch)
     return input_grad, weight_grad
 

time: 110 us -> 118 us (1.073)
  blocking collectives: 26 us -> 52.3 us
  waiting for transfers between devices: 22.9 us -> 14.6 us
  starting transfers between devices: 40.7 us -> 33.9 us
  Pallas kernels: 14.4 us -> 12.4 us
    all_to_all x2 -> x4, blocking collectives: 26 us -> 52.3 us  [swap(): return lax.all_to_all(parts, axis, 0, 0, tiled=True)]
    all_to_all x3 -> x1, starting transfers between devices: 23.6 us -> 11.7 us  [swap(): return lax.all_to_all(parts, axis, 0, 0, tiled=True)]
    ppermute x2, starting transfers between devices: 3.84 us -> 13.9 us  [band_edges(): high = lax.ppermute(block[:1], ROWS, backward)]
    ppermute x2, waiting for transfers between devices: 9.38 us -> 0.01 us  [band_edges(): high = lax.ppermute(block[:1], ROWS, backward)]
    ppermute x2, starting transfers between devices: 8.25 us -> 4.45 us  [band_edges(): low = lax.ppermute(block[-1:], ROWS, forward)]
    pallas_call x1, Pallas kernels: 10.2 us -> 8.32 us  [call_grad(): pl.pallas_call(grad_kernel, in_specs=smem(2) + [HBM] * 3 + vmem(2) + [HBM...]
    all_to_all x3 -> x1, waiting for transfers between devices: 7.66 us -> 7.69 us  [swap(): return lax.all_to_all(parts, axis, 0, 0, tiled=True)]
  transfers between devices with their start and end apart: 9 -> 7, of which waited for: 7 -> 4; matrix products, arithmetic and copies ran while one was open for 0% -> 0% of each run, Pallas kernels for 4% -> 4%
where the time goes in v3:
time: 118 us; the launch traced here: 117 us
  blocking collectives  52.3 us (44%)
  starting transfers between devices  33.9 us (29%)
  waiting for transfers between devices  14.6 us (12%)
  Pallas kernels  12.4 us (11%)
  local copies, waits for them, and re-layouts  2.77 us (2%)
    all_to_all x4, blocking collectives, swap(): return lax.all_to_all(parts, axis, 0, 0, tiled=True)  52.3 us
    ppermute x2, starting transfers between devices, band_edges(): high = lax.ppermute(block[:1], ROWS, backward)  13.9 us
    all_to_all x1, starting transfers between devices, swap(): return lax.all_to_all(parts, axis, 0, 0, tiled=True)  11.7 us
    pallas_call x1, Pallas kernels, call_grad(): pl.pallas_call(grad_kernel, in_specs=smem(2) + [HBM] * 3 + vmem(2) + [HBM...  8.32 us
    all_to_all x1, waiting for transfers between devices, swap(): return lax.all_to_all(parts, axis, 0, 0, tiled=True)  7.69 us
    ppermute x2, starting transfers between devices, band_edges(): low = lax.ppermute(block[-1:], ROWS, forward)  4.45 us
    pallas_call x1, Pallas kernels, call_input(): pl.pallas_call(input_kernel, in_specs=smem(1) + vmem(5), out_specs=vmem(1...  4.11 us
    ppermute x2, starting transfers between devices, exchange(): return lax.ppermute(block, 'core', [(0, 1), (1, 0)])  3.95 us
  transfers between devices with their start and end apart: 7, of which 4 were waited for; matrix products, arithmetic and copies ran while one was open for 0% of the time, Pallas kernels for 4%

profile of v3, /device:TPU:1, one launch (start us, length us, event | category | flops | bytes accessed | tf_op | source)
XLA Modules:
  0.0 117.2 jit_solution(11634222566769419088)
XLA Ops:
  0.6 0.0 copy-start
  0.6 1.1 fusion.1
  1.7 0.0 copy-start.1
  1.8 8.7 %collective-permute-start.1 = (bf16[1,256,512]{2,1,0:T(8,128)(2,1)S(1)}, bf16[1,256,512]{2,1,0:T(8,128)(2,1)S(1)}, u32[]{:S(2)}, u32[]{:S(2)}) collective-permute-start(bf16[1,256,512]{2,1,0:T(8,128)(2,1)S(1)} %get-tuple-element.24), channel_id=1, source_target_pairs={{16,0},{32,16},{48,32},{64,48},{80,64},{96,80},{112,96},{128,112},... | collective-permute-start | bytes 786440 | tf_op jit(solution)/shard_map/ppermute | solution.py:184
  10.5 1.9 %collective-permute-start = (bf16[1,256,512]{2,1,0:T(8,128)(2,1)S(1)}, bf16[1,256,512]{2,1,0:T(8,128)(2,1)S(1)}, u32[]{:S(2)}, u32[]{:S(2)}) collective-permute-start(bf16[1,256,512]{2,1,0:T(8,128)(2,1)S(1)} %get-tuple-element.25), channel_id=1, source_target_pairs={{0,16},{16,32},{32,48},{48,64},{64,80},{80,96},{96,112},{112,128},... | collective-permute-start | bytes 786440 | tf_op jit(solution)/shard_map/ppermute | solution.py:183
  12.5 0.0 collective-permute-done.1.high_hbm
  12.5 0.0 copy-start.2
  12.5 3.2 %collective-permute-done.low_hbm = bf16[1,256,512]{2,1,0:T(8,128)(2,1)S(1)} collective-permute-done((bf16[1,256,512]{2,1,0:T(8,128)(2,1)S(1)}, bf16[1,256,512]{2,1,0:T(8,128)(2,1)S(1)}, u32[]{:S(2)}, u32[]{:S(2)}) %collective-permute-start) | collective-permute-done | bytes 262176 | tf_op jit(solution)/shard_map/ppermute | solution.py:183
  15.7 0.1 broadcast_in_dim.9
  15.8 13.9 %all_to_all.25.mine_ref = bf16[16,9,16,128]{3,2,1,0:T(8,128)(2,1)S(1)} all-to-all(bf16[16,9,16,128]{3,2,1,0:T(8,128)(2,1)S(1)} %broadcast_in_dim.9), channel_id=1, replica_groups=mesh['z_far'=4,'z_near'=4,'core'=2,'ch_0'=4,'ch_1'=4] {'ch_0','ch_1'}, dimensions={0} | all-to-all | bytes 1179648 | tf_op jit(solution)/shard_map/all_to_all | solution.py:193
  29.7 1.9 %collective-permute-start.2 = (bf16[16,9,16,128]{3,2,1,0:T(8,128)(2,1)S(1)}, bf16[16,9,16,128]{3,2,1,0:T(8,128)(2,1)S(1)}, u32[]{:S(2)}, u32[]{:S(2)}) collective-permute-start(bf16[16,9,16,128]{3,2,1,0:T(8,128)(2,1)S(1)} %all_to_all.25.mine_ref), channel_id=1, source_target_pairs={{0,16},{16,0},{1,17},{17,1},{2,18},{18,2},{3,19},{19,3},{4,20},{20... | collective-permute-start | bytes 1769480 | tf_op jit(solution)/shard_map/ppermute | solution.py:176
  31.7 0.1 dynamic-slice_subtract_fusion.limits_ref
  31.7 1.9 %collective-permute-done.2.theirs_ref = bf16[16,9,16,128]{3,2,1,0:T(8,128)(2,1)S(1)} collective-permute-done((bf16[16,9,16,128]{3,2,1,0:T(8,128)(2,1)S(1)}, bf16[16,9,16,128]{3,2,1,0:T(8,128)(2,1)S(1)}, u32[]{:S(2)}, u32[]{:S(2)}) %collective-permute-start.2) | collective-permute-done | bytes 589856 | tf_op jit(solution)/shard_map/ppermute | solution.py:176
  33.6 0.0 copy-done.2
  33.6 8.3 %grad.1 = (bf16[4,256,512]{2,1,0:T(8,128)(2,1)S(1)}, f32[16,9,16,128]{3,2,1,0:T(8,128)S(1)}, bf16[16,9,16,128]{3,2,1,0:T(8,128)(2,1)S(1)}) custom-call(s32[4]{0:T(128)S(1)} %dynamic-slice_subtract_fusion.limits_ref, s32[1]{0:T(128)} %bitcast.core_ref, bf16[1,256,512]{2,1,0:T(8,128)(2,1)} %copy-done.3, bf16[4,256,512]{2,1,0:T(8,128)(2,1)} %feat_hbm.1, ...), custom_call_target="tpu_custom_call" | custom-call | flops 4831838208 | bytes 8388608 | tf_op jit(solution)/shard_map/grad/pallas_call | solution.py:136
  41.9 2.0 %collective-permute-start.3 = (bf16[16,9,16,128]{3,2,1,0:T(8,128)(2,1)S(1)}, bf16[16,9,16,128]{3,2,1,0:T(8,128)(2,1)S(1)}, u32[]{:S(2)}, u32[]{:S(2)}) collective-permute-start(bf16[16,9,16,128]{3,2,1,0:T(8,128)(2,1)S(1)} %get-tuple-element.16), channel_id=1, source_target_pairs={{0,16},{16,0},{1,17},{17,1},{2,18},{18,2},{3,19},{19,3},{4,20},{20... | collective-permute-start | bytes 1769480 | tf_op jit(solution)/shard_map/ppermute | solution.py:176
  44.0 1.8 %collective-permute-done.3 = bf16[16,9,16,128]{3,2,1,0:T(8,128)(2,1)S(1)} collective-permute-done((bf16[16,9,16,128]{3,2,1,0:T(8,128)(2,1)S(1)}, bf16[16,9,16,128]{3,2,1,0:T(8,128)(2,1)S(1)}, u32[]{:S(2)}, u32[]{:S(2)}) %collective-permute-start.3) | collective-permute-done | bytes 589856 | tf_op jit(solution)/shard_map/ppermute | solution.py:176
  45.8 0.1 add_convert_fusion
  46.0 14.5 %all_to_all.26 = bf16[16,9,16,128]{3,2,1,0:T(8,128)(2,1)S(1)} all-to-all(bf16[16,9,16,128]{3,2,1,0:T(8,128)(2,1)S(1)} %add_convert_fusion), channel_id=1, replica_groups=mesh['z_far'=4,'z_near'=4,'core'=2,'ch_0'=4,'ch_1'=4] {'ch_0','ch_1'}, dimensions={0} | all-to-all | bytes 1179648 | tf_op jit(solution)/shard_map/all_to_all | solution.py:193
  60.5 0.1 convert_reduce_fusion
  60.6 12.7 %all_to_all.27 = f32[4,36,128]{2,1,0:T(8,128)S(1)} all-to-all(f32[4,36,128]{2,1,0:T(8,128)S(1)} %reshape.20), channel_id=1, replica_groups=mesh['z_far'=4,'z_near'=4,'core'=2,'ch_0'=4,'ch_1'=4] {'z_near'}, dimensions={0} | all-to-all | bytes 147456 | tf_op jit(solution)/shard_map/all_to_all | solution.py:193
  73.3 0.6 broadcast_in_dim.10
  74.0 5.1 %collective-permute-start.5 = (bf16[1,256,512]{2,1,0:T(8,128)(2,1)S(1)}, bf16[1,256,512]{2,1,0:T(8,128)(2,1)S(1)}, u32[]{:S(2)}, u32[]{:S(2)}) collective-permute-start(bf16[1,256,512]{2,1,0:T(8,128)(2,1)S(1)} %get-tuple-element.22), channel_id=1, source_target_pairs={{16,0},{32,16},{48,32},{64,48},{80,64},{96,80},{112,96},{128,112},... | collective-permute-start | bytes 786440 | tf_op jit(solution)/shard_map/ppermute | solution.py:184
  79.1 2.5 %collective-permute-start.4 = (bf16[1,256,512]{2,1,0:T(8,128)(2,1)S(1)}, bf16[1,256,512]{2,1,0:T(8,128)(2,1)S(1)}, u32[]{:S(2)}, u32[]{:S(2)}) collective-permute-start(bf16[1,256,512]{2,1,0:T(8,128)(2,1)S(1)} %get-tuple-element.23), channel_id=1, source_target_pairs={{0,16},{16,32},{32,48},{48,64},{64,80},{80,96},{96,112},{112,128},... | collective-permute-start | bytes 786440 | tf_op jit(solution)/shard_map/ppermute | solution.py:183
  81.6 11.7 %all-to-all-start.3 = ((f32[4,36,128]{2,1,0:T(8,128)}), f32[4,36,128]{2,1,0:T(8,128)S(1)}, u32[]{:S(2)}, u32[]{:S(2)}) async-start(f32[4,36,128]{2,1,0:T(8,128)} %broadcast_in_dim.10), calls=%async_computation.3 | async-start | bytes 163840 | tf_op jit(solution)/shard_map/all_to_all | solution.py:193
  93.3 0.0 collective-permute-done.5.high_ref
  93.3 0.0 collective-permute-done.4.low_ref
  93.3 4.1 %input.1 = bf16[4,256,512]{2,1,0:T(8,128)(2,1)} custom-call(s32[1]{0:T(128)} %bitcast.core_ref, bf16[1,256,512]{2,1,0:T(8,128)(2,1)S(1)} %collective-permute-done.4.low_ref, bf16[4,256,512]{2,1,0:T(8,128)(2,1)S(1)} %get-tuple-element.19.grad_ref, bf16[1,256,512]{2,1,0:T(8,128)(2,1)S(1)} %collective-permute-done.5.high_ref, ...), custom_call_target="tpu_custom_call" | custom-call | flops 2415919104 | bytes 4194304 | tf_op jit(solution)/shard_map/input/pallas_call | solution.py:160
  97.4 7.7 %all-to-all-done.3 = f32[4,36,128]{2,1,0:T(8,128)S(1)} async-done(((f32[4,36,128]{2,1,0:T(8,128)}), f32[4,36,128]{2,1,0:T(8,128)S(1)}, u32[]{:S(2)}, u32[]{:S(2)}) %all-to-all-start.3) | async-done | bytes 73760 | tf_op jit(solution)/shard_map/all_to_all | solution.py:193
  105.1 11.2 %all_to_all.28 = f32[8,36,128]{2,1,0:T(8,128)S(1)} all-to-all(f32[8,36,128]{2,1,0:T(8,128)S(1)} %broadcast_in_dim.22), channel_id=1, replica_groups=mesh['z_far'=4,'z_near'=4,'core'=2,'ch_0'=4,'ch_1'=4] {'z_near','core'}, dimensions={0} | all-to-all | bytes 294912 | tf_op jit(solution)/shard_map/all_to_all | solution.py:193
  116.4 0.1 copy.8
  116.4 0.8 reshape.22
  (11 shorter events, 0.1 us)
Async XLA Ops:
  0.6 11.8 %copy-start = (bf16[3,3,16,256]{3,2,1,0:T(8,128)(2,1)S(1)}, bf16[3,3,16,256]{3,2,1,0:T(8,128)(2,1)}, u32[]{:S(2)}) copy-start(bf16[3,3,16,256]{3,2,1,0:T(8,128)(2,1)} %param.5) | copy-start | bytes 221188
  1.7 29.9 %copy-start.1 = (s32[64]{0:T(128)S(1)}, s32[64]{0:T(128)}, u32[]{:S(2)}) copy-start(s32[64]{0:T(128)} %param.7) | copy-start | bytes 772
  1.8 10.7 %collective-permute-start.1 = (bf16[1,256,512]{2,1,0:T(8,128)(2,1)S(1)}, bf16[1,256,512]{2,1,0:T(8,128)(2,1)S(1)}, u32[]{:S(2)}, u32[]{:S(2)}) collective-permute-start(bf16[1,256,512]{2,1,0:T(8,128)(2,1)S(1)} %get-tuple-element.24), channel_id=1, source_target_pairs={{16,0},{32,16},{48,32},{64,48},{80,64},{96,80},{112,96},{128,112},... | collective-permute-start | bytes 786440 | tf_op jit(solution)/shard_map/ppermute | solution.py:184
  10.5 5.2 %collective-permute-start = (bf16[1,256,512]{2,1,0:T(8,128)(2,1)S(1)}, bf16[1,256,512]{2,1,0:T(8,128)(2,1)S(1)}, u32[]{:S(2)}, u32[]{:S(2)}) collective-permute-start(bf16[1,256,512]{2,1,0:T(8,128)(2,1)S(1)} %get-tuple-element.25), channel_id=1, source_target_pairs={{0,16},{16,32},{32,48},{48,64},{64,80},{80,96},{96,112},{112,128},... | collective-permute-start | bytes 786440 | tf_op jit(solution)/shard_map/ppermute | solution.py:183
  12.5 21.1 %copy-start.2 = (bf16[1,256,512]{2,1,0:T(8,128)(2,1)}, bf16[1,256,512]{2,1,0:T(8,128)(2,1)S(1)}, u32[]{:S(2)}) copy-start(bf16[1,256,512]{2,1,0:T(8,128)(2,1)S(1)} %collective-permute-done.1.high_hbm) | copy-start | bytes 786436
  15.7 17.9 %copy-start.3 = (bf16[1,256,512]{2,1,0:T(8,128)(2,1)}, bf16[1,256,512]{2,1,0:T(8,128)(2,1)S(1)}, u32[]{:S(2)}) copy-start(bf16[1,256,512]{2,1,0:T(8,128)(2,1)S(1)} %collective-permute-done.low_hbm) | copy-start | bytes 786436
  29.7 3.9 %collective-permute-start.2 = (bf16[16,9,16,128]{3,2,1,0:T(8,128)(2,1)S(1)}, bf16[16,9,16,128]{3,2,1,0:T(8,128)(2,1)S(1)}, u32[]{:S(2)}, u32[]{:S(2)}) collective-permute-start(bf16[16,9,16,128]{3,2,1,0:T(8,128)(2,1)S(1)} %all_to_all.25.mine_ref), channel_id=1, source_target_pairs={{0,16},{16,0},{1,17},{17,1},{2,18},{18,2},{3,19},{19,3},{4,20},{20... | collective-permute-start | bytes 1769480 | tf_op jit(solution)/shard_map/ppermute | solution.py:176
  41.9 3.9 %collective-permute-start.3 = (bf16[16,9,16,128]{3,2,1,0:T(8,128)(2,1)S(1)}, bf16[16,9,16,128]{3,2,1,0:T(8,128)(2,1)S(1)}, u32[]{:S(2)}, u32[]{:S(2)}) collective-permute-start(bf16[16,9,16,128]{3,2,1,0:T(8,128)(2,1)S(1)} %get-tuple-element.16), channel_id=1, source_target_pairs={{0,16},{16,0},{1,17},{17,1},{2,18},{18,2},{3,19},{19,3},{4,20},{20... | collective-permute-start | bytes 1769480 | tf_op jit(solution)/shard_map/ppermute | solution.py:176
  74.0 19.3 %collective-permute-start.5 = (bf16[1,256,512]{2,1,0:T(8,128)(2,1)S(1)}, bf16[1,256,512]{2,1,0:T(8,128)(2,1)S(1)}, u32[]{:S(2)}, u32[]{:S(2)}) collective-permute-start(bf16[1,256,512]{2,1,0:T(8,128)(2,1)S(1)} %get-tuple-element.22), channel_id=1, source_target_pairs={{16,0},{32,16},{48,32},{64,48},{80,64},{96,80},{112,96},{128,112},... | collective-permute-start | bytes 786440 | tf_op jit(solution)/shard_map/ppermute | solution.py:184
  79.1 14.2 %collective-permute-start.4 = (bf16[1,256,512]{2,1,0:T(8,128)(2,1)S(1)}, bf16[1,256,512]{2,1,0:T(8,128)(2,1)S(1)}, u32[]{:S(2)}, u32[]{:S(2)}) collective-permute-start(bf16[1,256,512]{2,1,0:T(8,128)(2,1)S(1)} %get-tuple-element.23), channel_id=1, source_target_pairs={{0,16},{16,32},{32,48},{48,64},{64,80},{80,96},{96,112},{112,128},... | collective-permute-start | bytes 786440 | tf_op jit(solution)/shard_map/ppermute | solution.py:183
  81.6 23.5 %all-to-all-start.3 = ((f32[4,36,128]{2,1,0:T(8,128)}), f32[4,36,128]{2,1,0:T(8,128)S(1)}, u32[]{:S(2)}, u32[]{:S(2)}) async-start(f32[4,36,128]{2,1,0:T(8,128)} %broadcast_in_dim.10), calls=%async_computation.3 | async-start | bytes 163840 | tf_op jit(solution)/shard_map/all_to_all | solution.py:193

commit v4 on v3

--- a/solution.py
+++ b/solution.py
@@ -35,21 +35,23 @@
                 out_ref[side, rows, pl.ds(row * cells + image * COLS, COLS)] = side_shift(tile, side - 1)
 
 
-def grad_kernel(limits_ref, core_ref, low_hbm, feat_hbm, high_hbm, mine_ref, theirs_ref, cot_hbm,
-                grad_ref, own_ref, other_ref, feat_ref, cot_ref, shifted_ref, flat_ref, sems):
+def grad_kernel(limits_ref, core_ref, inner_hbm, feat_hbm, outer_hbm, mine_ref, theirs_ref, cot_hbm,
+                grad_hbm, outer_ref, own_ref, sent_ref,
+                feat_ref, cot_ref, shifted_ref, flat_ref, grad_ref, sems):
     band, ch, cells = cot_ref.shape
     images = cells // COLS
     half = ch // 2
-    sources = [low_hbm.at[0]] + [feat_hbm.at[h] for h in range(band)] + [high_hbm.at[0]]
-    loads = [pltpu.make_async_copy(s, feat_ref.at[h], sems.at[h]) for h, s in enumerate(sources)]
-    masks = [
-        pltpu.make_async_copy(cot_hbm.at[h], cot_ref.at[h], sems.at[band + 2 + h]) for h in range(band)
-    ]
-    for load in loads + masks:
+    core = core_ref[0]
+    rows = [(inner_hbm.at[0], (1 - core) * (band + 1)), (outer_hbm.at[0], core * (band + 1))]
+    rows += [(feat_hbm.at[h], h + 1) for h in range(band)]
+    copies = [(source, feat_ref.at[row]) for source, row in rows]
+    copies += [(cot_hbm.at[h], cot_ref.at[h]) for h in range(band)]
+    loads = [pltpu.make_async_copy(src, dst, sems.at[i]) for i, (src, dst) in enumerate(copies)]
+    for load in loads:
         load.start()
-    near = pl.ds(pl.multiple_of(core_ref[0] * half, half), half)
-    far = pl.ds(pl.multiple_of((1 - core_ref[0]) * half, half), half)
-    for load in loads + masks:
+    near = pl.ds(pl.multiple_of(core * half, half), half)
+    far = pl.ds(pl.multiple_of((1 - core) * half, half), half)
+    for load in loads:
         load.wait()
     for h in range(band + 2):
         fill_shifted(shifted_ref, h, [feat_ref[h, near], feat_ref[h, far]])
@@ -77,24 +79,45 @@
         grad = (inverse * (masked - total - normed * cross)).astype(BF16)
         grad_ref[h] = grad
         flat_ref[:, pl.ds(h * cells, cells)] = grad
-    parts = own_ref.shape[0], own_ref.shape[2], half
+    parts, taps, near_ch, _ = own_ref.shape
+    saves = [pltpu.make_async_copy(grad_ref.at[h], grad_hbm.at[h], sems.at[h]) for h in range(band)]
     for r in range(3):
         for c in range(3):
             t = 3 * r + c
+            if t == 1:
+                for save in saves:
+                    save.start()
             tap = dot(flat_ref[...], shifted_ref[c, :, pl.ds(r * cells, band * cells)], ((1,), (1,)))
-            own_ref[:, t] = tap[:, :half].reshape(parts)
-            other_ref[:, t] = tap[:, half:].astype(BF16).reshape(parts)
-
-
-def input_kernel(core_ref, low_ref, grad_ref, high_ref, mine_ref, theirs_ref, out_ref, shifted_ref, wt_ref):
+            own_ref[:, t] = tap[:, :half].reshape(parts, near_ch, half)
+            sent_ref[:parts, t] = tap[:, half:].astype(BF16).reshape(parts, near_ch, half)
+    first = core == 0
+    bottom, top = grad_ref[0], grad_ref[band - 1]
+    outer_ref[0] = jnp.where(first, bottom, top)
+    inner = jnp.where(first, top, bottom)
+    for g in range(images * parts):
+        n, p = divmod(g, parts)
+        sent_ref[parts + g // taps, g % taps] = inner[
+            p * near_ch : (p + 1) * near_ch, n * COLS : (n + 1) * COLS
+        ]
+    for save in saves:
+        save.wait()
+
+
+def input_kernel(core_ref, got_ref, grad_ref, outer_ref, mine_ref, theirs_ref, out_ref, shifted_ref, wt_ref):
     band, ch, cells = grad_ref.shape
     half = ch // 2
+    first = core_ref[0] == 0
+    parts, taps = mine_ref.shape[:2]
+    groups = [got_ref[parts + g // taps, g % taps] for g in range(parts * (cells // COLS))]
+    images = [jnp.concatenate(groups[k : k + parts], 0) for k in range(0, len(groups), parts)]
+    inner = jnp.concatenate(images, 1)
+    outer = outer_ref[0]
     near = pl.ds(pl.multiple_of(core_ref[0] * half, half), half)
     far = pl.ds(pl.multiple_of((1 - core_ref[0]) * half, half), half)
-    fill_shifted(shifted_ref, 0, [low_ref[0]])
+    fill_shifted(shifted_ref, 0, [jnp.where(first, outer, inner)])
     for h in range(band):
         fill_shifted(shifted_ref, h + 1, [grad_ref[h]])
-    fill_shifted(shifted_ref, band + 1, [high_ref[0]])
+    fill_shifted(shifted_ref, band + 1, [jnp.where(first, inner, outer)])
     for t in range(9):
         wt_ref[t, :half] = mine_ref[:, t].reshape(ch, half).T
         wt_ref[t, half:] = theirs_ref[:, t].reshape(ch, half).T
@@ -131,31 +154,35 @@
     )
 
 
-def call_grad(limits, core, low, features, high, mine, theirs, cotangent):
+def call_grad(limits, core, inner, features, outer, mine, theirs, cotangent):
     band, ch, cells = features.shape
+    parts, taps, _, _ = mine.shape
+    edge_parts = pl.cdiv(parts * (cells // COLS), taps)
     return pl.pallas_call(
         grad_kernel,
         in_specs=smem(2) + [HBM] * 3 + vmem(2) + [HBM],
-        out_specs=vmem(3),
+        out_specs=[HBM] + vmem(3),
         out_shape=[
-            jax.ShapeDtypeStruct(features.shape, BF16),
+            pltpu.HBM(features.shape, BF16),
+            jax.ShapeDtypeStruct(outer.shape, BF16),
             jax.ShapeDtypeStruct(mine.shape, F32),
-            jax.ShapeDtypeStruct(mine.shape, BF16),
+            jax.ShapeDtypeStruct((parts + edge_parts, *mine.shape[1:]), BF16),
         ],
         scratch_shapes=[
             pltpu.VMEM((band + 2, ch, cells), BF16),
             pltpu.VMEM(features.shape, BF16),
             pltpu.VMEM((3, ch, (band + 2) * cells), BF16),
             pltpu.VMEM((ch, band * cells), BF16),
+            pltpu.VMEM(features.shape, BF16),
             pltpu.SemaphoreType.DMA((2 * band + 2,)),
         ],
         cost_estimate=work(features, 2),
         compiler_params=pltpu.CompilerParams(vmem_limit_bytes=24 << 20),
         name="grad",
-    )(limits, core, *map(in_hbm, (low, features, high)), mine, theirs, in_hbm(cotangent))
-
-
-def call_input(core, low, grad, high, mine, theirs):
+    )(limits, core, *map(in_hbm, (inner, features, outer)), mine, theirs, in_hbm(cotangent))
+
+
+def call_input(core, got, grad, outer, mine, theirs):
     band, ch, cells = grad.shape
     return pl.pallas_call(
         input_kernel,
@@ -169,20 +196,16 @@
         cost_estimate=work(grad, 1),
         compiler_params=pltpu.CompilerParams(vmem_limit_bytes=20 << 20),
         name="input",
-    )(core, low, grad, high, mine, theirs)
+    )(core, got, grad, outer, mine, theirs)
 
 
 def exchange(block):
     return lax.ppermute(block, "core", [(0, 1), (1, 0)])
 
 
-def band_edges(block):
-    count = lax.axis_size(ROWS)
-    forward = [(i, i + 1) for i in range(count - 1)]
-    backward = [(target, source) for source, target in forward]
-    low = lax.ppermute(block[-1:], ROWS, forward)
-    high = lax.ppermute(block[:1], ROWS, backward)
-    return low, high
+def across_chips(block):
+    pairs = [(i, i + 1) for i in range(1, lax.axis_size(ROWS) - 1, 2)]
+    return lax.ppermute(block, ROWS, pairs + [(b, a) for a, b in pairs])
 
 
 def copies(block, axis):
@@ -191,6 +214,10 @@
 
 def swap(parts, axis):
     return lax.all_to_all(parts, axis, 0, 0, tiled=True)
+
+
+def total(parts):
+    return lax.optimization_barrier(parts.astype(F32).sum(0))
 
 
 def body(features, conv_weight, cotangent, valid_rows):
@@ -202,24 +229,30 @@
     limits = lax.dynamic_slice_in_dim(valid_rows, lax.axis_index(CH) * images, images, 0)
     limits = limits - lax.axis_index(ROWS) * band
     share = lax.dynamic_slice_in_dim(conv_weight, core * half, half, 3).reshape(9, near, half)
-    low, high = band_edges(features)
-    parts, low, high = lax.optimization_barrier((copies(share, CH), low, high))
-    mine = swap(parts, CH)
+    inner = exchange(lax.dynamic_slice_in_dim(features, (1 - core) * (band - 1), 1, 0))
+    outer = across_chips(lax.dynamic_slice_in_dim(features, core * (band - 1), 1, 0))
+    mine = swap(copies(share, CH), CH)
+    mine, inner, outer = lax.optimization_barrier((mine, inner, outer))
     theirs = exchange(mine)
-    core = core.reshape(1)
-    grad_pre, own, other = call_grad(limits, core, low, features, high, mine, theirs, cotangent)
-    pair = (own + exchange(other).astype(F32)).astype(BF16)
-    plane = swap(pair, CH).astype(F32).sum(0)
-    lines = plane.reshape(lax.axis_size("z_near"), -1, half)
-    block = copies(swap(lines, "z_near").sum(0), "z_far")
-    block, grad_pre = lax.optimization_barrier((block, grad_pre))
-    grad_low, grad_high = band_edges(grad_pre)
-    input_grad = call_input(core, grad_low, grad_pre, grad_high, mine, theirs)
-    block = swap(block, "z_far")
+    where = core.reshape(1)
+    grad_pre, outer_grad, own, sent = call_grad(
+        limits, where, inner, features, outer, mine, theirs, cotangent
+    )
+    got = exchange(sent)
+    other = got[: own.shape[0]]
+    plane = swap((own + other.astype(F32)).astype(BF16), CH)
+    plane, outer_grad = lax.optimization_barrier((plane, across_chips(outer_grad)))
+    input_grad = call_input(where, got, grad_pre, outer_grad, mine, theirs)
+    block = total(plane).astype(BF16)
+    block = total(swap(copies(block, "z_near"), "z_near")).astype(BF16)
+    block = swap(copies(block, "z_far"), "z_far")
     block, input_grad = lax.optimization_barrier((block, input_grad))
-    pieces = ("z_near", "core")
-    whole = swap(copies(block.sum(0), pieces), pieces).reshape(-1, 2, *block.shape[1:])
-    weight_grad = whole.swapaxes(1, 2).reshape(3, 3, near, ch)
+    mine = total(block)
+    theirs = exchange(mine)
+    first = core == 0
+    weight_grad = jnp.concatenate(
+        [jnp.where(first, mine, theirs), jnp.where(first, theirs, mine)], 2
+    ).reshape(3, 3, near, ch)
     return input_grad, weight_grad
 
 

time: 118 us -> 103 us (0.87)
  blocking collectives: 52.3 us -> 10.3 us
  starting transfers between devices: 33.9 us -> 46.4 us
  waiting for transfers between devices: 14.6 us -> 26.7 us
  other arithmetic: 0.3 us -> 1.83 us
    all_to_all x4 -> x1, blocking collectives: 52.3 us -> 10.3 us  [swap(): return lax.all_to_all(parts, axis, 0, 0, tiled=True)]
    all_to_all x1 -> x3, starting transfers between devices: 11.7 us -> 26.3 us  [swap(): return lax.all_to_all(parts, axis, 0, 0, tiled=True)]
    ppermute x4 -> x2, starting transfers between devices: 18.3 us -> 4.12 us  [across_chips(): return lax.ppermute(block, ROWS, pairs + [(b, a) for a, b in pairs])]
    ppermute x2 -> x4, starting transfers between devices: 3.95 us -> 16 us  [exchange(): return lax.ppermute(block, 'core', [(0, 1), (1, 0)])]
    ppermute x4 -> x2, waiting for transfers between devices: 3.24 us -> 11.8 us  [across_chips(): return lax.ppermute(block, ROWS, pairs + [(b, a) for a, b in pairs])]
    all_to_all x1 -> x3, waiting for transfers between devices: 7.69 us -> 10.5 us  [swap(): return lax.all_to_all(parts, axis, 0, 0, tiled=True)]
    unnamed x8 -> x12, local copies, waits for them, and re-layouts: 0.02 us -> 2.11 us
    ppermute x2 -> x4, waiting for transfers between devices: 3.71 us -> 4.43 us  [exchange(): return lax.ppermute(block, 'core', [(0, 1), (1, 0)])]
  transfers between devices with their start and end apart: 7 -> 9, of which waited for: 4 -> 7; matrix products, arithmetic and copies ran while one was open for 0% -> 0% of each run, Pallas kernels for 4% -> 4%
where the time goes in v4:
time: 103 us; the launch traced here: 102 us
  starting transfers between devices  46.4 us (45%)
  waiting for transfers between devices  26.7 us (26%)
  Pallas kernels  12.5 us (12%)
  blocking collectives  10.3 us (10%)
  local copies, waits for them, and re-layouts  3.75 us (4%)
  other arithmetic  1.83 us (2%)
    all_to_all x3, starting transfers between devices, swap(): return lax.all_to_all(parts, axis, 0, 0, tiled=True)  26.3 us
    ppermute x4, starting transfers between devices, exchange(): return lax.ppermute(block, 'core', [(0, 1), (1, 0)])  16 us
    ppermute x2, waiting for transfers between devices, across_chips(): return lax.ppermute(block, ROWS, pairs + [(b, a) for a, b in pairs])  11.8 us
    all_to_all x3, waiting for transfers between devices, swap(): return lax.all_to_all(parts, axis, 0, 0, tiled=True)  10.5 us
    all_to_all x1, blocking collectives, swap(): return lax.all_to_all(parts, axis, 0, 0, tiled=True)  10.3 us
    pallas_call x1, Pallas kernels, call_grad(): pl.pallas_call(grad_kernel, in_specs=smem(2) + [HBM] * 3 + vmem(2) + [HBM...  8.36 us
    ppermute x4, waiting for transfers between devices, exchange(): return lax.ppermute(block, 'core', [(0, 1), (1, 0)])  4.43 us
    pallas_call x1, Pallas kernels, call_input(): pl.pallas_call(input_kernel, in_specs=smem(1) + vmem(5), out_specs=vmem(1...  4.14 us
  transfers between devices with their start and end apart: 9, of which 7 were waited for; matrix products, arithmetic and copies ran while one was open for 0% of the time, Pallas kernels for 4%

profile of v4, /device:TPU:1, one launch (start us, length us, event | category | flops | bytes accessed | tf_op | source)
XLA Modules:
  0.0 102.3 jit_solution(5979693922061093174)
XLA Ops:
  0.6 0.0 copy-start
  0.6 0.0 copy-start.2
  0.7 0.9 copy-done
  1.5 0.9 broadcast_in_dim.9
  2.4 7.7 %all-to-all-start = ((bf16[16,9,16,128]{3,2,1,0:T(8,128)(2,1)}), bf16[16,9,16,128]{3,2,1,0:T(8,128)(2,1)S(1)}, u32[]{:S(2)}, u32[]{:S(2)}) async-start(bf16[16,9,16,128]{3,2,1,0:T(8,128)(2,1)} %broadcast_in_dim.9), calls=%async_computation | async-start | bytes 1179648 | tf_op jit(solution)/shard_map/all_to_all | solution.py:216
  10.1 0.0 copy-done.2
  10.2 4.8 %collective-permute-start = (bf16[1,256,512]{2,1,0:T(8,128)(2,1)S(1)}, bf16[1,256,512]{2,1,0:T(8,128)(2,1)S(1)}, u32[]{:S(2)}, u32[]{:S(2)}) collective-permute-start(bf16[1,256,512]{2,1,0:T(8,128)(2,1)S(1)} %get-tuple-element.25), channel_id=1, source_target_pairs={{0,16},{16,0},{1,17},{17,1},{2,18},{18,2},{3,19},{19,3},{4,20},{20... | collective-permute-start | bytes 786440 | tf_op jit(solution)/shard_map/ppermute | solution.py:203
  15.0 1.9 %collective-permute-start.1 = (bf16[1,256,512]{2,1,0:T(8,128)(2,1)S(1)}, bf16[1,256,512]{2,1,0:T(8,128)(2,1)S(1)}, u32[]{:S(2)}, u32[]{:S(2)}) collective-permute-start(bf16[1,256,512]{2,1,0:T(8,128)(2,1)S(1)} %get-tuple-element.24), channel_id=1, source_target_pairs={{16,32},{48,64},{80,96},{112,128},{144,160},{176,192},{208,224},{2... | collective-permute-start | bytes 786440 | tf_op jit(solution)/shard_map/ppermute | solution.py:208
  16.9 0.0 collective-permute-done.inner_hbm
  16.9 6.0 %collective-permute-done.1.outer_hbm = bf16[1,256,512]{2,1,0:T(8,128)(2,1)S(1)} collective-permute-done((bf16[1,256,512]{2,1,0:T(8,128)(2,1)S(1)}, bf16[1,256,512]{2,1,0:T(8,128)(2,1)S(1)}, u32[]{:S(2)}, u32[]{:S(2)}) %collective-permute-start.1) | collective-permute-done | bytes 262176 | tf_op jit(solution)/shard_map/ppermute | solution.py:208
  23.0 0.0 all-to-all-done.mine_ref
  23.0 2.3 %collective-permute-start.2 = (bf16[16,9,16,128]{3,2,1,0:T(8,128)(2,1)S(1)}, bf16[16,9,16,128]{3,2,1,0:T(8,128)(2,1)S(1)}, u32[]{:S(2)}, u32[]{:S(2)}) collective-permute-start(bf16[16,9,16,128]{3,2,1,0:T(8,128)(2,1)S(1)} %all-to-all-done.mine_ref), channel_id=1, source_target_pairs={{0,16},{16,0},{1,17},{17,1},{2,18},{18,2},{3,19},{19,3},{4,20},{20... | collective-permute-start | bytes 1769480 | tf_op jit(solution)/shard_map/ppermute | solution.py:203
  25.3 0.1 dynamic-slice_subtract_fusion.limits_ref
  25.4 1.5 %collective-permute-done.2.theirs_ref = bf16[16,9,16,128]{3,2,1,0:T(8,128)(2,1)S(1)} collective-permute-done((bf16[16,9,16,128]{3,2,1,0:T(8,128)(2,1)S(1)}, bf16[16,9,16,128]{3,2,1,0:T(8,128)(2,1)S(1)}, u32[]{:S(2)}, u32[]{:S(2)}) %collective-permute-start.2) | collective-permute-done | bytes 589856 | tf_op jit(solution)/shard_map/ppermute | solution.py:203
  26.9 8.4 %grad.1 = (bf16[4,256,512]{2,1,0:T(8,128)(2,1)}, bf16[1,256,512]{2,1,0:T(8,128)(2,1)S(1)}, f32[16,9,16,128]{3,2,1,0:T(8,128)S(1)}, bf16[24,9,16,128]{3,2,1,0:T(8,128)(2,1)S(1)}) custom-call(s32[4]{0:T(128)S(1)} %dynamic-slice_subtract_fusion.limits_ref, s32[1]{0:T(128)} %bitcast.core_ref, bf16[1,256,512]{2,1,0:T(8,128)(2,1)} %copy-done.4, ...), custom_call_target="tpu_custom_call" | custom-call | flops 4831838208 | bytes 8388608 | tf_op jit(solution)/shard_map/grad/pallas_call | solution.py:161
  35.3 2.3 %collective-permute-start.3 = (bf16[24,9,16,128]{3,2,1,0:T(8,128)(2,1)S(1)}, bf16[24,9,16,128]{3,2,1,0:T(8,128)(2,1)S(1)}, u32[]{:S(2)}, u32[]{:S(2)}) collective-permute-start(bf16[24,9,16,128]{3,2,1,0:T(8,128)(2,1)S(1)} %get-tuple-element.17), channel_id=1, source_target_pairs={{0,16},{16,0},{1,17},{17,1},{2,18},{18,2},{3,19},{19,3},{4,20},{20... | collective-permute-start | bytes 2654216 | tf_op jit(solution)/shard_map/ppermute | solution.py:203
  37.6 2.0 %collective-permute-done.3.got_ref = bf16[24,9,16,128]{3,2,1,0:T(8,128)(2,1)S(1)} collective-permute-done((bf16[24,9,16,128]{3,2,1,0:T(8,128)(2,1)S(1)}, bf16[24,9,16,128]{3,2,1,0:T(8,128)(2,1)S(1)}, u32[]{:S(2)}, u32[]{:S(2)}) %collective-permute-start.3) | collective-permute-done | bytes 884768 | tf_op jit(solution)/shard_map/ppermute | solution.py:203
  39.6 0.9 add_convert_fusion
  40.5 6.5 %all-to-all-start.1 = ((bf16[16,9,16,128]{3,2,1,0:T(8,128)(2,1)}), bf16[16,9,16,128]{3,2,1,0:T(8,128)(2,1)S(1)}, u32[]{:S(2)}, u32[]{:S(2)}) async-start(bf16[16,9,16,128]{3,2,1,0:T(8,128)(2,1)} %add_convert_fusion), calls=%async_computation.1 | async-start | bytes 1179648 | tf_op jit(solution)/shard_map/all_to_all | solution.py:216
  47.1 2.2 %collective-permute-start.4 = (bf16[1,256,512]{2,1,0:T(8,128)(2,1)S(1)}, bf16[1,256,512]{2,1,0:T(8,128)(2,1)S(1)}, u32[]{:S(2)}, u32[]{:S(2)}) collective-permute-start(bf16[1,256,512]{2,1,0:T(8,128)(2,1)S(1)} %get-tuple-element.18), channel_id=1, source_target_pairs={{16,32},{48,64},{80,96},{112,128},{144,160},{176,192},{208,224},{2... | collective-permute-start | bytes 786440 | tf_op jit(solution)/shard_map/ppermute | solution.py:208
  49.3 5.8 %collective-permute-done.4.outer_ref = bf16[1,256,512]{2,1,0:T(8,128)(2,1)S(1)} collective-permute-done((bf16[1,256,512]{2,1,0:T(8,128)(2,1)S(1)}, bf16[1,256,512]{2,1,0:T(8,128)(2,1)S(1)}, u32[]{:S(2)}, u32[]{:S(2)}) %collective-permute-start.4) | collective-permute-done | bytes 262176 | tf_op jit(solution)/shard_map/ppermute | solution.py:208
  55.0 3.6 %all-to-all-done.1 = bf16[16,9,16,128]{3,2,1,0:T(8,128)(2,1)S(1)} async-done(((bf16[16,9,16,128]{3,2,1,0:T(8,128)(2,1)}), bf16[16,9,16,128]{3,2,1,0:T(8,128)(2,1)S(1)}, u32[]{:S(2)}, u32[]{:S(2)}) %all-to-all-start.1) | async-done | bytes 589856 | tf_op jit(solution)/shard_map/all_to_all | solution.py:216
  58.7 0.1 convert_reduce_fusion
  58.8 10.3 %all_to_all.20 = bf16[4,9,16,128]{3,2,1,0:T(8,128)(2,1)S(1)} all-to-all(bf16[4,9,16,128]{3,2,1,0:T(8,128)(2,1)S(1)} %broadcast_in_dim.10), channel_id=1, replica_groups=mesh['z_far'=4,'z_near'=4,'core'=2,'ch_0'=4,'ch_1'=4] {'z_near'}, dimensions={0} | all-to-all | bytes 294912 | tf_op jit(solution)/shard_map/all_to_all | solution.py:216
  69.1 0.7 broadcast_in_dim.22
  69.8 12.1 %all-to-all-start.3 = ((bf16[4,9,16,128]{3,2,1,0:T(8,128)(2,1)}), bf16[4,9,16,128]{3,2,1,0:T(8,128)(2,1)S(1)}, u32[]{:S(2)}, u32[]{:S(2)}) async-start(bf16[4,9,16,128]{3,2,1,0:T(8,128)(2,1)} %broadcast_in_dim.22), calls=%async_computation.3 | async-start | bytes 294912 | tf_op jit(solution)/shard_map/all_to_all | solution.py:216
  81.9 1.2 %copy-done.1 = bf16[4,256,512]{2,1,0:T(8,128)(2,1)S(1)} copy-done((bf16[4,256,512]{2,1,0:T(8,128)(2,1)S(1)}, bf16[4,256,512]{2,1,0:T(8,128)(2,1)}, u32[]{:S(2)}) %copy-start.1) | copy-done | bytes 1048600
  83.1 4.1 %input.1 = bf16[4,256,512]{2,1,0:T(8,128)(2,1)} custom-call(s32[1]{0:T(128)} %bitcast.core_ref, bf16[24,9,16,128]{3,2,1,0:T(8,128)(2,1)S(1)} %collective-permute-done.3.got_ref, bf16[4,256,512]{2,1,0:T(8,128)(2,1)S(1)} %copy-done.1, bf16[1,256,512]{2,1,0:T(8,128)(2,1)S(1)} %collective-permute-done.4.outer_ref, ...), custom_call_target="tpu_custom_call" | custom-call | flops 2415919104 | bytes 4194304 | tf_op jit(solution)/shard_map/input/pallas_call | solution.py:187
  87.3 6.9 %all-to-all-done.3 = bf16[4,9,16,128]{3,2,1,0:T(8,128)(2,1)S(1)} async-done(((bf16[4,9,16,128]{3,2,1,0:T(8,128)(2,1)}), bf16[4,9,16,128]{3,2,1,0:T(8,128)(2,1)S(1)}, u32[]{:S(2)}, u32[]{:S(2)}) %all-to-all-start.3) | async-done | bytes 147488 | tf_op jit(solution)/shard_map/all_to_all | solution.py:216
  94.2 6.6 %collective-permute-start.5 = (f32[9,16,128]{2,1,0:T(8,128)S(1)}, f32[9,16,128]{2,1,0:T(8,128)S(1)}, u32[]{:S(2)}, u32[]{:S(2)}) collective-permute-start(f32[9,16,128]{2,1,0:T(8,128)S(1)} %convert_reduce_fusion.1), channel_id=1, source_target_pairs={{0,16},{16,0},{1,17},{17,1},{2,18},{18,2},{3,19},{19,3},{4,20},{20... | collective-permute-start | bytes 221192 | tf_op jit(solution)/shard_map/ppermute | solution.py:203
  100.8 0.9 collective-permute-done.5
  101.7 0.7 pad_maximum_fusion
  (13 shorter events, 0.1 us)
Async XLA Ops:
  0.6 0.9 copy-start
  0.6 9.5 %copy-start.2 = (bf16[4,256,512]{2,1,0:T(8,128)(2,1)S(1)}, bf16[4,256,512]{2,1,0:T(8,128)(2,1)}, u32[]{:S(2)}) copy-start(bf16[4,256,512]{2,1,0:T(8,128)(2,1)} %feat_hbm.1) | copy-start | bytes 3145732
  2.4 22.9 %copy-start.3 = (s32[64]{0:T(128)S(1)}, s32[64]{0:T(128)}, u32[]{:S(2)}) copy-start(s32[64]{0:T(128)} %param.7) | copy-start | bytes 772
  2.4 20.5 %all-to-all-start = ((bf16[16,9,16,128]{3,2,1,0:T(8,128)(2,1)}), bf16[16,9,16,128]{3,2,1,0:T(8,128)(2,1)S(1)}, u32[]{:S(2)}, u32[]{:S(2)}) async-start(bf16[16,9,16,128]{3,2,1,0:T(8,128)(2,1)} %broadcast_in_dim.9), calls=%async_computation | async-start | bytes 1179648 | tf_op jit(solution)/shard_map/all_to_all | solution.py:216
  10.2 6.7 %collective-permute-start = (bf16[1,256,512]{2,1,0:T(8,128)(2,1)S(1)}, bf16[1,256,512]{2,1,0:T(8,128)(2,1)S(1)}, u32[]{:S(2)}, u32[]{:S(2)}) collective-permute-start(bf16[1,256,512]{2,1,0:T(8,128)(2,1)S(1)} %get-tuple-element.25), channel_id=1, source_target_pairs={{0,16},{16,0},{1,17},{17,1},{2,18},{18,2},{3,19},{19,3},{4,20},{20... | collective-permute-start | bytes 786440 | tf_op jit(solution)/shard_map/ppermute | solution.py:203
  15.0 8.0 %collective-permute-start.1 = (bf16[1,256,512]{2,1,0:T(8,128)(2,1)S(1)}, bf16[1,256,512]{2,1,0:T(8,128)(2,1)S(1)}, u32[]{:S(2)}, u32[]{:S(2)}) collective-permute-start(bf16[1,256,512]{2,1,0:T(8,128)(2,1)S(1)} %get-tuple-element.24), channel_id=1, source_target_pairs={{16,32},{48,64},{80,96},{112,128},{144,160},{176,192},{208,224},{2... | collective-permute-start | bytes 786440 | tf_op jit(solution)/shard_map/ppermute | solution.py:208
  16.9 10.0 %copy-start.4 = (bf16[1,256,512]{2,1,0:T(8,128)(2,1)}, bf16[1,256,512]{2,1,0:T(8,128)(2,1)S(1)}, u32[]{:S(2)}) copy-start(bf16[1,256,512]{2,1,0:T(8,128)(2,1)S(1)} %collective-permute-done.inner_hbm) | copy-start | bytes 786436
  22.9 4.0 %copy-start.5 = (bf16[1,256,512]{2,1,0:T(8,128)(2,1)}, bf16[1,256,512]{2,1,0:T(8,128)(2,1)S(1)}, u32[]{:S(2)}) copy-start(bf16[1,256,512]{2,1,0:T(8,128)(2,1)S(1)} %collective-permute-done.1.outer_hbm) | copy-start | bytes 786436
  23.0 4.0 %collective-permute-start.2 = (bf16[16,9,16,128]{3,2,1,0:T(8,128)(2,1)S(1)}, bf16[16,9,16,128]{3,2,1,0:T(8,128)(2,1)S(1)}, u32[]{:S(2)}, u32[]{:S(2)}) collective-permute-start(bf16[16,9,16,128]{3,2,1,0:T(8,128)(2,1)S(1)} %all-to-all-done.mine_ref), channel_id=1, source_target_pairs={{0,16},{16,0},{1,17},{17,1},{2,18},{18,2},{3,19},{19,3},{4,20},{20... | collective-permute-start | bytes 1769480 | tf_op jit(solution)/shard_map/ppermute | solution.py:203
  35.3 4.3 %collective-permute-start.3 = (bf16[24,9,16,128]{3,2,1,0:T(8,128)(2,1)S(1)}, bf16[24,9,16,128]{3,2,1,0:T(8,128)(2,1)S(1)}, u32[]{:S(2)}, u32[]{:S(2)}) collective-permute-start(bf16[24,9,16,128]{3,2,1,0:T(8,128)(2,1)S(1)} %get-tuple-element.17), channel_id=1, source_target_pairs={{0,16},{16,0},{1,17},{17,1},{2,18},{18,2},{3,19},{19,3},{4,20},{20... | collective-permute-start | bytes 2654216 | tf_op jit(solution)/shard_map/ppermute | solution.py:203
  40.5 18.1 %all-to-all-start.1 = ((bf16[16,9,16,128]{3,2,1,0:T(8,128)(2,1)}), bf16[16,9,16,128]{3,2,1,0:T(8,128)(2,1)S(1)}, u32[]{:S(2)}, u32[]{:S(2)}) async-start(bf16[16,9,16,128]{3,2,1,0:T(8,128)(2,1)} %add_convert_fusion), calls=%async_computation.1 | async-start | bytes 1179648 | tf_op jit(solution)/shard_map/all_to_all | solution.py:216
  47.1 8.0 %collective-permute-start.4 = (bf16[1,256,512]{2,1,0:T(8,128)(2,1)S(1)}, bf16[1,256,512]{2,1,0:T(8,128)(2,1)S(1)}, u32[]{:S(2)}, u32[]{:S(2)}) collective-permute-start(bf16[1,256,512]{2,1,0:T(8,128)(2,1)S(1)} %get-tuple-element.18), channel_id=1, source_target_pairs={{16,32},{48,64},{80,96},{112,128},{144,160},{176,192},{208,224},{2... | collective-permute-start | bytes 786440 | tf_op jit(solution)/shard_map/ppermute | solution.py:208
  69.8 24.3 %all-to-all-start.3 = ((bf16[4,9,16,128]{3,2,1,0:T(8,128)(2,1)}), bf16[4,9,16,128]{3,2,1,0:T(8,128)(2,1)S(1)}, u32[]{:S(2)}, u32[]{:S(2)}) async-start(bf16[4,9,16,128]{3,2,1,0:T(8,128)(2,1)} %broadcast_in_dim.22), calls=%async_computation.3 | async-start | bytes 294912 | tf_op jit(solution)/shard_map/all_to_all | solution.py:216
  81.9 1.2 %copy-start.1 = (bf16[4,256,512]{2,1,0:T(8,128)(2,1)S(1)}, bf16[4,256,512]{2,1,0:T(8,128)(2,1)}, u32[]{:S(2)}) copy-start(bf16[4,256,512]{2,1,0:T(8,128)(2,1)} %get-tuple-element.20.grad_ref) | copy-start | bytes 3145732
  94.2 7.5 %collective-permute-start.5 = (f32[9,16,128]{2,1,0:T(8,128)S(1)}, f32[9,16,128]{2,1,0:T(8,128)S(1)}, u32[]{:S(2)}, u32[]{:S(2)}) collective-permute-start(f32[9,16,128]{2,1,0:T(8,128)S(1)} %convert_reduce_fusion.1), channel_id=1, source_target_pairs={{0,16},{16,0},{1,17},{17,1},{2,18},{18,2},{3,19},{19,3},{4,20},{20... | collective-permute-start | bytes 221192 | tf_op jit(solution)/shard_map/ppermute | solution.py:203

commit v5 on v4

--- a/solution.py
+++ b/solution.py
@@ -35,26 +35,32 @@
                 out_ref[side, rows, pl.ds(row * cells + image * COLS, COLS)] = side_shift(tile, side - 1)
 
 
-def grad_kernel(limits_ref, core_ref, inner_hbm, feat_hbm, outer_hbm, mine_ref, theirs_ref, cot_hbm,
-                grad_hbm, outer_ref, own_ref, sent_ref,
-                feat_ref, cot_ref, shifted_ref, flat_ref, grad_ref, sems):
+def stage_kernel(feat_hbm, cot_hbm, feat_ref, cot_ref, sems):
+    loads = [
+        pltpu.make_async_copy(feat_hbm, feat_ref, sems.at[0]),
+        pltpu.make_async_copy(cot_hbm, cot_ref, sems.at[1]),
+    ]
+    for load in loads:
+        load.start()
+    for load in loads:
+        load.wait()
+
+
+def grad_kernel(limits_ref, core_ref, inner_ref, feat_ref, outer_ref, mine_ref, theirs_ref, cot_ref,
+                grad_hbm, edge_ref, own_ref, sent_ref, shifted_ref, flat_ref, grad_ref, sems):
     band, ch, cells = cot_ref.shape
     images = cells // COLS
     half = ch // 2
     core = core_ref[0]
-    rows = [(inner_hbm.at[0], (1 - core) * (band + 1)), (outer_hbm.at[0], core * (band + 1))]
-    rows += [(feat_hbm.at[h], h + 1) for h in range(band)]
-    copies = [(source, feat_ref.at[row]) for source, row in rows]
-    copies += [(cot_hbm.at[h], cot_ref.at[h]) for h in range(band)]
-    loads = [pltpu.make_async_copy(src, dst, sems.at[i]) for i, (src, dst) in enumerate(copies)]
-    for load in loads:
-        load.start()
+    first = core == 0
     near = pl.ds(pl.multiple_of(core * half, half), half)
     far = pl.ds(pl.multiple_of((1 - core) * half, half), half)
-    for load in loads:
-        load.wait()
-    for h in range(band + 2):
-        fill_shifted(shifted_ref, h, [feat_ref[h, near], feat_ref[h, far]])
+    inner = [inner_ref[0, near], inner_ref[0, far]]
+    outer = [outer_ref[0, near], outer_ref[0, far]]
+    fill_shifted(shifted_ref, 0, [jnp.where(first, o, i) for o, i in zip(outer, inner)])
+    for h in range(band):
+        fill_shifted(shifted_ref, h + 1, [feat_ref[h, near], feat_ref[h, far]])
+    fill_shifted(shifted_ref, band + 1, [jnp.where(first, i, o) for o, i in zip(outer, inner)])
     for h in range(band):
         summed = None
         for r in range(3):
@@ -90,9 +96,8 @@
             tap = dot(flat_ref[...], shifted_ref[c, :, pl.ds(r * cells, band * cells)], ((1,), (1,)))
             own_ref[:, t] = tap[:, :half].reshape(parts, near_ch, half)
             sent_ref[:parts, t] = tap[:, half:].astype(BF16).reshape(parts, near_ch, half)
-    first = core == 0
     bottom, top = grad_ref[0], grad_ref[band - 1]
-    outer_ref[0] = jnp.where(first, bottom, top)
+    edge_ref[0] = jnp.where(first, bottom, top)
     inner = jnp.where(first, top, bottom)
     for g in range(images * parts):
         n, p = divmod(g, parts)
@@ -154,13 +159,26 @@
     )
 
 
+def call_stage(features, cotangent):
+    return pl.pallas_call(
+        stage_kernel,
+        in_specs=[HBM] * 2,
+        out_specs=vmem(2),
+        out_shape=[jax.ShapeDtypeStruct(v.shape, v.dtype) for v in (features, cotangent)],
+        scratch_shapes=[pltpu.SemaphoreType.DMA((2,))],
+        cost_estimate=pl.CostEstimate(flops=1 << 20, bytes_accessed=4 << 20, transcendentals=0),
+        compiler_params=pltpu.CompilerParams(vmem_limit_bytes=8 << 20),
+        name="stage",
+    )(in_hbm(features), in_hbm(cotangent))
+
+
 def call_grad(limits, core, inner, features, outer, mine, theirs, cotangent):
     band, ch, cells = features.shape
     parts, taps, _, _ = mine.shape
     edge_parts = pl.cdiv(parts * (cells // COLS), taps)
     return pl.pallas_call(
         grad_kernel,
-        in_specs=smem(2) + [HBM] * 3 + vmem(2) + [HBM],
+        in_specs=smem(2) + vmem(6),
         out_specs=[HBM] + vmem(3),
         out_shape=[
             pltpu.HBM(features.shape, BF16),
@@ -169,17 +187,15 @@
             jax.ShapeDtypeStruct((parts + edge_parts, *mine.shape[1:]), BF16),
         ],
         scratch_shapes=[
-            pltpu.VMEM((band + 2, ch, cells), BF16),
-            pltpu.VMEM(features.shape, BF16),
             pltpu.VMEM((3, ch, (band + 2) * cells), BF16),
             pltpu.VMEM((ch, band * cells), BF16),
             pltpu.VMEM(features.shape, BF16),
-            pltpu.SemaphoreType.DMA((2 * band + 2,)),
+            pltpu.SemaphoreType.DMA((band,)),
         ],
         cost_estimate=work(features, 2),
         compiler_params=pltpu.CompilerParams(vmem_limit_bytes=24 << 20),
         name="grad",
-    )(limits, core, *map(in_hbm, (inner, features, outer)), mine, theirs, in_hbm(cotangent))
+    )(limits, core, inner, features, outer, mine, theirs, cotangent)
 
 
 def call_input(core, got, grad, outer, mine, theirs):
@@ -232,8 +248,8 @@
     inner = exchange(lax.dynamic_slice_in_dim(features, (1 - core) * (band - 1), 1, 0))
     outer = across_chips(lax.dynamic_slice_in_dim(features, core * (band - 1), 1, 0))
     mine = swap(copies(share, CH), CH)
-    mine, inner, outer = lax.optimization_barrier((mine, inner, outer))
     theirs = exchange(mine)
+    features, cotangent = call_stage(features, cotangent)
     where = core.reshape(1)
     grad_pre, outer_grad, own, sent = call_grad(
         limits, where, inner, features, outer, mine, theirs, cotangent

time: 103 us -> 107 us (1.039)
  blocking collectives: 10.3 us -> 29.9 us
  starting transfers between devices: 46.4 us -> 37.6 us
  waiting for transfers between devices: 26.7 us -> 20.7 us
    all_to_all x1 -> x2, blocking collectives: 10.3 us -> 29.9 us  [swap(): return lax.all_to_all(parts, axis, 0, 0, tiled=True)]
    all_to_all x3 -> x2, starting transfers between devices: 26.3 us -> 15.4 us  [swap(): return lax.all_to_all(parts, axis, 0, 0, tiled=True)]
    ppermute x2, waiting for transfers between devices: 11.8 us -> 6.7 us  [across_chips(): return lax.ppermute(block, ROWS, pairs + [(b, a) for a, b in pairs])]
    ppermute x2, starting transfers between devices: 4.12 us -> 7.53 us  [across_chips(): return lax.ppermute(block, ROWS, pairs + [(b, a) for a, b in pairs])]
    ppermute x4, starting transfers between devices: 16 us -> 14.7 us  [exchange(): return lax.ppermute(block, 'core', [(0, 1), (1, 0)])]
    ppermute x4, waiting for transfers between devices: 4.43 us -> 3.28 us  [exchange(): return lax.ppermute(block, 'core', [(0, 1), (1, 0)])]
    all_to_all x3 -> x2, waiting for transfers between devices: 10.5 us -> 10.7 us  [swap(): return lax.all_to_all(parts, axis, 0, 0, tiled=True)]
    pallas_call x1 -> x2, Pallas kernels: 8.36 us -> 8.28 us  [the longest x1 6.72 us: call_grad(): pl.pallas_call(grad_kernel, in_specs=smem(2) + vmem(6), out_specs=[HBM] +...]
  transfers between devices with their start and end apart: 9 -> 8, of which waited for: 7 -> 6; matrix products, arithmetic and copies ran while one was open for 0% -> 0% of each run, Pallas kernels for 4% -> 5%
where the time goes in v5:
time: 107 us; the launch traced here: 106 us
  starting transfers between devices  37.6 us (35%)
  blocking collectives  29.9 us (28%)
  waiting for transfers between devices  20.7 us (19%)
  Pallas kernels  12.4 us (12%)
  local copies, waits for them, and re-layouts  2.93 us (3%)
  other arithmetic  1.83 us (2%)
    all_to_all x2, blocking collectives, swap(): return lax.all_to_all(parts, axis, 0, 0, tiled=True)  29.9 us
    all_to_all x2, starting transfers between devices, swap(): return lax.all_to_all(parts, axis, 0, 0, tiled=True)  15.4 us
    ppermute x4, starting transfers between devices, exchange(): return lax.ppermute(block, 'core', [(0, 1), (1, 0)])  14.7 us
    all_to_all x2, waiting for transfers between devices, swap(): return lax.all_to_all(parts, axis, 0, 0, tiled=True)  10.7 us
    ppermute x2, starting transfers between devices, across_chips(): return lax.ppermute(block, ROWS, pairs + [(b, a) for a, b in pairs])  7.53 us
    pallas_call x1, Pallas kernels, call_grad(): pl.pallas_call(grad_kernel, in_specs=smem(2) + vmem(6), out_specs=[HBM] +...  6.72 us
    ppermute x2, waiting for transfers between devices, across_chips(): return lax.ppermute(block, ROWS, pairs + [(b, a) for a, b in pairs])  6.7 us
    pallas_call x1, Pallas kernels, call_input(): pl.pallas_call(input_kernel, in_specs=smem(1) + vmem(5), out_specs=vmem(1...  4.14 us
  transfers between devices with their start and end apart: 8, of which 6 were waited for; matrix products, arithmetic and copies ran while one was open for 0% of the time, Pallas kernels for 5%

profile of v5, /device:TPU:1, one launch (start us, length us, event | category | flops | bytes accessed | tf_op | source)
XLA Modules:
  0.0 106.2 jit_solution(4229768920024360661)
XLA Ops:
  0.6 0.0 copy-start
  0.6 0.0 copy-start.2
  0.7 0.9 copy-done
  1.5 0.1 broadcast_in_dim.9
  1.6 17.8 %all_to_all.20.mine_ref = bf16[16,9,16,128]{3,2,1,0:T(8,128)(2,1)S(1)} all-to-all(bf16[16,9,16,128]{3,2,1,0:T(8,128)(2,1)S(1)} %broadcast_in_dim.9), channel_id=1, replica_groups=mesh['z_far'=4,'z_near'=4,'core'=2,'ch_0'=4,'ch_1'=4] {'ch_0','ch_1'}, dimensions={0} | all-to-all | bytes 1179648 | tf_op jit(solution)/shard_map/all_to_all | solution.py:232
  19.4 4.8 %collective-permute-start.2 = (bf16[16,9,16,128]{3,2,1,0:T(8,128)(2,1)S(1)}, bf16[16,9,16,128]{3,2,1,0:T(8,128)(2,1)S(1)}, u32[]{:S(2)}, u32[]{:S(2)}) collective-permute-start(bf16[16,9,16,128]{3,2,1,0:T(8,128)(2,1)S(1)} %all_to_all.20.mine_ref), channel_id=1, source_target_pairs={{0,16},{16,0},{1,17},{17,1},{2,18},{18,2},{3,19},{19,3},{4,20},{20... | collective-permute-start | bytes 1769480 | tf_op jit(solution)/shard_map/ppermute | solution.py:219
  24.2 0.0 copy-start.3
  24.2 1.9 %collective-permute-start = (bf16[1,256,512]{2,1,0:T(8,128)(2,1)S(1)}, bf16[1,256,512]{2,1,0:T(8,128)(2,1)S(1)}, u32[]{:S(2)}, u32[]{:S(2)}) collective-permute-start(bf16[1,256,512]{2,1,0:T(8,128)(2,1)S(1)} %get-tuple-element.23), channel_id=1, source_target_pairs={{0,16},{16,0},{1,17},{17,1},{2,18},{18,2},{3,19},{19,3},{4,20},{20... | collective-permute-start | bytes 786440 | tf_op jit(solution)/shard_map/ppermute | solution.py:219
  26.2 3.9 %collective-permute-start.1 = (bf16[1,256,512]{2,1,0:T(8,128)(2,1)S(1)}, bf16[1,256,512]{2,1,0:T(8,128)(2,1)S(1)}, u32[]{:S(2)}, u32[]{:S(2)}) collective-permute-start(bf16[1,256,512]{2,1,0:T(8,128)(2,1)S(1)} %get-tuple-element.22), channel_id=1, source_target_pairs={{16,32},{48,64},{80,96},{112,128},{144,160},{176,192},{208,224},{2... | collective-permute-start | bytes 786440 | tf_op jit(solution)/shard_map/ppermute | solution.py:224
  30.1 1.6 %stage.1 = (bf16[4,256,512]{2,1,0:T(8,128)(2,1)S(1)}, bf16[4,256,512]{2,1,0:T(8,128)(2,1)S(1)}) custom-call(bf16[4,256,512]{2,1,0:T(8,128)(2,1)} %feat_hbm.1, bf16[4,256,512]{2,1,0:T(8,128)(2,1)} %cot_hbm.1), custom_call_target="tpu_custom_call" | custom-call | flops 1048576 | bytes 4194304 | tf_op jit(solution)/shard_map/stage/pallas_call | solution.py:163
  31.6 0.1 dynamic-slice_subtract_fusion.limits_ref
  31.7 0.0 collective-permute-done.inner_ref
  31.7 2.4 %collective-permute-done.1.outer_ref = bf16[1,256,512]{2,1,0:T(8,128)(2,1)S(1)} collective-permute-done((bf16[1,256,512]{2,1,0:T(8,128)(2,1)S(1)}, bf16[1,256,512]{2,1,0:T(8,128)(2,1)S(1)}, u32[]{:S(2)}, u32[]{:S(2)}) %collective-permute-start.1) | collective-permute-done | bytes 262176 | tf_op jit(solution)/shard_map/ppermute | solution.py:224
  34.1 0.0 collective-permute-done.2.theirs_ref
  34.1 6.7 %grad.1 = (bf16[4,256,512]{2,1,0:T(8,128)(2,1)}, bf16[1,256,512]{2,1,0:T(8,128)(2,1)S(1)}, f32[16,9,16,128]{3,2,1,0:T(8,128)S(1)}, bf16[24,9,16,128]{3,2,1,0:T(8,128)(2,1)S(1)}) custom-call(s32[4]{0:T(128)S(1)} %dynamic-slice_subtract_fusion.limits_ref, s32[1]{0:T(128)} %bitcast.core_ref, bf16[1,256,512]{2,1,0:T(8,128)(2,1)S(1)} %collective-permute-done.inner_ref, ...), custom_call_target="tpu_custom_call" | custom-call | flops 4831838208 | bytes 8388608 | tf_op jit(solution)/shard_map/grad/pallas_call | solution.py:179
  40.8 1.9 %collective-permute-start.3 = (bf16[24,9,16,128]{3,2,1,0:T(8,128)(2,1)S(1)}, bf16[24,9,16,128]{3,2,1,0:T(8,128)(2,1)S(1)}, u32[]{:S(2)}, u32[]{:S(2)}) collective-permute-start(bf16[24,9,16,128]{3,2,1,0:T(8,128)(2,1)S(1)} %get-tuple-element.15), channel_id=1, source_target_pairs={{0,16},{16,0},{1,17},{17,1},{2,18},{18,2},{3,19},{19,3},{4,20},{20... | collective-permute-start | bytes 2654216 | tf_op jit(solution)/shard_map/ppermute | solution.py:219
  42.7 2.4 %collective-permute-done.3.got_ref = bf16[24,9,16,128]{3,2,1,0:T(8,128)(2,1)S(1)} collective-permute-done((bf16[24,9,16,128]{3,2,1,0:T(8,128)(2,1)S(1)}, bf16[24,9,16,128]{3,2,1,0:T(8,128)(2,1)S(1)}, u32[]{:S(2)}, u32[]{:S(2)}) %collective-permute-start.3) | collective-permute-done | bytes 884768 | tf_op jit(solution)/shard_map/ppermute | solution.py:219
  45.1 0.9 add_convert_fusion
  46.1 3.6 %all-to-all-start.1 = ((bf16[16,9,16,128]{3,2,1,0:T(8,128)(2,1)}), bf16[16,9,16,128]{3,2,1,0:T(8,128)(2,1)S(1)}, u32[]{:S(2)}, u32[]{:S(2)}) async-start(bf16[16,9,16,128]{3,2,1,0:T(8,128)(2,1)} %add_convert_fusion), calls=%async_computation.1 | async-start | bytes 1179648 | tf_op jit(solution)/shard_map/all_to_all | solution.py:232
  49.7 3.6 %collective-permute-start.4 = (bf16[1,256,512]{2,1,0:T(8,128)(2,1)S(1)}, bf16[1,256,512]{2,1,0:T(8,128)(2,1)S(1)}, u32[]{:S(2)}, u32[]{:S(2)}) collective-permute-start(bf16[1,256,512]{2,1,0:T(8,128)(2,1)S(1)} %get-tuple-element.16), channel_id=1, source_target_pairs={{16,32},{48,64},{80,96},{112,128},{144,160},{176,192},{208,224},{2... | collective-permute-start | bytes 786440 | tf_op jit(solution)/shard_map/ppermute | solution.py:224
  53.3 4.3 %collective-permute-done.4.outer_ref = bf16[1,256,512]{2,1,0:T(8,128)(2,1)S(1)} collective-permute-done((bf16[1,256,512]{2,1,0:T(8,128)(2,1)S(1)}, bf16[1,256,512]{2,1,0:T(8,128)(2,1)S(1)}, u32[]{:S(2)}, u32[]{:S(2)}) %collective-permute-start.4) | collective-permute-done | bytes 262176 | tf_op jit(solution)/shard_map/ppermute | solution.py:224
  57.6 3.9 %all-to-all-done.1 = bf16[16,9,16,128]{3,2,1,0:T(8,128)(2,1)S(1)} async-done(((bf16[16,9,16,128]{3,2,1,0:T(8,128)(2,1)}), bf16[16,9,16,128]{3,2,1,0:T(8,128)(2,1)S(1)}, u32[]{:S(2)}, u32[]{:S(2)}) %all-to-all-start.1) | async-done | bytes 589856 | tf_op jit(solution)/shard_map/all_to_all | solution.py:232
  61.5 0.1 convert_reduce_fusion
  61.6 12.1 %all_to_all.21 = bf16[4,9,16,128]{3,2,1,0:T(8,128)(2,1)S(1)} all-to-all(bf16[4,9,16,128]{3,2,1,0:T(8,128)(2,1)S(1)} %broadcast_in_dim.10), channel_id=1, replica_groups=mesh['z_far'=4,'z_near'=4,'core'=2,'ch_0'=4,'ch_1'=4] {'z_near'}, dimensions={0} | all-to-all | bytes 294912 | tf_op jit(solution)/shard_map/all_to_all | solution.py:232
  73.8 0.7 broadcast_in_dim.22
  74.5 11.8 %all-to-all-start.3 = ((bf16[4,9,16,128]{3,2,1,0:T(8,128)(2,1)}), bf16[4,9,16,128]{3,2,1,0:T(8,128)(2,1)S(1)}, u32[]{:S(2)}, u32[]{:S(2)}) async-start(bf16[4,9,16,128]{3,2,1,0:T(8,128)(2,1)} %broadcast_in_dim.22), calls=%async_computation.3 | async-start | bytes 294912 | tf_op jit(solution)/shard_map/all_to_all | solution.py:232
  86.3 1.2 %copy-done.1 = bf16[4,256,512]{2,1,0:T(8,128)(2,1)S(1)} copy-done((bf16[4,256,512]{2,1,0:T(8,128)(2,1)S(1)}, bf16[4,256,512]{2,1,0:T(8,128)(2,1)}, u32[]{:S(2)}) %copy-start.1) | copy-done | bytes 1048600
  87.5 4.1 %input.1 = bf16[4,256,512]{2,1,0:T(8,128)(2,1)} custom-call(s32[1]{0:T(128)} %bitcast.core_ref, bf16[24,9,16,128]{3,2,1,0:T(8,128)(2,1)S(1)} %collective-permute-done.3.got_ref, bf16[4,256,512]{2,1,0:T(8,128)(2,1)S(1)} %copy-done.1, bf16[1,256,512]{2,1,0:T(8,128)(2,1)S(1)} %collective-permute-done.4.outer_ref, ...), custom_call_target="tpu_custom_call" | custom-call | flops 2415919104 | bytes 4194304 | tf_op jit(solution)/shard_map/input/pallas_call | solution.py:203
  91.7 6.9 %all-to-all-done.3 = bf16[4,9,16,128]{3,2,1,0:T(8,128)(2,1)S(1)} async-done(((bf16[4,9,16,128]{3,2,1,0:T(8,128)(2,1)}), bf16[4,9,16,128]{3,2,1,0:T(8,128)(2,1)S(1)}, u32[]{:S(2)}, u32[]{:S(2)}) %all-to-all-start.3) | async-done | bytes 147488 | tf_op jit(solution)/shard_map/all_to_all | solution.py:232
  98.6 6.1 %collective-permute-start.5 = (f32[9,16,128]{2,1,0:T(8,128)S(1)}, f32[9,16,128]{2,1,0:T(8,128)S(1)}, u32[]{:S(2)}, u32[]{:S(2)}) collective-permute-start(f32[9,16,128]{2,1,0:T(8,128)S(1)} %convert_reduce_fusion.1), channel_id=1, source_target_pairs={{0,16},{16,0},{1,17},{17,1},{2,18},{18,2},{3,19},{19,3},{4,20},{20... | collective-permute-start | bytes 221192 | tf_op jit(solution)/shard_map/ppermute | solution.py:219
  104.6 0.9 collective-permute-done.5
  105.5 0.7 pad_maximum_fusion
  (9 shorter events, 0.1 us)
Async XLA Ops:
  0.6 0.9 copy-start
  0.6 23.5 %copy-start.2 = (bf16[4,256,512]{2,1,0:T(8,128)(2,1)S(1)}, bf16[4,256,512]{2,1,0:T(8,128)(2,1)}, u32[]{:S(2)}) copy-start(bf16[4,256,512]{2,1,0:T(8,128)(2,1)} %feat_hbm.1) | copy-start | bytes 3145732
  19.4 14.7 %collective-permute-start.2 = (bf16[16,9,16,128]{3,2,1,0:T(8,128)(2,1)S(1)}, bf16[16,9,16,128]{3,2,1,0:T(8,128)(2,1)S(1)}, u32[]{:S(2)}, u32[]{:S(2)}) collective-permute-start(bf16[16,9,16,128]{3,2,1,0:T(8,128)(2,1)S(1)} %all_to_all.20.mine_ref), channel_id=1, source_target_pairs={{0,16},{16,0},{1,17},{17,1},{2,18},{18,2},{3,19},{19,3},{4,20},{20... | collective-permute-start | bytes 1769480 | tf_op jit(solution)/shard_map/ppermute | solution.py:219
  24.2 7.4 %copy-start.3 = (s32[64]{0:T(128)S(1)}, s32[64]{0:T(128)}, u32[]{:S(2)}) copy-start(s32[64]{0:T(128)} %param.7) | copy-start | bytes 772
  24.2 7.5 %collective-permute-start = (bf16[1,256,512]{2,1,0:T(8,128)(2,1)S(1)}, bf16[1,256,512]{2,1,0:T(8,128)(2,1)S(1)}, u32[]{:S(2)}, u32[]{:S(2)}) collective-permute-start(bf16[1,256,512]{2,1,0:T(8,128)(2,1)S(1)} %get-tuple-element.23), channel_id=1, source_target_pairs={{0,16},{16,0},{1,17},{17,1},{2,18},{18,2},{3,19},{19,3},{4,20},{20... | collective-permute-start | bytes 786440 | tf_op jit(solution)/shard_map/ppermute | solution.py:219
  26.2 7.9 %collective-permute-start.1 = (bf16[1,256,512]{2,1,0:T(8,128)(2,1)S(1)}, bf16[1,256,512]{2,1,0:T(8,128)(2,1)S(1)}, u32[]{:S(2)}, u32[]{:S(2)}) collective-permute-start(bf16[1,256,512]{2,1,0:T(8,128)(2,1)S(1)} %get-tuple-element.22), channel_id=1, source_target_pairs={{16,32},{48,64},{80,96},{112,128},{144,160},{176,192},{208,224},{2... | collective-permute-start | bytes 786440 | tf_op jit(solution)/shard_map/ppermute | solution.py:224
  40.8 4.3 %collective-permute-start.3 = (bf16[24,9,16,128]{3,2,1,0:T(8,128)(2,1)S(1)}, bf16[24,9,16,128]{3,2,1,0:T(8,128)(2,1)S(1)}, u32[]{:S(2)}, u32[]{:S(2)}) collective-permute-start(bf16[24,9,16,128]{3,2,1,0:T(8,128)(2,1)S(1)} %get-tuple-element.15), channel_id=1, source_target_pairs={{0,16},{16,0},{1,17},{17,1},{2,18},{18,2},{3,19},{19,3},{4,20},{20... | collective-permute-start | bytes 2654216 | tf_op jit(solution)/shard_map/ppermute | solution.py:219
  46.1 15.5 %all-to-all-start.1 = ((bf16[16,9,16,128]{3,2,1,0:T(8,128)(2,1)}), bf16[16,9,16,128]{3,2,1,0:T(8,128)(2,1)S(1)}, u32[]{:S(2)}, u32[]{:S(2)}) async-start(bf16[16,9,16,128]{3,2,1,0:T(8,128)(2,1)} %add_convert_fusion), calls=%async_computation.1 | async-start | bytes 1179648 | tf_op jit(solution)/shard_map/all_to_all | solution.py:232
  49.7 8.0 %collective-permute-start.4 = (bf16[1,256,512]{2,1,0:T(8,128)(2,1)S(1)}, bf16[1,256,512]{2,1,0:T(8,128)(2,1)S(1)}, u32[]{:S(2)}, u32[]{:S(2)}) collective-permute-start(bf16[1,256,512]{2,1,0:T(8,128)(2,1)S(1)} %get-tuple-element.16), channel_id=1, source_target_pairs={{16,32},{48,64},{80,96},{112,128},{144,160},{176,192},{208,224},{2... | collective-permute-start | bytes 786440 | tf_op jit(solution)/shard_map/ppermute | solution.py:224
  74.5 24.0 %all-to-all-start.3 = ((bf16[4,9,16,128]{3,2,1,0:T(8,128)(2,1)}), bf16[4,9,16,128]{3,2,1,0:T(8,128)(2,1)S(1)}, u32[]{:S(2)}, u32[]{:S(2)}) async-start(bf16[4,9,16,128]{3,2,1,0:T(8,128)(2,1)} %broadcast_in_dim.22), calls=%async_computation.3 | async-start | bytes 294912 | tf_op jit(solution)/shard_map/all_to_all | solution.py:232
  86.3 1.2 %copy-start.1 = (bf16[4,256,512]{2,1,0:T(8,128)(2,1)S(1)}, bf16[4,256,512]{2,1,0:T(8,128)(2,1)}, u32[]{:S(2)}) copy-start(bf16[4,256,512]{2,1,0:T(8,128)(2,1)} %get-tuple-element.18.grad_ref) | copy-start | bytes 3145732
  98.6 7.0 %collective-permute-start.5 = (f32[9,16,128]{2,1,0:T(8,128)S(1)}, f32[9,16,128]{2,1,0:T(8,128)S(1)}, u32[]{:S(2)}, u32[]{:S(2)}) collective-permute-start(f32[9,16,128]{2,1,0:T(8,128)S(1)} %convert_reduce_fusion.1), channel_id=1, source_target_pairs={{0,16},{16,0},{1,17},{17,1},{2,18},{18,2},{3,19},{19,3},{4,20},{20... | collective-permute-start | bytes 221192 | tf_op jit(solution)/shard_map/ppermute | solution.py:219

commit v6 on v5

--- a/solution.py
+++ b/solution.py
@@ -108,9 +108,15 @@
         save.wait()
 
 
-def input_kernel(core_ref, got_ref, grad_ref, outer_ref, mine_ref, theirs_ref, out_ref, shifted_ref, wt_ref):
+def input_kernel(core_ref, got_ref, grad_hbm, outer_ref, mine_ref, theirs_ref, out_ref,
+                 grad_ref, shifted_ref, wt_ref, sem):
     band, ch, cells = grad_ref.shape
     half = ch // 2
+    load = pltpu.make_async_copy(grad_hbm, grad_ref, sem.at[0])
+    load.start()
+    for t in range(9):
+        wt_ref[t, :half] = mine_ref[:, t].reshape(ch, half).T
+        wt_ref[t, half:] = theirs_ref[:, t].reshape(ch, half).T
     first = core_ref[0] == 0
     parts, taps = mine_ref.shape[:2]
     groups = [got_ref[parts + g // taps, g % taps] for g in range(parts * (cells // COLS))]
@@ -120,12 +126,10 @@
     near = pl.ds(pl.multiple_of(core_ref[0] * half, half), half)
     far = pl.ds(pl.multiple_of((1 - core_ref[0]) * half, half), half)
     fill_shifted(shifted_ref, 0, [jnp.where(first, outer, inner)])
+    fill_shifted(shifted_ref, band + 1, [jnp.where(first, inner, outer)])
+    load.wait()
     for h in range(band):
         fill_shifted(shifted_ref, h + 1, [grad_ref[h]])
-    fill_shifted(shifted_ref, band + 1, [jnp.where(first, inner, outer)])
-    for t in range(9):
-        wt_ref[t, :half] = mine_ref[:, t].reshape(ch, half).T
-        wt_ref[t, half:] = theirs_ref[:, t].reshape(ch, half).T
     for h in range(band):
         summed = None
         for r in range(3):
@@ -202,17 +206,19 @@
     band, ch, cells = grad.shape
     return pl.pallas_call(
         input_kernel,
-        in_specs=smem(1) + vmem(5),
+        in_specs=smem(1) + vmem(1) + [HBM] + vmem(3),
         out_specs=vmem(1)[0],
         out_shape=jax.ShapeDtypeStruct(grad.shape, BF16),
         scratch_shapes=[
+            pltpu.VMEM(grad.shape, BF16),
             pltpu.VMEM((3, ch, (band + 2) * cells), BF16),
             pltpu.VMEM((9, ch, ch), BF16),
+            pltpu.SemaphoreType.DMA((1,)),
         ],
         cost_estimate=work(grad, 1),
         compiler_params=pltpu.CompilerParams(vmem_limit_bytes=20 << 20),
         name="input",
-    )(core, got, grad, outer, mine, theirs)
+    )(core, got, in_hbm(grad), outer, mine, theirs)
 
 
 def exchange(block):
@@ -255,14 +261,14 @@
         limits, where, inner, features, outer, mine, theirs, cotangent
     )
     got = exchange(sent)
+    outer_grad = across_chips(outer_grad)
+    input_grad = call_input(where, got, grad_pre, outer_grad, mine, theirs)
     other = got[: own.shape[0]]
-    plane = swap((own + other.astype(F32)).astype(BF16), CH)
-    plane, outer_grad = lax.optimization_barrier((plane, across_chips(outer_grad)))
-    input_grad = call_input(where, got, grad_pre, outer_grad, mine, theirs)
+    pair = (own + other.astype(F32)).astype(BF16)
+    plane = swap(pair, CH)
     block = total(plane).astype(BF16)
     block = total(swap(copies(block, "z_near"), "z_near")).astype(BF16)
     block = swap(copies(block, "z_far"), "z_far")
-    block, input_grad = lax.optimization_barrier((block, input_grad))
     mine = total(block)
     theirs = exchange(mine)
     first = core == 0

time: 107 us -> 110 us (1.028)
  blocking collectives: 29.9 us -> 44.4 us
  waiting for transfers between devices: 20.7 us -> 11.5 us
  starting transfers between devices: 37.6 us -> 36.1 us
  Pallas kernels: 12.4 us -> 13.8 us
  local copies, waits for them, and re-layouts: 2.93 us -> 1.7 us
    all_to_all x2 -> x3, blocking collectives: 29.9 us -> 44.4 us  [swap(): return lax.all_to_all(parts, axis, 0, 0, tiled=True)]
    ppermute x2, waiting for transfers between devices: 6.7 us -> 2.37 us  [across_chips(): return lax.ppermute(block, ROWS, pairs + [(b, a) for a, b in pairs])]
    all_to_all x2 -> x1, waiting for transfers between devices: 10.7 us -> 6.76 us  [swap(): return lax.all_to_all(parts, axis, 0, 0, tiled=True)]
    all_to_all x2 -> x1, starting transfers between devices: 15.4 us -> 11.8 us  [swap(): return lax.all_to_all(parts, axis, 0, 0, tiled=True)]
    ppermute x2, starting transfers between devices: 7.53 us -> 9.34 us  [across_chips(): return lax.ppermute(block, ROWS, pairs + [(b, a) for a, b in pairs])]
    pallas_call x1, Pallas kernels: 4.14 us -> 5.59 us  [call_input(): pl.pallas_call(input_kernel, in_specs=smem(1) + vmem(1) + [HBM] + vmem(3)...]
    unnamed x8 -> x6, local copies, waits for them, and re-layouts: 2.1 us -> 0.88 us
  transfers between devices with their start and end apart: 8 -> 7, of which waited for: 6 -> 3; matrix products, arithmetic and copies ran while one was open for 0% -> 0% of each run, Pallas kernels for 5% -> 7%
where the time goes in v6:
time: 110 us; the launch traced here: 109 us
  blocking collectives  44.4 us (40%)
  starting transfers between devices  36.1 us (33%)
  Pallas kernels  13.8 us (13%)
  waiting for transfers between devices  11.5 us (10%)
  local copies, waits for them, and re-layouts  1.7 us (2%)
    all_to_all x3, blocking collectives, swap(): return lax.all_to_all(parts, axis, 0, 0, tiled=True)  44.4 us
    ppermute x4, starting transfers between devices, exchange(): return lax.ppermute(block, 'core', [(0, 1), (1, 0)])  15 us
    all_to_all x1, starting transfers between devices, swap(): return lax.all_to_all(parts, axis, 0, 0, tiled=True)  11.8 us
    ppermute x2, starting transfers between devices, across_chips(): return lax.ppermute(block, ROWS, pairs + [(b, a) for a, b in pairs])  9.34 us
    all_to_all x1, waiting for transfers between devices, swap(): return lax.all_to_all(parts, axis, 0, 0, tiled=True)  6.76 us
    pallas_call x1, Pallas kernels, call_grad(): pl.pallas_call(grad_kernel, in_specs=smem(2) + vmem(6), out_specs=[HBM] +...  6.69 us
    pallas_call x1, Pallas kernels, call_input(): pl.pallas_call(input_kernel, in_specs=smem(1) + vmem(1) + [HBM] + vmem(3)...  5.59 us
    ppermute x4, waiting for transfers between devices, exchange(): return lax.ppermute(block, 'core', [(0, 1), (1, 0)])  2.4 us
  transfers between devices with their start and end apart: 7, of which 3 were waited for; matrix products, arithmetic and copies ran while one was open for 0% of the time, Pallas kernels for 7%

profile of v6, /device:TPU:1, one launch (start us, length us, event | category | flops | bytes accessed | tf_op | source)
XLA Modules:
  0.0 109.4 jit_solution(3797071260083675787)
XLA Ops:
  0.6 0.0 copy-start
  0.6 0.0 copy-start.1
  0.7 0.9 copy-done
  1.5 0.1 broadcast_in_dim.9
  1.6 17.8 %all_to_all.20.mine_ref = bf16[16,9,16,128]{3,2,1,0:T(8,128)(2,1)S(1)} all-to-all(bf16[16,9,16,128]{3,2,1,0:T(8,128)(2,1)S(1)} %broadcast_in_dim.9), channel_id=1, replica_groups=mesh['z_far'=4,'z_near'=4,'core'=2,'ch_0'=4,'ch_1'=4] {'ch_0','ch_1'}, dimensions={0} | all-to-all | bytes 1179648 | tf_op jit(solution)/shard_map/all_to_all | solution.py:238
  19.4 4.8 %collective-permute-start.2 = (bf16[16,9,16,128]{3,2,1,0:T(8,128)(2,1)S(1)}, bf16[16,9,16,128]{3,2,1,0:T(8,128)(2,1)S(1)}, u32[]{:S(2)}, u32[]{:S(2)}) collective-permute-start(bf16[16,9,16,128]{3,2,1,0:T(8,128)(2,1)S(1)} %all_to_all.20.mine_ref), channel_id=1, source_target_pairs={{0,16},{16,0},{1,17},{17,1},{2,18},{18,2},{3,19},{19,3},{4,20},{20... | collective-permute-start | bytes 1769480 | tf_op jit(solution)/shard_map/ppermute | solution.py:225
  24.2 0.0 copy-done.1
  24.2 0.0 copy-start.2
  24.2 1.9 %collective-permute-start = (bf16[1,256,512]{2,1,0:T(8,128)(2,1)S(1)}, bf16[1,256,512]{2,1,0:T(8,128)(2,1)S(1)}, u32[]{:S(2)}, u32[]{:S(2)}) collective-permute-start(bf16[1,256,512]{2,1,0:T(8,128)(2,1)S(1)} %get-tuple-element.15), channel_id=1, source_target_pairs={{0,16},{16,0},{1,17},{17,1},{2,18},{18,2},{3,19},{19,3},{4,20},{20... | collective-permute-start | bytes 786440 | tf_op jit(solution)/shard_map/ppermute | solution.py:225
  26.2 3.9 %collective-permute-start.1 = (bf16[1,256,512]{2,1,0:T(8,128)(2,1)S(1)}, bf16[1,256,512]{2,1,0:T(8,128)(2,1)S(1)}, u32[]{:S(2)}, u32[]{:S(2)}) collective-permute-start(bf16[1,256,512]{2,1,0:T(8,128)(2,1)S(1)} %get-tuple-element.14), channel_id=1, source_target_pairs={{16,32},{48,64},{80,96},{112,128},{144,160},{176,192},{208,224},{2... | collective-permute-start | bytes 786440 | tf_op jit(solution)/shard_map/ppermute | solution.py:230
  30.1 1.6 %stage.1 = (bf16[4,256,512]{2,1,0:T(8,128)(2,1)S(1)}, bf16[4,256,512]{2,1,0:T(8,128)(2,1)S(1)}) custom-call(bf16[4,256,512]{2,1,0:T(8,128)(2,1)} %feat_hbm.1, bf16[4,256,512]{2,1,0:T(8,128)(2,1)} %cot_hbm.1), custom_call_target="tpu_custom_call" | custom-call | flops 1048576 | bytes 4194304 | tf_op jit(solution)/shard_map/stage/pallas_call | solution.py:167
  31.6 0.0 copy-done.2
  31.6 0.1 dynamic-slice_subtract_fusion.limits_ref
  31.7 0.0 collective-permute-done.inner_ref
  31.7 2.4 %collective-permute-done.1.outer_ref = bf16[1,256,512]{2,1,0:T(8,128)(2,1)S(1)} collective-permute-done((bf16[1,256,512]{2,1,0:T(8,128)(2,1)S(1)}, bf16[1,256,512]{2,1,0:T(8,128)(2,1)S(1)}, u32[]{:S(2)}, u32[]{:S(2)}) %collective-permute-start.1) | collective-permute-done | bytes 262176 | tf_op jit(solution)/shard_map/ppermute | solution.py:230
  34.1 0.0 collective-permute-done.2.theirs_ref
  34.1 6.7 %grad.1 = (bf16[4,256,512]{2,1,0:T(8,128)(2,1)}, bf16[1,256,512]{2,1,0:T(8,128)(2,1)S(1)}, f32[16,9,16,128]{3,2,1,0:T(8,128)S(1)}, bf16[24,9,16,128]{3,2,1,0:T(8,128)(2,1)S(1)}) custom-call(s32[4]{0:T(128)S(1)} %dynamic-slice_subtract_fusion.limits_ref, s32[1]{0:T(128)} %bitcast.core_ref, bf16[1,256,512]{2,1,0:T(8,128)(2,1)S(1)} %collective-permute-done.inner_ref, ...), custom_call_target="tpu_custom_call" | custom-call | flops 4831838208 | bytes 8388608 | tf_op jit(solution)/shard_map/grad/pallas_call | solution.py:183
  40.8 1.9 %collective-permute-start.3 = (bf16[24,9,16,128]{3,2,1,0:T(8,128)(2,1)S(1)}, bf16[24,9,16,128]{3,2,1,0:T(8,128)(2,1)S(1)}, u32[]{:S(2)}, u32[]{:S(2)}) collective-permute-start(bf16[24,9,16,128]{3,2,1,0:T(8,128)(2,1)S(1)} %get-tuple-element.10), channel_id=1, source_target_pairs={{0,16},{16,0},{1,17},{17,1},{2,18},{18,2},{3,19},{19,3},{4,20},{20... | collective-permute-start | bytes 2654216 | tf_op jit(solution)/shard_map/ppermute | solution.py:225
  42.7 2.4 %collective-permute-done.3.got_ref = bf16[24,9,16,128]{3,2,1,0:T(8,128)(2,1)S(1)} collective-permute-done((bf16[24,9,16,128]{3,2,1,0:T(8,128)(2,1)S(1)}, bf16[24,9,16,128]{3,2,1,0:T(8,128)(2,1)S(1)}, u32[]{:S(2)}, u32[]{:S(2)}) %collective-permute-start.3) | collective-permute-done | bytes 884768 | tf_op jit(solution)/shard_map/ppermute | solution.py:225
  45.1 0.1 add_convert_fusion
  45.2 14.5 %all_to_all.21 = bf16[16,9,16,128]{3,2,1,0:T(8,128)(2,1)S(1)} all-to-all(bf16[16,9,16,128]{3,2,1,0:T(8,128)(2,1)S(1)} %add_convert_fusion), channel_id=1, replica_groups=mesh['z_far'=4,'z_near'=4,'core'=2,'ch_0'=4,'ch_1'=4] {'ch_0','ch_1'}, dimensions={0} | all-to-all | bytes 1179648 | tf_op jit(solution)/shard_map/all_to_all | solution.py:238
  59.7 0.1 convert_reduce_fusion
  59.8 12.1 %all_to_all.22 = bf16[4,9,16,128]{3,2,1,0:T(8,128)(2,1)S(1)} all-to-all(bf16[4,9,16,128]{3,2,1,0:T(8,128)(2,1)S(1)} %broadcast_in_dim.10), channel_id=1, replica_groups=mesh['z_far'=4,'z_near'=4,'core'=2,'ch_0'=4,'ch_1'=4] {'z_near'}, dimensions={0} | all-to-all | bytes 294912 | tf_op jit(solution)/shard_map/all_to_all | solution.py:238
  72.0 0.7 broadcast_in_dim.22
  72.7 11.8 %all-to-all-start.3 = ((bf16[4,9,16,128]{3,2,1,0:T(8,128)(2,1)}), bf16[4,9,16,128]{3,2,1,0:T(8,128)(2,1)S(1)}, u32[]{:S(2)}, u32[]{:S(2)}) async-start(bf16[4,9,16,128]{3,2,1,0:T(8,128)(2,1)} %broadcast_in_dim.22), calls=%async_computation.3 | async-start | bytes 294912 | tf_op jit(solution)/shard_map/all_to_all | solution.py:238
  84.5 5.5 %collective-permute-start.4 = (bf16[1,256,512]{2,1,0:T(8,128)(2,1)S(1)}, bf16[1,256,512]{2,1,0:T(8,128)(2,1)S(1)}, u32[]{:S(2)}, u32[]{:S(2)}) collective-permute-start(bf16[1,256,512]{2,1,0:T(8,128)(2,1)S(1)} %get-tuple-element.12), channel_id=1, source_target_pairs={{16,32},{48,64},{80,96},{112,128},{144,160},{176,192},{208,224},{2... | collective-permute-start | bytes 786440 | tf_op jit(solution)/shard_map/ppermute | solution.py:230
  90.0 6.8 %all-to-all-done.3 = bf16[4,9,16,128]{3,2,1,0:T(8,128)(2,1)S(1)} async-done(((bf16[4,9,16,128]{3,2,1,0:T(8,128)(2,1)}), bf16[4,9,16,128]{3,2,1,0:T(8,128)(2,1)S(1)}, u32[]{:S(2)}, u32[]{:S(2)}) %all-to-all-start.3) | async-done | bytes 147488 | tf_op jit(solution)/shard_map/all_to_all | solution.py:238
  96.7 6.4 %collective-permute-start.5 = (f32[9,16,128]{2,1,0:T(8,128)S(1)}, f32[9,16,128]{2,1,0:T(8,128)S(1)}, u32[]{:S(2)}, u32[]{:S(2)}) collective-permute-start(f32[9,16,128]{2,1,0:T(8,128)S(1)} %convert_reduce_fusion.1), channel_id=1, source_target_pairs={{0,16},{16,0},{1,17},{17,1},{2,18},{18,2},{3,19},{19,3},{4,20},{20... | collective-permute-start | bytes 221192 | tf_op jit(solution)/shard_map/ppermute | solution.py:225
  103.1 0.0 collective-permute-done.4.outer_ref
  103.1 5.6 %input.1 = bf16[4,256,512]{2,1,0:T(8,128)(2,1)} custom-call(s32[1]{0:T(128)} %bitcast.core_ref, bf16[24,9,16,128]{3,2,1,0:T(8,128)(2,1)S(1)} %collective-permute-done.3.got_ref, bf16[4,256,512]{2,1,0:T(8,128)(2,1)} %get-tuple-element.11.grad_hbm, bf16[1,256,512]{2,1,0:T(8,128)(2,1)S(1)} %collective-permute-done.4.outer_ref, ...), custom_call_target="tpu_custom_call" | custom-call | flops 2415919104 | bytes 4194304 | tf_op jit(solution)/shard_map/input/pallas_call | solution.py:207
  108.7 0.0 collective-permute-done.5
  108.8 0.7 pad_maximum_fusion
  (6 shorter events, 0.1 us)
Async XLA Ops:
  0.6 0.9 copy-start
  0.6 23.5 %copy-start.1 = (bf16[4,256,512]{2,1,0:T(8,128)(2,1)S(1)}, bf16[4,256,512]{2,1,0:T(8,128)(2,1)}, u32[]{:S(2)}) copy-start(bf16[4,256,512]{2,1,0:T(8,128)(2,1)} %feat_hbm.1) | copy-start | bytes 3145732
  19.4 14.7 %collective-permute-start.2 = (bf16[16,9,16,128]{3,2,1,0:T(8,128)(2,1)S(1)}, bf16[16,9,16,128]{3,2,1,0:T(8,128)(2,1)S(1)}, u32[]{:S(2)}, u32[]{:S(2)}) collective-permute-start(bf16[16,9,16,128]{3,2,1,0:T(8,128)(2,1)S(1)} %all_to_all.20.mine_ref), channel_id=1, source_target_pairs={{0,16},{16,0},{1,17},{17,1},{2,18},{18,2},{3,19},{19,3},{4,20},{20... | collective-permute-start | bytes 1769480 | tf_op jit(solution)/shard_map/ppermute | solution.py:225
  24.2 7.4 %copy-start.2 = (s32[64]{0:T(128)S(1)}, s32[64]{0:T(128)}, u32[]{:S(2)}) copy-start(s32[64]{0:T(128)} %param.7) | copy-start | bytes 772
  24.2 7.5 %collective-permute-start = (bf16[1,256,512]{2,1,0:T(8,128)(2,1)S(1)}, bf16[1,256,512]{2,1,0:T(8,128)(2,1)S(1)}, u32[]{:S(2)}, u32[]{:S(2)}) collective-permute-start(bf16[1,256,512]{2,1,0:T(8,128)(2,1)S(1)} %get-tuple-element.15), channel_id=1, source_target_pairs={{0,16},{16,0},{1,17},{17,1},{2,18},{18,2},{3,19},{19,3},{4,20},{20... | collective-permute-start | bytes 786440 | tf_op jit(solution)/shard_map/ppermute | solution.py:225
  26.2 7.9 %collective-permute-start.1 = (bf16[1,256,512]{2,1,0:T(8,128)(2,1)S(1)}, bf16[1,256,512]{2,1,0:T(8,128)(2,1)S(1)}, u32[]{:S(2)}, u32[]{:S(2)}) collective-permute-start(bf16[1,256,512]{2,1,0:T(8,128)(2,1)S(1)} %get-tuple-element.14), channel_id=1, source_target_pairs={{16,32},{48,64},{80,96},{112,128},{144,160},{176,192},{208,224},{2... | collective-permute-start | bytes 786440 | tf_op jit(solution)/shard_map/ppermute | solution.py:230
  40.8 4.3 %collective-permute-start.3 = (bf16[24,9,16,128]{3,2,1,0:T(8,128)(2,1)S(1)}, bf16[24,9,16,128]{3,2,1,0:T(8,128)(2,1)S(1)}, u32[]{:S(2)}, u32[]{:S(2)}) collective-permute-start(bf16[24,9,16,128]{3,2,1,0:T(8,128)(2,1)S(1)} %get-tuple-element.10), channel_id=1, source_target_pairs={{0,16},{16,0},{1,17},{17,1},{2,18},{18,2},{3,19},{19,3},{4,20},{20... | collective-permute-start | bytes 2654216 | tf_op jit(solution)/shard_map/ppermute | solution.py:225
  72.7 24.0 %all-to-all-start.3 = ((bf16[4,9,16,128]{3,2,1,0:T(8,128)(2,1)}), bf16[4,9,16,128]{3,2,1,0:T(8,128)(2,1)S(1)}, u32[]{:S(2)}, u32[]{:S(2)}) async-start(bf16[4,9,16,128]{3,2,1,0:T(8,128)(2,1)} %broadcast_in_dim.22), calls=%async_computation.3 | async-start | bytes 294912 | tf_op jit(solution)/shard_map/all_to_all | solution.py:238
  84.5 18.6 %collective-permute-start.4 = (bf16[1,256,512]{2,1,0:T(8,128)(2,1)S(1)}, bf16[1,256,512]{2,1,0:T(8,128)(2,1)S(1)}, u32[]{:S(2)}, u32[]{:S(2)}) collective-permute-start(bf16[1,256,512]{2,1,0:T(8,128)(2,1)S(1)} %get-tuple-element.12), channel_id=1, source_target_pairs={{16,32},{48,64},{80,96},{112,128},{144,160},{176,192},{208,224},{2... | collective-permute-start | bytes 786440 | tf_op jit(solution)/shard_map/ppermute | solution.py:230
  96.7 12.0 %collective-permute-start.5 = (f32[9,16,128]{2,1,0:T(8,128)S(1)}, f32[9,16,128]{2,1,0:T(8,128)S(1)}, u32[]{:S(2)}, u32[]{:S(2)}) collective-permute-start(f32[9,16,128]{2,1,0:T(8,128)S(1)} %convert_reduce_fusion.1), channel_id=1, source_target_pairs={{0,16},{16,0},{1,17},{17,1},{2,18},{18,2},{3,19},{19,3},{4,20},{20... | collective-permute-start | bytes 221192 | tf_op jit(solution)/shard_map/ppermute | solution.py:225

commit v7 on v5

--- a/solution.py
+++ b/solution.py
@@ -255,14 +255,12 @@
         limits, where, inner, features, outer, mine, theirs, cotangent
     )
     got = exchange(sent)
+    outer_grad = across_chips(outer_grad)
+    input_grad = call_input(where, got, grad_pre, outer_grad, mine, theirs)
     other = got[: own.shape[0]]
-    plane = swap((own + other.astype(F32)).astype(BF16), CH)
-    plane, outer_grad = lax.optimization_barrier((plane, across_chips(outer_grad)))
-    input_grad = call_input(where, got, grad_pre, outer_grad, mine, theirs)
-    block = total(plane).astype(BF16)
+    block = total(swap((own + other.astype(F32)).astype(BF16), CH)).astype(BF16)
     block = total(swap(copies(block, "z_near"), "z_near")).astype(BF16)
     block = swap(copies(block, "z_far"), "z_far")
-    block, input_grad = lax.optimization_barrier((block, input_grad))
     mine = total(block)
     theirs = exchange(mine)
     first = core == 0

time: 107 us -> 110 us (1.028)
  blocking collectives: 29.9 us -> 44.4 us
  waiting for transfers between devices: 20.7 us -> 11.5 us
  starting transfers between devices: 37.6 us -> 36.1 us
    all_to_all x2 -> x3, blocking collectives: 29.9 us -> 44.4 us  [swap(): return lax.all_to_all(parts, axis, 0, 0, tiled=True)]
    ppermute x2, waiting for transfers between devices: 6.7 us -> 2.37 us  [across_chips(): return lax.ppermute(block, ROWS, pairs + [(b, a) for a, b in pairs])]
    all_to_all x2 -> x1, waiting for transfers between devices: 10.7 us -> 6.76 us  [swap(): return lax.all_to_all(parts, axis, 0, 0, tiled=True)]
    all_to_all x2 -> x1, starting transfers between devices: 15.4 us -> 11.8 us  [swap(): return lax.all_to_all(parts, axis, 0, 0, tiled=True)]
    ppermute x2, starting transfers between devices: 7.53 us -> 9.34 us  [across_chips(): return lax.ppermute(block, ROWS, pairs + [(b, a) for a, b in pairs])]
  transfers between devices with their start and end apart: 8 -> 7, of which waited for: 6 -> 3; matrix products, arithmetic and copies ran while one was open for 0% -> 0% of each run, Pallas kernels for 5% -> 5%
where the time goes in v7:
time: 110 us; the launch traced here: 109 us
  blocking collectives  44.4 us (40%)
  starting transfers between devices  36.1 us (33%)
  Pallas kernels  12.4 us (11%)
  waiting for transfers between devices  11.5 us (10%)
  local copies, waits for them, and re-layouts  2.92 us (3%)
    all_to_all x3, blocking collectives, swap(): return lax.all_to_all(parts, axis, 0, 0, tiled=True)  44.4 us
    ppermute x4, starting transfers between devices, exchange(): return lax.ppermute(block, 'core', [(0, 1), (1, 0)])  15 us
    all_to_all x1, starting transfers between devices, swap(): return lax.all_to_all(parts, axis, 0, 0, tiled=True)  11.8 us
    ppermute x2, starting transfers between devices, across_chips(): return lax.ppermute(block, ROWS, pairs + [(b, a) for a, b in pairs])  9.34 us
    all_to_all x1, waiting for transfers between devices, swap(): return lax.all_to_all(parts, axis, 0, 0, tiled=True)  6.76 us
    pallas_call x1, Pallas kernels, call_grad(): pl.pallas_call(grad_kernel, in_specs=smem(2) + vmem(6), out_specs=[HBM] +...  6.69 us
    pallas_call x1, Pallas kernels, call_input(): pl.pallas_call(input_kernel, in_specs=smem(1) + vmem(5), out_specs=vmem(1...  4.14 us
    ppermute x4, waiting for transfers between devices, exchange(): return lax.ppermute(block, 'core', [(0, 1), (1, 0)])  2.4 us
  transfers between devices with their start and end apart: 7, of which 3 were waited for; matrix products, arithmetic and copies ran while one was open for 0% of the time, Pallas kernels for 5%

profile of v7, /device:TPU:1, one launch (start us, length us, event | category | flops | bytes accessed | tf_op | source)
XLA Modules:
  0.0 109.2 jit_solution(11921094151608330573)
XLA Ops:
  0.6 0.0 copy-start
  0.6 0.0 copy-start.2
  0.7 0.9 copy-done
  1.5 0.1 broadcast_in_dim.9
  1.6 17.8 %all_to_all.20.mine_ref = bf16[16,9,16,128]{3,2,1,0:T(8,128)(2,1)S(1)} all-to-all(bf16[16,9,16,128]{3,2,1,0:T(8,128)(2,1)S(1)} %broadcast_in_dim.9), channel_id=1, replica_groups=mesh['z_far'=4,'z_near'=4,'core'=2,'ch_0'=4,'ch_1'=4] {'ch_0','ch_1'}, dimensions={0} | all-to-all | bytes 1179648 | tf_op jit(solution)/shard_map/all_to_all | solution.py:232
  19.4 4.8 %collective-permute-start.2 = (bf16[16,9,16,128]{3,2,1,0:T(8,128)(2,1)S(1)}, bf16[16,9,16,128]{3,2,1,0:T(8,128)(2,1)S(1)}, u32[]{:S(2)}, u32[]{:S(2)}) collective-permute-start(bf16[16,9,16,128]{3,2,1,0:T(8,128)(2,1)S(1)} %all_to_all.20.mine_ref), channel_id=1, source_target_pairs={{0,16},{16,0},{1,17},{17,1},{2,18},{18,2},{3,19},{19,3},{4,20},{20... | collective-permute-start | bytes 1769480 | tf_op jit(solution)/shard_map/ppermute | solution.py:219
  24.2 0.0 copy-start.3
  24.2 1.9 %collective-permute-start = (bf16[1,256,512]{2,1,0:T(8,128)(2,1)S(1)}, bf16[1,256,512]{2,1,0:T(8,128)(2,1)S(1)}, u32[]{:S(2)}, u32[]{:S(2)}) collective-permute-start(bf16[1,256,512]{2,1,0:T(8,128)(2,1)S(1)} %get-tuple-element.15), channel_id=1, source_target_pairs={{0,16},{16,0},{1,17},{17,1},{2,18},{18,2},{3,19},{19,3},{4,20},{20... | collective-permute-start | bytes 786440 | tf_op jit(solution)/shard_map/ppermute | solution.py:219
  26.2 3.9 %collective-permute-start.1 = (bf16[1,256,512]{2,1,0:T(8,128)(2,1)S(1)}, bf16[1,256,512]{2,1,0:T(8,128)(2,1)S(1)}, u32[]{:S(2)}, u32[]{:S(2)}) collective-permute-start(bf16[1,256,512]{2,1,0:T(8,128)(2,1)S(1)} %get-tuple-element.14), channel_id=1, source_target_pairs={{16,32},{48,64},{80,96},{112,128},{144,160},{176,192},{208,224},{2... | collective-permute-start | bytes 786440 | tf_op jit(solution)/shard_map/ppermute | solution.py:224
  30.1 1.6 %stage.1 = (bf16[4,256,512]{2,1,0:T(8,128)(2,1)S(1)}, bf16[4,256,512]{2,1,0:T(8,128)(2,1)S(1)}) custom-call(bf16[4,256,512]{2,1,0:T(8,128)(2,1)} %feat_hbm.1, bf16[4,256,512]{2,1,0:T(8,128)(2,1)} %cot_hbm.1), custom_call_target="tpu_custom_call" | custom-call | flops 1048576 | bytes 4194304 | tf_op jit(solution)/shard_map/stage/pallas_call | solution.py:163
  31.6 0.1 dynamic-slice_subtract_fusion.limits_ref
  31.7 0.0 collective-permute-done.inner_ref
  31.7 2.4 %collective-permute-done.1.outer_ref = bf16[1,256,512]{2,1,0:T(8,128)(2,1)S(1)} collective-permute-done((bf16[1,256,512]{2,1,0:T(8,128)(2,1)S(1)}, bf16[1,256,512]{2,1,0:T(8,128)(2,1)S(1)}, u32[]{:S(2)}, u32[]{:S(2)}) %collective-permute-start.1) | collective-permute-done | bytes 262176 | tf_op jit(solution)/shard_map/ppermute | solution.py:224
  34.1 0.0 collective-permute-done.2.theirs_ref
  34.1 6.7 %grad.1 = (bf16[4,256,512]{2,1,0:T(8,128)(2,1)}, bf16[1,256,512]{2,1,0:T(8,128)(2,1)S(1)}, f32[16,9,16,128]{3,2,1,0:T(8,128)S(1)}, bf16[24,9,16,128]{3,2,1,0:T(8,128)(2,1)S(1)}) custom-call(s32[4]{0:T(128)S(1)} %dynamic-slice_subtract_fusion.limits_ref, s32[1]{0:T(128)} %bitcast.core_ref, bf16[1,256,512]{2,1,0:T(8,128)(2,1)S(1)} %collective-permute-done.inner_ref, ...), custom_call_target="tpu_custom_call" | custom-call | flops 4831838208 | bytes 8388608 | tf_op jit(solution)/shard_map/grad/pallas_call | solution.py:179
  40.8 1.9 %collective-permute-start.3 = (bf16[24,9,16,128]{3,2,1,0:T(8,128)(2,1)S(1)}, bf16[24,9,16,128]{3,2,1,0:T(8,128)(2,1)S(1)}, u32[]{:S(2)}, u32[]{:S(2)}) collective-permute-start(bf16[24,9,16,128]{3,2,1,0:T(8,128)(2,1)S(1)} %get-tuple-element.10), channel_id=1, source_target_pairs={{0,16},{16,0},{1,17},{17,1},{2,18},{18,2},{3,19},{19,3},{4,20},{20... | collective-permute-start | bytes 2654216 | tf_op jit(solution)/shard_map/ppermute | solution.py:219
  42.7 2.4 %collective-permute-done.3.got_ref = bf16[24,9,16,128]{3,2,1,0:T(8,128)(2,1)S(1)} collective-permute-done((bf16[24,9,16,128]{3,2,1,0:T(8,128)(2,1)S(1)}, bf16[24,9,16,128]{3,2,1,0:T(8,128)(2,1)S(1)}, u32[]{:S(2)}, u32[]{:S(2)}) %collective-permute-start.3) | collective-permute-done | bytes 884768 | tf_op jit(solution)/shard_map/ppermute | solution.py:219
  45.1 0.1 add_convert_fusion
  45.2 14.5 %all_to_all.21 = bf16[16,9,16,128]{3,2,1,0:T(8,128)(2,1)S(1)} all-to-all(bf16[16,9,16,128]{3,2,1,0:T(8,128)(2,1)S(1)} %add_convert_fusion), channel_id=1, replica_groups=mesh['z_far'=4,'z_near'=4,'core'=2,'ch_0'=4,'ch_1'=4] {'ch_0','ch_1'}, dimensions={0} | all-to-all | bytes 1179648 | tf_op jit(solution)/shard_map/all_to_all | solution.py:232
  59.7 0.1 convert_reduce_fusion
  59.8 12.1 %all_to_all.22 = bf16[4,9,16,128]{3,2,1,0:T(8,128)(2,1)S(1)} all-to-all(bf16[4,9,16,128]{3,2,1,0:T(8,128)(2,1)S(1)} %broadcast_in_dim.10), channel_id=1, replica_groups=mesh['z_far'=4,'z_near'=4,'core'=2,'ch_0'=4,'ch_1'=4] {'z_near'}, dimensions={0} | all-to-all | bytes 294912 | tf_op jit(solution)/shard_map/all_to_all | solution.py:232
  72.0 0.7 broadcast_in_dim.22
  72.7 11.8 %all-to-all-start.3 = ((bf16[4,9,16,128]{3,2,1,0:T(8,128)(2,1)}), bf16[4,9,16,128]{3,2,1,0:T(8,128)(2,1)S(1)}, u32[]{:S(2)}, u32[]{:S(2)}) async-start(bf16[4,9,16,128]{3,2,1,0:T(8,128)(2,1)} %broadcast_in_dim.22), calls=%async_computation.3 | async-start | bytes 294912 | tf_op jit(solution)/shard_map/all_to_all | solution.py:232
  84.5 5.5 %collective-permute-start.4 = (bf16[1,256,512]{2,1,0:T(8,128)(2,1)S(1)}, bf16[1,256,512]{2,1,0:T(8,128)(2,1)S(1)}, u32[]{:S(2)}, u32[]{:S(2)}) collective-permute-start(bf16[1,256,512]{2,1,0:T(8,128)(2,1)S(1)} %get-tuple-element.12), channel_id=1, source_target_pairs={{16,32},{48,64},{80,96},{112,128},{144,160},{176,192},{208,224},{2... | collective-permute-start | bytes 786440 | tf_op jit(solution)/shard_map/ppermute | solution.py:224
  90.0 6.8 %all-to-all-done.3 = bf16[4,9,16,128]{3,2,1,0:T(8,128)(2,1)S(1)} async-done(((bf16[4,9,16,128]{3,2,1,0:T(8,128)(2,1)}), bf16[4,9,16,128]{3,2,1,0:T(8,128)(2,1)S(1)}, u32[]{:S(2)}, u32[]{:S(2)}) %all-to-all-start.3) | async-done | bytes 147488 | tf_op jit(solution)/shard_map/all_to_all | solution.py:232
  96.7 6.4 %collective-permute-start.5 = (f32[9,16,128]{2,1,0:T(8,128)S(1)}, f32[9,16,128]{2,1,0:T(8,128)S(1)}, u32[]{:S(2)}, u32[]{:S(2)}) collective-permute-start(f32[9,16,128]{2,1,0:T(8,128)S(1)} %convert_reduce_fusion.1), channel_id=1, source_target_pairs={{0,16},{16,0},{1,17},{17,1},{2,18},{18,2},{3,19},{19,3},{4,20},{20... | collective-permute-start | bytes 221192 | tf_op jit(solution)/shard_map/ppermute | solution.py:219
  103.1 0.0 collective-permute-done.4.outer_ref
  103.1 0.0 copy-start.1
  103.1 1.2 %copy-done.1 = bf16[4,256,512]{2,1,0:T(8,128)(2,1)S(1)} copy-done((bf16[4,256,512]{2,1,0:T(8,128)(2,1)S(1)}, bf16[4,256,512]{2,1,0:T(8,128)(2,1)}, u32[]{:S(2)}) %copy-start.1) | copy-done | bytes 1048600
  104.4 4.1 %input.1 = bf16[4,256,512]{2,1,0:T(8,128)(2,1)} custom-call(s32[1]{0:T(128)} %bitcast.core_ref, bf16[24,9,16,128]{3,2,1,0:T(8,128)(2,1)S(1)} %collective-permute-done.3.got_ref, bf16[4,256,512]{2,1,0:T(8,128)(2,1)S(1)} %copy-done.1, bf16[1,256,512]{2,1,0:T(8,128)(2,1)S(1)} %collective-permute-done.4.outer_ref, ...), custom_call_target="tpu_custom_call" | custom-call | flops 2415919104 | bytes 4194304 | tf_op jit(solution)/shard_map/input/pallas_call | solution.py:203
  108.5 0.0 collective-permute-done.5
  108.5 0.7 pad_maximum_fusion
  (8 shorter events, 0.1 us)
Async XLA Ops:
  0.6 0.9 copy-start
  0.6 23.5 %copy-start.2 = (bf16[4,256,512]{2,1,0:T(8,128)(2,1)S(1)}, bf16[4,256,512]{2,1,0:T(8,128)(2,1)}, u32[]{:S(2)}) copy-start(bf16[4,256,512]{2,1,0:T(8,128)(2,1)} %feat_hbm.1) | copy-start | bytes 3145732
  19.4 14.7 %collective-permute-start.2 = (bf16[16,9,16,128]{3,2,1,0:T(8,128)(2,1)S(1)}, bf16[16,9,16,128]{3,2,1,0:T(8,128)(2,1)S(1)}, u32[]{:S(2)}, u32[]{:S(2)}) collective-permute-start(bf16[16,9,16,128]{3,2,1,0:T(8,128)(2,1)S(1)} %all_to_all.20.mine_ref), channel_id=1, source_target_pairs={{0,16},{16,0},{1,17},{17,1},{2,18},{18,2},{3,19},{19,3},{4,20},{20... | collective-permute-start | bytes 1769480 | tf_op jit(solution)/shard_map/ppermute | solution.py:219
  24.2 7.4 %copy-start.3 = (s32[64]{0:T(128)S(1)}, s32[64]{0:T(128)}, u32[]{:S(2)}) copy-start(s32[64]{0:T(128)} %param.7) | copy-start | bytes 772
  24.2 7.5 %collective-permute-start = (bf16[1,256,512]{2,1,0:T(8,128)(2,1)S(1)}, bf16[1,256,512]{2,1,0:T(8,128)(2,1)S(1)}, u32[]{:S(2)}, u32[]{:S(2)}) collective-permute-start(bf16[1,256,512]{2,1,0:T(8,128)(2,1)S(1)} %get-tuple-element.15), channel_id=1, source_target_pairs={{0,16},{16,0},{1,17},{17,1},{2,18},{18,2},{3,19},{19,3},{4,20},{20... | collective-permute-start | bytes 786440 | tf_op jit(solution)/shard_map/ppermute | solution.py:219
  26.2 7.9 %collective-permute-start.1 = (bf16[1,256,512]{2,1,0:T(8,128)(2,1)S(1)}, bf16[1,256,512]{2,1,0:T(8,128)(2,1)S(1)}, u32[]{:S(2)}, u32[]{:S(2)}) collective-permute-start(bf16[1,256,512]{2,1,0:T(8,128)(2,1)S(1)} %get-tuple-element.14), channel_id=1, source_target_pairs={{16,32},{48,64},{80,96},{112,128},{144,160},{176,192},{208,224},{2... | collective-permute-start | bytes 786440 | tf_op jit(solution)/shard_map/ppermute | solution.py:224
  40.8 4.3 %collective-permute-start.3 = (bf16[24,9,16,128]{3,2,1,0:T(8,128)(2,1)S(1)}, bf16[24,9,16,128]{3,2,1,0:T(8,128)(2,1)S(1)}, u32[]{:S(2)}, u32[]{:S(2)}) collective-permute-start(bf16[24,9,16,128]{3,2,1,0:T(8,128)(2,1)S(1)} %get-tuple-element.10), channel_id=1, source_target_pairs={{0,16},{16,0},{1,17},{17,1},{2,18},{18,2},{3,19},{19,3},{4,20},{20... | collective-permute-start | bytes 2654216 | tf_op jit(solution)/shard_map/ppermute | solution.py:219
  72.7 24.0 %all-to-all-start.3 = ((bf16[4,9,16,128]{3,2,1,0:T(8,128)(2,1)}), bf16[4,9,16,128]{3,2,1,0:T(8,128)(2,1)S(1)}, u32[]{:S(2)}, u32[]{:S(2)}) async-start(bf16[4,9,16,128]{3,2,1,0:T(8,128)(2,1)} %broadcast_in_dim.22), calls=%async_computation.3 | async-start | bytes 294912 | tf_op jit(solution)/shard_map/all_to_all | solution.py:232
  84.5 18.6 %collective-permute-start.4 = (bf16[1,256,512]{2,1,0:T(8,128)(2,1)S(1)}, bf16[1,256,512]{2,1,0:T(8,128)(2,1)S(1)}, u32[]{:S(2)}, u32[]{:S(2)}) collective-permute-start(bf16[1,256,512]{2,1,0:T(8,128)(2,1)S(1)} %get-tuple-element.12), channel_id=1, source_target_pairs={{16,32},{48,64},{80,96},{112,128},{144,160},{176,192},{208,224},{2... | collective-permute-start | bytes 786440 | tf_op jit(solution)/shard_map/ppermute | solution.py:224
  96.7 11.7 %collective-permute-start.5 = (f32[9,16,128]{2,1,0:T(8,128)S(1)}, f32[9,16,128]{2,1,0:T(8,128)S(1)}, u32[]{:S(2)}, u32[]{:S(2)}) collective-permute-start(f32[9,16,128]{2,1,0:T(8,128)S(1)} %convert_reduce_fusion.1), channel_id=1, source_target_pairs={{0,16},{16,0},{1,17},{17,1},{2,18},{18,2},{3,19},{19,3},{4,20},{20... | collective-permute-start | bytes 221192 | tf_op jit(solution)/shard_map/ppermute | solution.py:219
  103.1 1.2 %copy-start.1 = (bf16[4,256,512]{2,1,0:T(8,128)(2,1)S(1)}, bf16[4,256,512]{2,1,0:T(8,128)(2,1)}, u32[]{:S(2)}) copy-start(bf16[4,256,512]{2,1,0:T(8,128)(2,1)} %get-tuple-element.11.grad_ref) | copy-start | bytes 3145732

commit v8 on v7

--- a/solution.py
+++ b/solution.py
@@ -113,7 +113,7 @@
     half = ch // 2
     first = core_ref[0] == 0
     parts, taps = mine_ref.shape[:2]
-    groups = [got_ref[parts + g // taps, g % taps] for g in range(parts * (cells // COLS))]
+    groups = [got_ref[g // taps, g % taps] for g in range(parts * (cells // COLS))]
     images = [jnp.concatenate(groups[k : k + parts], 0) for k in range(0, len(groups), parts)]
     inner = jnp.concatenate(images, 1)
     outer = outer_ref[0]
@@ -256,9 +256,11 @@
     )
     got = exchange(sent)
     outer_grad = across_chips(outer_grad)
-    input_grad = call_input(where, got, grad_pre, outer_grad, mine, theirs)
-    other = got[: own.shape[0]]
-    block = total(swap((own + other.astype(F32)).astype(BF16), CH)).astype(BF16)
+    parts = own.shape[0]
+    pair = (own + got[:parts].astype(F32)).astype(BF16)
+    pair, inner_grad = lax.optimization_barrier((pair, got[parts:]))
+    input_grad = call_input(where, inner_grad, grad_pre, outer_grad, mine, theirs)
+    block = total(swap(pair, CH)).astype(BF16)
     block = total(swap(copies(block, "z_near"), "z_near")).astype(BF16)
     block = swap(copies(block, "z_far"), "z_far")
     mine = total(block)

time: 110 us -> 109 us (level)
  local copies, waits for them, and re-layouts: 2.92 us -> 1.73 us
    unnamed x8, local copies, waits for them, and re-layouts: 2.1 us -> 0.88 us
where the time goes in v8:
time: 109 us; the launch traced here: 108 us
  blocking collectives  44.5 us (41%)
  starting transfers between devices  36.1 us (33%)
  Pallas kernels  12.4 us (11%)
  waiting for transfers between devices  11.5 us (11%)
  local copies, waits for them, and re-layouts  1.73 us (2%)
    all_to_all x3, blocking collectives, swap(): return lax.all_to_all(parts, axis, 0, 0, tiled=True)  44.5 us
    ppermute x4, starting transfers between devices, exchange(): return lax.ppermute(block, 'core', [(0, 1), (1, 0)])  15 us
    all_to_all x1, starting transfers between devices, swap(): return lax.all_to_all(parts, axis, 0, 0, tiled=True)  11.8 us
    ppermute x2, starting transfers between devices, across_chips(): return lax.ppermute(block, ROWS, pairs + [(b, a) for a, b in pairs])  9.34 us
    all_to_all x1, waiting for transfers between devices, swap(): return lax.all_to_all(parts, axis, 0, 0, tiled=True)  6.76 us
    pallas_call x1, Pallas kernels, call_grad(): pl.pallas_call(grad_kernel, in_specs=smem(2) + vmem(6), out_specs=[HBM] +...  6.69 us
    pallas_call x1, Pallas kernels, call_input(): pl.pallas_call(input_kernel, in_specs=smem(1) + vmem(5), out_specs=vmem(1...  4.13 us
    ppermute x4, waiting for transfers between devices, exchange(): return lax.ppermute(block, 'core', [(0, 1), (1, 0)])  2.4 us
  transfers between devices with their start and end apart: 7, of which 3 were waited for; matrix products, arithmetic and copies ran while one was open for 0% of the time, Pallas kernels for 5%

profile of v8, /device:TPU:1, one launch (start us, length us, event | category | flops | bytes accessed | tf_op | source)
XLA Modules:
  0.0 108.1 jit_solution(17282695232872003939)
XLA Ops:
  0.6 0.0 copy-start
  0.6 0.0 copy-start.2
  0.7 0.9 copy-done
  1.5 0.1 broadcast_in_dim.9
  1.6 17.8 %all_to_all.20.mine_ref = bf16[16,9,16,128]{3,2,1,0:T(8,128)(2,1)S(1)} all-to-all(bf16[16,9,16,128]{3,2,1,0:T(8,128)(2,1)S(1)} %broadcast_in_dim.9), channel_id=1, replica_groups=mesh['z_far'=4,'z_near'=4,'core'=2,'ch_0'=4,'ch_1'=4] {'ch_0','ch_1'}, dimensions={0} | all-to-all | bytes 1179648 | tf_op jit(solution)/shard_map/all_to_all | solution.py:232
  19.4 4.8 %collective-permute-start.2 = (bf16[16,9,16,128]{3,2,1,0:T(8,128)(2,1)S(1)}, bf16[16,9,16,128]{3,2,1,0:T(8,128)(2,1)S(1)}, u32[]{:S(2)}, u32[]{:S(2)}) collective-permute-start(bf16[16,9,16,128]{3,2,1,0:T(8,128)(2,1)S(1)} %all_to_all.20.mine_ref), channel_id=1, source_target_pairs={{0,16},{16,0},{1,17},{17,1},{2,18},{18,2},{3,19},{19,3},{4,20},{20... | collective-permute-start | bytes 1769480 | tf_op jit(solution)/shard_map/ppermute | solution.py:219
  24.2 0.0 copy-done.2
  24.2 0.0 copy-start.3
  24.2 1.9 %collective-permute-start = (bf16[1,256,512]{2,1,0:T(8,128)(2,1)S(1)}, bf16[1,256,512]{2,1,0:T(8,128)(2,1)S(1)}, u32[]{:S(2)}, u32[]{:S(2)}) collective-permute-start(bf16[1,256,512]{2,1,0:T(8,128)(2,1)S(1)} %get-tuple-element.19), channel_id=1, source_target_pairs={{0,16},{16,0},{1,17},{17,1},{2,18},{18,2},{3,19},{19,3},{4,20},{20... | collective-permute-start | bytes 786440 | tf_op jit(solution)/shard_map/ppermute | solution.py:219
  26.2 3.9 %collective-permute-start.1 = (bf16[1,256,512]{2,1,0:T(8,128)(2,1)S(1)}, bf16[1,256,512]{2,1,0:T(8,128)(2,1)S(1)}, u32[]{:S(2)}, u32[]{:S(2)}) collective-permute-start(bf16[1,256,512]{2,1,0:T(8,128)(2,1)S(1)} %get-tuple-element.18), channel_id=1, source_target_pairs={{16,32},{48,64},{80,96},{112,128},{144,160},{176,192},{208,224},{2... | collective-permute-start | bytes 786440 | tf_op jit(solution)/shard_map/ppermute | solution.py:224
  30.1 1.6 %stage.1 = (bf16[4,256,512]{2,1,0:T(8,128)(2,1)S(1)}, bf16[4,256,512]{2,1,0:T(8,128)(2,1)S(1)}) custom-call(bf16[4,256,512]{2,1,0:T(8,128)(2,1)} %feat_hbm.1, bf16[4,256,512]{2,1,0:T(8,128)(2,1)} %cot_hbm.1), custom_call_target="tpu_custom_call" | custom-call | flops 1048576 | bytes 4194304 | tf_op jit(solution)/shard_map/stage/pallas_call | solution.py:163
  31.6 0.0 copy-done.3
  31.6 0.1 dynamic-slice_subtract_fusion.limits_ref
  31.7 0.0 collective-permute-done.inner_ref
  31.7 2.4 %collective-permute-done.1.outer_ref = bf16[1,256,512]{2,1,0:T(8,128)(2,1)S(1)} collective-permute-done((bf16[1,256,512]{2,1,0:T(8,128)(2,1)S(1)}, bf16[1,256,512]{2,1,0:T(8,128)(2,1)S(1)}, u32[]{:S(2)}, u32[]{:S(2)}) %collective-permute-start.1) | collective-permute-done | bytes 262176 | tf_op jit(solution)/shard_map/ppermute | solution.py:224
  34.1 0.0 collective-permute-done.2.theirs_ref
  34.1 6.7 %grad.1 = (bf16[4,256,512]{2,1,0:T(8,128)(2,1)}, bf16[1,256,512]{2,1,0:T(8,128)(2,1)S(1)}, f32[16,9,16,128]{3,2,1,0:T(8,128)S(1)}, bf16[24,9,16,128]{3,2,1,0:T(8,128)(2,1)S(1)}) custom-call(s32[4]{0:T(128)S(1)} %dynamic-slice_subtract_fusion.limits_ref, s32[1]{0:T(128)} %bitcast.core_ref, bf16[1,256,512]{2,1,0:T(8,128)(2,1)S(1)} %collective-permute-done.inner_ref, ...), custom_call_target="tpu_custom_call" | custom-call | flops 4831838208 | bytes 8388608 | tf_op jit(solution)/shard_map/grad/pallas_call | solution.py:179
  40.8 1.9 %collective-permute-start.3 = (bf16[24,9,16,128]{3,2,1,0:T(8,128)(2,1)S(1)}, bf16[24,9,16,128]{3,2,1,0:T(8,128)(2,1)S(1)}, u32[]{:S(2)}, u32[]{:S(2)}) collective-permute-start(bf16[24,9,16,128]{3,2,1,0:T(8,128)(2,1)S(1)} %get-tuple-element.13), channel_id=1, source_target_pairs={{0,16},{16,0},{1,17},{17,1},{2,18},{18,2},{3,19},{19,3},{4,20},{20... | collective-permute-start | bytes 2654216 | tf_op jit(solution)/shard_map/ppermute | solution.py:219
  42.7 2.4 %collective-permute-done.3 = bf16[24,9,16,128]{3,2,1,0:T(8,128)(2,1)S(1)} collective-permute-done((bf16[24,9,16,128]{3,2,1,0:T(8,128)(2,1)S(1)}, bf16[24,9,16,128]{3,2,1,0:T(8,128)(2,1)S(1)}, u32[]{:S(2)}, u32[]{:S(2)}) %collective-permute-start.3) | collective-permute-done | bytes 884768 | tf_op jit(solution)/shard_map/ppermute | solution.py:219
  45.1 0.1 add_convert_fusion
  45.3 14.5 %all_to_all.21 = bf16[16,9,16,128]{3,2,1,0:T(8,128)(2,1)S(1)} all-to-all(bf16[16,9,16,128]{3,2,1,0:T(8,128)(2,1)S(1)} %add_convert_fusion), channel_id=1, replica_groups=mesh['z_far'=4,'z_near'=4,'core'=2,'ch_0'=4,'ch_1'=4] {'ch_0','ch_1'}, dimensions={0} | all-to-all | bytes 1179648 | tf_op jit(solution)/shard_map/all_to_all | solution.py:232
  59.8 0.1 convert_reduce_fusion
  59.9 12.3 %all_to_all.22 = bf16[4,9,16,128]{3,2,1,0:T(8,128)(2,1)S(1)} all-to-all(bf16[4,9,16,128]{3,2,1,0:T(8,128)(2,1)S(1)} %broadcast_in_dim.10), channel_id=1, replica_groups=mesh['z_far'=4,'z_near'=4,'core'=2,'ch_0'=4,'ch_1'=4] {'z_near'}, dimensions={0} | all-to-all | bytes 294912 | tf_op jit(solution)/shard_map/all_to_all | solution.py:232
  72.2 0.7 broadcast_in_dim.22
  72.9 11.8 %all-to-all-start.3 = ((bf16[4,9,16,128]{3,2,1,0:T(8,128)(2,1)}), bf16[4,9,16,128]{3,2,1,0:T(8,128)(2,1)S(1)}, u32[]{:S(2)}, u32[]{:S(2)}) async-start(bf16[4,9,16,128]{3,2,1,0:T(8,128)(2,1)} %broadcast_in_dim.22), calls=%async_computation.3 | async-start | bytes 294912 | tf_op jit(solution)/shard_map/all_to_all | solution.py:232
  84.7 5.5 %collective-permute-start.4 = (bf16[1,256,512]{2,1,0:T(8,128)(2,1)S(1)}, bf16[1,256,512]{2,1,0:T(8,128)(2,1)S(1)}, u32[]{:S(2)}, u32[]{:S(2)}) collective-permute-start(bf16[1,256,512]{2,1,0:T(8,128)(2,1)S(1)} %get-tuple-element.16), channel_id=1, source_target_pairs={{16,32},{48,64},{80,96},{112,128},{144,160},{176,192},{208,224},{2... | collective-permute-start | bytes 786440 | tf_op jit(solution)/shard_map/ppermute | solution.py:224
  90.1 6.8 %all-to-all-done.3 = bf16[4,9,16,128]{3,2,1,0:T(8,128)(2,1)S(1)} async-done(((bf16[4,9,16,128]{3,2,1,0:T(8,128)(2,1)}), bf16[4,9,16,128]{3,2,1,0:T(8,128)(2,1)S(1)}, u32[]{:S(2)}, u32[]{:S(2)}) %all-to-all-start.3) | async-done | bytes 147488 | tf_op jit(solution)/shard_map/all_to_all | solution.py:232
  96.9 6.4 %collective-permute-start.5 = (f32[9,16,128]{2,1,0:T(8,128)S(1)}, f32[9,16,128]{2,1,0:T(8,128)S(1)}, u32[]{:S(2)}, u32[]{:S(2)}) collective-permute-start(f32[9,16,128]{2,1,0:T(8,128)S(1)} %convert_reduce_fusion.1), channel_id=1, source_target_pairs={{0,16},{16,0},{1,17},{17,1},{2,18},{18,2},{3,19},{19,3},{4,20},{20... | collective-permute-start | bytes 221192 | tf_op jit(solution)/shard_map/ppermute | solution.py:219
  103.3 0.0 collective-permute-done.4.outer_ref
  103.3 4.1 %input.1 = bf16[4,256,512]{2,1,0:T(8,128)(2,1)} custom-call(s32[1]{0:T(128)} %bitcast.core_ref, bf16[8,9,16,128]{3,2,1,0:T(8,128)(2,1)S(1)} %slice.9.got_ref, bf16[4,256,512]{2,1,0:T(8,128)(2,1)S(1)} %copy-done.1, bf16[1,256,512]{2,1,0:T(8,128)(2,1)S(1)} %collective-permute-done.4.outer_ref, bf16[16,9,16,128]{3,2,1,0:T(8,128)(2,1)S(1)} %all_to_all.20.mine_ref, ...), custom_call_target="tpu_custom_call" | custom-call | flops 2415919104 | bytes 4194304 | tf_op jit(solution)/shard_map/input/pallas_call | solution.py:203
  107.4 0.0 collective-permute-done.5
  107.5 0.7 pad_maximum_fusion
  (9 shorter events, 0.2 us)
Async XLA Ops:
  0.6 0.9 copy-start
  0.6 23.5 %copy-start.2 = (bf16[4,256,512]{2,1,0:T(8,128)(2,1)S(1)}, bf16[4,256,512]{2,1,0:T(8,128)(2,1)}, u32[]{:S(2)}) copy-start(bf16[4,256,512]{2,1,0:T(8,128)(2,1)} %feat_hbm.1) | copy-start | bytes 3145732
  19.4 14.7 %collective-permute-start.2 = (bf16[16,9,16,128]{3,2,1,0:T(8,128)(2,1)S(1)}, bf16[16,9,16,128]{3,2,1,0:T(8,128)(2,1)S(1)}, u32[]{:S(2)}, u32[]{:S(2)}) collective-permute-start(bf16[16,9,16,128]{3,2,1,0:T(8,128)(2,1)S(1)} %all_to_all.20.mine_ref), channel_id=1, source_target_pairs={{0,16},{16,0},{1,17},{17,1},{2,18},{18,2},{3,19},{19,3},{4,20},{20... | collective-permute-start | bytes 1769480 | tf_op jit(solution)/shard_map/ppermute | solution.py:219
  24.2 7.4 %copy-start.3 = (s32[64]{0:T(128)S(1)}, s32[64]{0:T(128)}, u32[]{:S(2)}) copy-start(s32[64]{0:T(128)} %param.7) | copy-start | bytes 772
  24.2 7.5 %collective-permute-start = (bf16[1,256,512]{2,1,0:T(8,128)(2,1)S(1)}, bf16[1,256,512]{2,1,0:T(8,128)(2,1)S(1)}, u32[]{:S(2)}, u32[]{:S(2)}) collective-permute-start(bf16[1,256,512]{2,1,0:T(8,128)(2,1)S(1)} %get-tuple-element.19), channel_id=1, source_target_pairs={{0,16},{16,0},{1,17},{17,1},{2,18},{18,2},{3,19},{19,3},{4,20},{20... | collective-permute-start | bytes 786440 | tf_op jit(solution)/shard_map/ppermute | solution.py:219
  26.2 7.9 %collective-permute-start.1 = (bf16[1,256,512]{2,1,0:T(8,128)(2,1)S(1)}, bf16[1,256,512]{2,1,0:T(8,128)(2,1)S(1)}, u32[]{:S(2)}, u32[]{:S(2)}) collective-permute-start(bf16[1,256,512]{2,1,0:T(8,128)(2,1)S(1)} %get-tuple-element.18), channel_id=1, source_target_pairs={{16,32},{48,64},{80,96},{112,128},{144,160},{176,192},{208,224},{2... | collective-permute-start | bytes 786440 | tf_op jit(solution)/shard_map/ppermute | solution.py:224
  40.8 4.3 %collective-permute-start.3 = (bf16[24,9,16,128]{3,2,1,0:T(8,128)(2,1)S(1)}, bf16[24,9,16,128]{3,2,1,0:T(8,128)(2,1)S(1)}, u32[]{:S(2)}, u32[]{:S(2)}) collective-permute-start(bf16[24,9,16,128]{3,2,1,0:T(8,128)(2,1)S(1)} %get-tuple-element.13), channel_id=1, source_target_pairs={{0,16},{16,0},{1,17},{17,1},{2,18},{18,2},{3,19},{19,3},{4,20},{20... | collective-permute-start | bytes 2654216 | tf_op jit(solution)/shard_map/ppermute | solution.py:219
  59.8 43.6 %copy-start.1 = (bf16[4,256,512]{2,1,0:T(8,128)(2,1)S(1)}, bf16[4,256,512]{2,1,0:T(8,128)(2,1)}, u32[]{:S(2)}) copy-start(bf16[4,256,512]{2,1,0:T(8,128)(2,1)} %get-tuple-element.15.grad_ref) | copy-start | bytes 3145732
  72.9 24.0 %all-to-all-start.3 = ((bf16[4,9,16,128]{3,2,1,0:T(8,128)(2,1)}), bf16[4,9,16,128]{3,2,1,0:T(8,128)(2,1)S(1)}, u32[]{:S(2)}, u32[]{:S(2)}) async-start(bf16[4,9,16,128]{3,2,1,0:T(8,128)(2,1)} %broadcast_in_dim.22), calls=%async_computation.3 | async-start | bytes 294912 | tf_op jit(solution)/shard_map/all_to_all | solution.py:232
  84.7 18.6 %collective-permute-start.4 = (bf16[1,256,512]{2,1,0:T(8,128)(2,1)S(1)}, bf16[1,256,512]{2,1,0:T(8,128)(2,1)S(1)}, u32[]{:S(2)}, u32[]{:S(2)}) collective-permute-start(bf16[1,256,512]{2,1,0:T(8,128)(2,1)S(1)} %get-tuple-element.16), channel_id=1, source_target_pairs={{16,32},{48,64},{80,96},{112,128},{144,160},{176,192},{208,224},{2... | collective-permute-start | bytes 786440 | tf_op jit(solution)/shard_map/ppermute | solution.py:224
  96.9 10.5 %collective-permute-start.5 = (f32[9,16,128]{2,1,0:T(8,128)S(1)}, f32[9,16,128]{2,1,0:T(8,128)S(1)}, u32[]{:S(2)}, u32[]{:S(2)}) collective-permute-start(f32[9,16,128]{2,1,0:T(8,128)S(1)} %convert_reduce_fusion.1), channel_id=1, source_target_pairs={{0,16},{16,0},{1,17},{17,1},{2,18},{18,2},{3,19},{19,3},{4,20},{20... | collective-permute-start | bytes 221192 | tf_op jit(solution)/shard_map/ppermute | solution.py:219

commit v9 on v8

--- a/solution.py
+++ b/solution.py
@@ -33,6 +33,19 @@
             tile = source[:, image * COLS : (image + 1) * COLS]
             for side in (0, 2):
                 out_ref[side, rows, pl.ds(row * cells + image * COLS, COLS)] = side_shift(tile, side - 1)
+
+
+def spread_kernel(core_ref, weight_hbm, out_hbm, half_ref, sems):
+    peers, _, _, half = out_hbm.shape
+    lanes = pl.ds(pl.multiple_of(core_ref[0] * half, half), half)
+    load = pltpu.make_async_copy(weight_hbm.at[:, :, lanes], half_ref, sems.at[peers])
+    load.start()
+    load.wait()
+    saves = [pltpu.make_async_copy(half_ref, out_hbm.at[p], sems.at[p]) for p in range(peers)]
+    for save in saves:
+        save.start()
+    for save in saves:
+        save.wait()
 
 
 def stage_kernel(feat_hbm, cot_hbm, feat_ref, cot_ref, sems):
@@ -159,6 +172,21 @@
     )
 
 
+def call_spread(core, weight, peers):
+    taps, near_ch, ch = weight.shape
+    part = (taps, near_ch, ch // 2)
+    return pl.pallas_call(
+        spread_kernel,
+        in_specs=smem(1) + [HBM],
+        out_specs=HBM,
+        out_shape=pltpu.HBM((peers, *part), BF16),
+        scratch_shapes=[pltpu.VMEM(part, BF16), pltpu.SemaphoreType.DMA((peers + 1,))],
+        cost_estimate=pl.CostEstimate(flops=1 << 10, bytes_accessed=1 << 20, transcendentals=0),
+        compiler_params=pltpu.CompilerParams(vmem_limit_bytes=4 << 20),
+        name="spread",
+    )(core, in_hbm(weight))
+
+
 def call_stage(features, cotangent):
     return pl.pallas_call(
         stage_kernel,
@@ -240,17 +268,16 @@
     band, ch, cells = features.shape
     images = cells // COLS
     near = conv_weight.shape[2]
-    half = ch // 2
     core = lax.axis_index("core").astype(jnp.int32)
     limits = lax.dynamic_slice_in_dim(valid_rows, lax.axis_index(CH) * images, images, 0)
     limits = limits - lax.axis_index(ROWS) * band
-    share = lax.dynamic_slice_in_dim(conv_weight, core * half, half, 3).reshape(9, near, half)
+    where = core.reshape(1)
+    shares = call_spread(where, conv_weight.reshape(9, near, ch), lax.axis_size(CH))
     inner = exchange(lax.dynamic_slice_in_dim(features, (1 - core) * (band - 1), 1, 0))
     outer = across_chips(lax.dynamic_slice_in_dim(features, core * (band - 1), 1, 0))
-    mine = swap(copies(share, CH), CH)
+    mine = swap(shares, CH)
     theirs = exchange(mine)
     features, cotangent = call_stage(features, cotangent)
-    where = core.reshape(1)
     grad_pre, outer_grad, own, sent = call_grad(
         limits, where, inner, features, outer, mine, theirs, cotangent
     )

time: 109 us -> 109 us (level)
  Pallas kernels: 12.4 us -> 13.9 us
    pallas_call x0 -> x1, Pallas kernels: none -> 1.8 us  [call_spread(): pl.pallas_call(spread_kernel, in_specs=smem(1) + [HBM], out_specs=HBM, ou...]
where the time goes in v9:
time: 109 us
  blocking collectives  44.1 us (40%)
  starting transfers between devices  36.8 us (34%)
  Pallas kernels  13.9 us (13%)
  waiting for transfers between devices  11.5 us (11%)
    all_to_all x3, blocking collectives, swap(): return lax.all_to_all(parts, axis, 0, 0, tiled=True)  44.1 us
    ppermute x4, starting transfers between devices, exchange(): return lax.ppermute(block, 'core', [(0, 1), (1, 0)])  15.6 us
    all_to_all x1, starting transfers between devices, swap(): return lax.all_to_all(parts, axis, 0, 0, tiled=True)  11.8 us
    ppermute x2, starting transfers between devices, across_chips(): return lax.ppermute(block, ROWS, pairs + [(b, a) for a, b in pairs])  9.35 us
    all_to_all x1, waiting for transfers between devices, swap(): return lax.all_to_all(parts, axis, 0, 0, tiled=True)  6.76 us
    pallas_call x1, Pallas kernels, call_grad(): pl.pallas_call(grad_kernel, in_specs=smem(2) + vmem(6), out_specs=[HBM] +...  6.43 us
    pallas_call x1, Pallas kernels, call_input(): pl.pallas_call(input_kernel, in_specs=smem(1) + vmem(5), out_specs=vmem(1...  4.1 us
    ppermute x4, waiting for transfers between devices, exchange(): return lax.ppermute(block, 'core', [(0, 1), (1, 0)])  2.4 us
  transfers between devices with their start and end apart: 7, of which 3 were waited for; matrix products, arithmetic and copies ran while one was open for 0% of the time, Pallas kernels for 5%

profile of v9, /device:TPU:1, one launch (start us, length us, event | category | flops | bytes accessed | tf_op | source)
XLA Modules:
  0.0 108.9 jit_solution(16848540130550238668)
XLA Ops:
  0.6 0.0 copy-start.1
  0.6 1.8 %spread.1 = bf16[16,9,16,128]{3,2,1,0:T(8,128)(2,1)} custom-call(s32[1]{0:T(128)} %bitcast.core_ref, bf16[9,16,256]{2,1,0:T(8,128)(2,1)} %bitcast.4), custom_call_target="tpu_custom_call" | custom-call | flops 1024 | bytes 1048576 | tf_op jit(solution)/shard_map/spread/pallas_call | solution.py:178
  2.5 17.4 %all_to_all.20.mine_ref = bf16[16,9,16,128]{3,2,1,0:T(8,128)(2,1)S(1)} all-to-all(bf16[16,9,16,128]{3,2,1,0:T(8,128)(2,1)} %spread.1), channel_id=1, replica_groups=mesh['z_far'=4,'z_near'=4,'core'=2,'ch_0'=4,'ch_1'=4] {'ch_0','ch_1'}, dimensions={0} | all-to-all | bytes 1179648 | tf_op jit(solution)/shard_map/all_to_all | solution.py:260
  19.8 5.4 %collective-permute-start.2 = (bf16[16,9,16,128]{3,2,1,0:T(8,128)(2,1)S(1)}, bf16[16,9,16,128]{3,2,1,0:T(8,128)(2,1)S(1)}, u32[]{:S(2)}, u32[]{:S(2)}) collective-permute-start(bf16[16,9,16,128]{3,2,1,0:T(8,128)(2,1)S(1)} %all_to_all.20.mine_ref), channel_id=1, source_target_pairs={{0,16},{16,0},{1,17},{17,1},{2,18},{18,2},{3,19},{19,3},{4,20},{20... | collective-permute-start | bytes 1769480 | tf_op jit(solution)/shard_map/ppermute | solution.py:247
  25.2 0.0 copy-done.1
  25.3 0.0 copy-start.2
  25.3 1.9 %collective-permute-start = (bf16[1,256,512]{2,1,0:T(8,128)(2,1)S(1)}, bf16[1,256,512]{2,1,0:T(8,128)(2,1)S(1)}, u32[]{:S(2)}, u32[]{:S(2)}) collective-permute-start(bf16[1,256,512]{2,1,0:T(8,128)(2,1)S(1)} %get-tuple-element.19), channel_id=1, source_target_pairs={{0,16},{16,0},{1,17},{17,1},{2,18},{18,2},{3,19},{19,3},{4,20},{20... | collective-permute-start | bytes 786440 | tf_op jit(solution)/shard_map/ppermute | solution.py:247
  27.2 3.9 %collective-permute-start.1 = (bf16[1,256,512]{2,1,0:T(8,128)(2,1)S(1)}, bf16[1,256,512]{2,1,0:T(8,128)(2,1)S(1)}, u32[]{:S(2)}, u32[]{:S(2)}) collective-permute-start(bf16[1,256,512]{2,1,0:T(8,128)(2,1)S(1)} %get-tuple-element.18), channel_id=1, source_target_pairs={{16,32},{48,64},{80,96},{112,128},{144,160},{176,192},{208,224},{2... | collective-permute-start | bytes 786440 | tf_op jit(solution)/shard_map/ppermute | solution.py:252
  31.1 1.6 %stage.1 = (bf16[4,256,512]{2,1,0:T(8,128)(2,1)S(1)}, bf16[4,256,512]{2,1,0:T(8,128)(2,1)S(1)}) custom-call(bf16[4,256,512]{2,1,0:T(8,128)(2,1)} %feat_hbm.1, bf16[4,256,512]{2,1,0:T(8,128)(2,1)} %cot_hbm.1), custom_call_target="tpu_custom_call" | custom-call | flops 1048576 | bytes 4194304 | tf_op jit(solution)/shard_map/stage/pallas_call | solution.py:191
  32.7 0.0 copy-done.2
  32.7 0.1 dynamic-slice_subtract_fusion.limits_ref
  32.8 0.0 collective-permute-done.inner_ref
  32.8 2.4 %collective-permute-done.1.outer_ref = bf16[1,256,512]{2,1,0:T(8,128)(2,1)S(1)} collective-permute-done((bf16[1,256,512]{2,1,0:T(8,128)(2,1)S(1)}, bf16[1,256,512]{2,1,0:T(8,128)(2,1)S(1)}, u32[]{:S(2)}, u32[]{:S(2)}) %collective-permute-start.1) | collective-permute-done | bytes 262176 | tf_op jit(solution)/shard_map/ppermute | solution.py:252
  35.1 0.0 collective-permute-done.2.theirs_ref
  35.2 6.4 %grad.1 = (bf16[4,256,512]{2,1,0:T(8,128)(2,1)}, bf16[1,256,512]{2,1,0:T(8,128)(2,1)S(1)}, f32[16,9,16,128]{3,2,1,0:T(8,128)S(1)}, bf16[24,9,16,128]{3,2,1,0:T(8,128)(2,1)S(1)}) custom-call(s32[4]{0:T(128)S(1)} %dynamic-slice_subtract_fusion.limits_ref, s32[1]{0:T(128)} %bitcast.core_ref, bf16[1,256,512]{2,1,0:T(8,128)(2,1)S(1)} %collective-permute-done.inner_ref, ...), custom_call_target="tpu_custom_call" | custom-call | flops 4831838208 | bytes 8388608 | tf_op jit(solution)/shard_map/grad/pallas_call | solution.py:207
  41.6 1.9 %collective-permute-start.3 = (bf16[24,9,16,128]{3,2,1,0:T(8,128)(2,1)S(1)}, bf16[24,9,16,128]{3,2,1,0:T(8,128)(2,1)S(1)}, u32[]{:S(2)}, u32[]{:S(2)}) collective-permute-start(bf16[24,9,16,128]{3,2,1,0:T(8,128)(2,1)S(1)} %get-tuple-element.13), channel_id=1, source_target_pairs={{0,16},{16,0},{1,17},{17,1},{2,18},{18,2},{3,19},{19,3},{4,20},{20... | collective-permute-start | bytes 2654216 | tf_op jit(solution)/shard_map/ppermute | solution.py:247
  43.5 2.4 %collective-permute-done.3 = bf16[24,9,16,128]{3,2,1,0:T(8,128)(2,1)S(1)} collective-permute-done((bf16[24,9,16,128]{3,2,1,0:T(8,128)(2,1)S(1)}, bf16[24,9,16,128]{3,2,1,0:T(8,128)(2,1)S(1)}, u32[]{:S(2)}, u32[]{:S(2)}) %collective-permute-start.3) | collective-permute-done | bytes 884768 | tf_op jit(solution)/shard_map/ppermute | solution.py:247
  45.9 0.1 add_convert_fusion
  46.1 14.5 %all_to_all.21 = bf16[16,9,16,128]{3,2,1,0:T(8,128)(2,1)S(1)} all-to-all(bf16[16,9,16,128]{3,2,1,0:T(8,128)(2,1)S(1)} %add_convert_fusion), channel_id=1, replica_groups=mesh['z_far'=4,'z_near'=4,'core'=2,'ch_0'=4,'ch_1'=4] {'ch_0','ch_1'}, dimensions={0} | all-to-all | bytes 1179648 | tf_op jit(solution)/shard_map/all_to_all | solution.py:260
  60.5 0.0 copy-start
  60.5 0.1 convert_reduce_fusion
  60.7 12.3 %all_to_all.22 = bf16[4,9,16,128]{3,2,1,0:T(8,128)(2,1)S(1)} all-to-all(bf16[4,9,16,128]{3,2,1,0:T(8,128)(2,1)S(1)} %broadcast_in_dim.4), channel_id=1, replica_groups=mesh['z_far'=4,'z_near'=4,'core'=2,'ch_0'=4,'ch_1'=4] {'z_near'}, dimensions={0} | all-to-all | bytes 294912 | tf_op jit(solution)/shard_map/all_to_all | solution.py:260
  73.0 0.7 broadcast_in_dim.5
  73.6 11.8 %all-to-all-start.3 = ((bf16[4,9,16,128]{3,2,1,0:T(8,128)(2,1)}), bf16[4,9,16,128]{3,2,1,0:T(8,128)(2,1)S(1)}, u32[]{:S(2)}, u32[]{:S(2)}) async-start(bf16[4,9,16,128]{3,2,1,0:T(8,128)(2,1)} %broadcast_in_dim.5), calls=%async_computation.3 | async-start | bytes 294912 | tf_op jit(solution)/shard_map/all_to_all | solution.py:260
  85.5 5.5 %collective-permute-start.4 = (bf16[1,256,512]{2,1,0:T(8,128)(2,1)S(1)}, bf16[1,256,512]{2,1,0:T(8,128)(2,1)S(1)}, u32[]{:S(2)}, u32[]{:S(2)}) collective-permute-start(bf16[1,256,512]{2,1,0:T(8,128)(2,1)S(1)} %get-tuple-element.16), channel_id=1, source_target_pairs={{16,32},{48,64},{80,96},{112,128},{144,160},{176,192},{208,224},{2... | collective-permute-start | bytes 786440 | tf_op jit(solution)/shard_map/ppermute | solution.py:252
  90.9 6.8 %all-to-all-done.3 = bf16[4,9,16,128]{3,2,1,0:T(8,128)(2,1)S(1)} async-done(((bf16[4,9,16,128]{3,2,1,0:T(8,128)(2,1)}), bf16[4,9,16,128]{3,2,1,0:T(8,128)(2,1)S(1)}, u32[]{:S(2)}, u32[]{:S(2)}) %all-to-all-start.3) | async-done | bytes 147488 | tf_op jit(solution)/shard_map/all_to_all | solution.py:260
  97.7 6.4 %collective-permute-start.5 = (f32[9,16,128]{2,1,0:T(8,128)S(1)}, f32[9,16,128]{2,1,0:T(8,128)S(1)}, u32[]{:S(2)}, u32[]{:S(2)}) collective-permute-start(f32[9,16,128]{2,1,0:T(8,128)S(1)} %convert_reduce_fusion.1), channel_id=1, source_target_pairs={{0,16},{16,0},{1,17},{17,1},{2,18},{18,2},{3,19},{19,3},{4,20},{20... | collective-permute-start | bytes 221192 | tf_op jit(solution)/shard_map/ppermute | solution.py:247
  104.1 0.0 collective-permute-done.4.outer_ref
  104.1 0.0 copy-done
  104.1 4.1 %input.1 = bf16[4,256,512]{2,1,0:T(8,128)(2,1)} custom-call(s32[1]{0:T(128)} %bitcast.core_ref, bf16[8,9,16,128]{3,2,1,0:T(8,128)(2,1)S(1)} %slice.9.got_ref, bf16[4,256,512]{2,1,0:T(8,128)(2,1)S(1)} %copy-done, bf16[1,256,512]{2,1,0:T(8,128)(2,1)S(1)} %collective-permute-done.4.outer_ref, bf16[16,9,16,128]{3,2,1,0:T(8,128)(2,1)S(1)} %all_to_all.20.mine_ref, ...), custom_call_target="tpu_custom_call" | custom-call | flops 2415919104 | bytes 4194304 | tf_op jit(solution)/shard_map/input/pallas_call | solution.py:231
  108.2 0.0 collective-permute-done.5
  108.2 0.7 pad_maximum_fusion
  (6 shorter events, 0.1 us)
Async XLA Ops:
  0.6 24.6 %copy-start.1 = (bf16[4,256,512]{2,1,0:T(8,128)(2,1)S(1)}, bf16[4,256,512]{2,1,0:T(8,128)(2,1)}, u32[]{:S(2)}) copy-start(bf16[4,256,512]{2,1,0:T(8,128)(2,1)} %feat_hbm.1) | copy-start | bytes 3145732
  19.8 15.3 %collective-permute-start.2 = (bf16[16,9,16,128]{3,2,1,0:T(8,128)(2,1)S(1)}, bf16[16,9,16,128]{3,2,1,0:T(8,128)(2,1)S(1)}, u32[]{:S(2)}, u32[]{:S(2)}) collective-permute-start(bf16[16,9,16,128]{3,2,1,0:T(8,128)(2,1)S(1)} %all_to_all.20.mine_ref), channel_id=1, source_target_pairs={{0,16},{16,0},{1,17},{17,1},{2,18},{18,2},{3,19},{19,3},{4,20},{20... | collective-permute-start | bytes 1769480 | tf_op jit(solution)/shard_map/ppermute | solution.py:247
  25.3 7.4 %copy-start.2 = (s32[64]{0:T(128)S(1)}, s32[64]{0:T(128)}, u32[]{:S(2)}) copy-start(s32[64]{0:T(128)} %param.7) | copy-start | bytes 772
  25.3 7.5 %collective-permute-start = (bf16[1,256,512]{2,1,0:T(8,128)(2,1)S(1)}, bf16[1,256,512]{2,1,0:T(8,128)(2,1)S(1)}, u32[]{:S(2)}, u32[]{:S(2)}) collective-permute-start(bf16[1,256,512]{2,1,0:T(8,128)(2,1)S(1)} %get-tuple-element.19), channel_id=1, source_target_pairs={{0,16},{16,0},{1,17},{17,1},{2,18},{18,2},{3,19},{19,3},{4,20},{20... | collective-permute-start | bytes 786440 | tf_op jit(solution)/shard_map/ppermute | solution.py:247
  27.2 7.9 %collective-permute-start.1 = (bf16[1,256,512]{2,1,0:T(8,128)(2,1)S(1)}, bf16[1,256,512]{2,1,0:T(8,128)(2,1)S(1)}, u32[]{:S(2)}, u32[]{:S(2)}) collective-permute-start(bf16[1,256,512]{2,1,0:T(8,128)(2,1)S(1)} %get-tuple-element.18), channel_id=1, source_target_pairs={{16,32},{48,64},{80,96},{112,128},{144,160},{176,192},{208,224},{2... | collective-permute-start | bytes 786440 | tf_op jit(solution)/shard_map/ppermute | solution.py:252
  41.6 4.3 %collective-permute-start.3 = (bf16[24,9,16,128]{3,2,1,0:T(8,128)(2,1)S(1)}, bf16[24,9,16,128]{3,2,1,0:T(8,128)(2,1)S(1)}, u32[]{:S(2)}, u32[]{:S(2)}) collective-permute-start(bf16[24,9,16,128]{3,2,1,0:T(8,128)(2,1)S(1)} %get-tuple-element.13), channel_id=1, source_target_pairs={{0,16},{16,0},{1,17},{17,1},{2,18},{18,2},{3,19},{19,3},{4,20},{20... | collective-permute-start | bytes 2654216 | tf_op jit(solution)/shard_map/ppermute | solution.py:247
  60.5 43.6 %copy-start = (bf16[4,256,512]{2,1,0:T(8,128)(2,1)S(1)}, bf16[4,256,512]{2,1,0:T(8,128)(2,1)}, u32[]{:S(2)}) copy-start(bf16[4,256,512]{2,1,0:T(8,128)(2,1)} %get-tuple-element.15.grad_ref) | copy-start | bytes 3145732
  73.6 24.1 %all-to-all-start.3 = ((bf16[4,9,16,128]{3,2,1,0:T(8,128)(2,1)}), bf16[4,9,16,128]{3,2,1,0:T(8,128)(2,1)S(1)}, u32[]{:S(2)}, u32[]{:S(2)}) async-start(bf16[4,9,16,128]{3,2,1,0:T(8,128)(2,1)} %broadcast_in_dim.5), calls=%async_computation.3 | async-start | bytes 294912 | tf_op jit(solution)/shard_map/all_to_all | solution.py:260
  85.5 18.6 %collective-permute-start.4 = (bf16[1,256,512]{2,1,0:T(8,128)(2,1)S(1)}, bf16[1,256,512]{2,1,0:T(8,128)(2,1)S(1)}, u32[]{:S(2)}, u32[]{:S(2)}) collective-permute-start(bf16[1,256,512]{2,1,0:T(8,128)(2,1)S(1)} %get-tuple-element.16), channel_id=1, source_target_pairs={{16,32},{48,64},{80,96},{112,128},{144,160},{176,192},{208,224},{2... | collective-permute-start | bytes 786440 | tf_op jit(solution)/shard_map/ppermute | solution.py:252
  97.7 10.5 %collective-permute-start.5 = (f32[9,16,128]{2,1,0:T(8,128)S(1)}, f32[9,16,128]{2,1,0:T(8,128)S(1)}, u32[]{:S(2)}, u32[]{:S(2)}) collective-permute-start(f32[9,16,128]{2,1,0:T(8,128)S(1)} %convert_reduce_fusion.1), channel_id=1, source_target_pairs={{0,16},{16,0},{1,17},{17,1},{2,18},{18,2},{3,19},{19,3},{4,20},{20... | collective-permute-start | bytes 221192 | tf_op jit(solution)/shard_map/ppermute | solution.py:247

commit v10 on v9

--- a/solution.py
+++ b/solution.py
@@ -42,6 +42,28 @@
     load.start()
     load.wait()
     saves = [pltpu.make_async_copy(half_ref, out_hbm.at[p], sems.at[p]) for p in range(peers)]
+    for save in saves:
+        save.start()
+    for save in saves:
+        save.wait()
+
+
+def sum_kernel(parts_ref, out_ref):
+    summed = parts_ref[0].astype(F32)
+    for p in range(1, parts_ref.shape[0]):
+        summed = summed + parts_ref[p].astype(F32)
+    for p in range(out_ref.shape[0]):
+        out_ref[p] = summed.astype(BF16)
+
+
+def join_kernel(core_ref, mine_ref, theirs_ref, out_hbm, sems):
+    half = mine_ref.shape[2]
+    near = pl.ds(pl.multiple_of(core_ref[0] * half, half), half)
+    far = pl.ds(pl.multiple_of((1 - core_ref[0]) * half, half), half)
+    saves = [
+        pltpu.make_async_copy(mine_ref, out_hbm.at[:, :, near], sems.at[0]),
+        pltpu.make_async_copy(theirs_ref, out_hbm.at[:, :, far], sems.at[1]),
+    ]
     for save in saves:
         save.start()
     for save in saves:
@@ -187,6 +209,32 @@
     )(core, in_hbm(weight))
 
 
+def call_sum(parts, copies):
+    return pl.pallas_call(
+        sum_kernel,
+        in_specs=vmem(1),
+        out_specs=vmem(1)[0],
+        out_shape=jax.ShapeDtypeStruct((copies, *parts.shape[1:]), BF16),
+        cost_estimate=pl.CostEstimate(flops=1 << 18, bytes_accessed=1 << 18, transcendentals=0),
+        compiler_params=pltpu.CompilerParams(vmem_limit_bytes=4 << 20),
+        name="sum",
+    )(parts)
+
+
+def call_join(core, mine, theirs):
+    taps, near_ch, half = mine.shape
+    return pl.pallas_call(
+        join_kernel,
+        in_specs=smem(1) + vmem(2),
+        out_specs=HBM,
+        out_shape=pltpu.HBM((taps, near_ch, 2 * half), F32),
+        scratch_shapes=[pltpu.SemaphoreType.DMA((2,))],
+        cost_estimate=pl.CostEstimate(flops=1 << 10, bytes_accessed=1 << 18, transcendentals=0),
+        compiler_params=pltpu.CompilerParams(vmem_limit_bytes=4 << 20),
+        name="join",
+    )(core, mine, theirs)
+
+
 def call_stage(features, cotangent):
     return pl.pallas_call(
         stage_kernel,
@@ -288,14 +336,11 @@
     pair, inner_grad = lax.optimization_barrier((pair, got[parts:]))
     input_grad = call_input(where, inner_grad, grad_pre, outer_grad, mine, theirs)
     block = total(swap(pair, CH)).astype(BF16)
-    block = total(swap(copies(block, "z_near"), "z_near")).astype(BF16)
-    block = swap(copies(block, "z_far"), "z_far")
+    block = call_sum(swap(copies(block, "z_near"), "z_near"), lax.axis_size("z_far"))
+    block = swap(block, "z_far")
     mine = total(block)
     theirs = exchange(mine)
-    first = core == 0
-    weight_grad = jnp.concatenate(
-        [jnp.where(first, mine, theirs), jnp.where(first, theirs, mine)], 2
-    ).reshape(3, 3, near, ch)
+    weight_grad = call_join(where, mine, theirs).reshape(3, 3, near, ch)
     return input_grad, weight_grad
 
 

time: 109 us -> 107 us (0.982)
  waiting for transfers between devices: 11.5 us -> 9.83 us
  Pallas kernels: 13.9 us -> 15.2 us
    ppermute x2, waiting for transfers between devices: 2.37 us -> 0.67 us  [across_chips(): return lax.ppermute(block, ROWS, pairs + [(b, a) for a, b in pairs])]
    pallas_call x0 -> x2, Pallas kernels: none -> 1.36 us  [the longest x1 0.68 us: call_sum(): pl.pallas_call(sum_kernel, in_specs=vmem(1), out_specs=vmem(1)[0], out_sh...]
where the time goes in v10:
time: 107 us
  blocking collectives  44.1 us (41%)
  starting transfers between devices  36.5 us (34%)
  Pallas kernels  15.2 us (14%)
  waiting for transfers between devices  9.83 us (9%)
    all_to_all x3, blocking collectives, swap(): return lax.all_to_all(parts, axis, 0, 0, tiled=True)  44.1 us
    ppermute x4, starting transfers between devices, exchange(): return lax.ppermute(block, 'core', [(0, 1), (1, 0)])  15.6 us
    all_to_all x1, starting transfers between devices, swap(): return lax.all_to_all(parts, axis, 0, 0, tiled=True)  12.1 us
    ppermute x2, starting transfers between devices, across_chips(): return lax.ppermute(block, ROWS, pairs + [(b, a) for a, b in pairs])  8.87 us
    all_to_all x1, waiting for transfers between devices, swap(): return lax.all_to_all(parts, axis, 0, 0, tiled=True)  6.76 us
    pallas_call x1, Pallas kernels, call_grad(): pl.pallas_call(grad_kernel, in_specs=smem(2) + vmem(6), out_specs=[HBM] +...  6.43 us
    pallas_call x1, Pallas kernels, call_input(): pl.pallas_call(input_kernel, in_specs=smem(1) + vmem(5), out_specs=vmem(1...  4.1 us
    ppermute x4, waiting for transfers between devices, exchange(): return lax.ppermute(block, 'core', [(0, 1), (1, 0)])  2.4 us
  transfers between devices with their start and end apart: 7, of which 3 were waited for; matrix products, arithmetic and copies ran while one was open for 0% of the time, Pallas kernels for 5%

profile of v10, /device:TPU:1, one launch (start us, length us, event | category | flops | bytes accessed | tf_op | source)
XLA Modules:
  0.0 106.9 jit_solution(17677957844275475336)
XLA Ops:
  0.6 0.0 copy-start.1
  0.6 1.8 %spread.1 = bf16[16,9,16,128]{3,2,1,0:T(8,128)(2,1)} custom-call(s32[1]{0:T(128)} %bitcast.core_ref, bf16[9,16,256]{2,1,0:T(8,128)(2,1)} %bitcast.4), custom_call_target="tpu_custom_call" | custom-call | flops 1024 | bytes 1048576 | tf_op jit(solution)/shard_map/spread/pallas_call | solution.py:200
  2.5 17.4 %all_to_all.20.mine_ref = bf16[16,9,16,128]{3,2,1,0:T(8,128)(2,1)S(1)} all-to-all(bf16[16,9,16,128]{3,2,1,0:T(8,128)(2,1)} %spread.1), channel_id=1, replica_groups=mesh['z_far'=4,'z_near'=4,'core'=2,'ch_0'=4,'ch_1'=4] {'ch_0','ch_1'}, dimensions={0} | all-to-all | bytes 1179648 | tf_op jit(solution)/shard_map/all_to_all | solution.py:308
  19.8 5.4 %collective-permute-start.2 = (bf16[16,9,16,128]{3,2,1,0:T(8,128)(2,1)S(1)}, bf16[16,9,16,128]{3,2,1,0:T(8,128)(2,1)S(1)}, u32[]{:S(2)}, u32[]{:S(2)}) collective-permute-start(bf16[16,9,16,128]{3,2,1,0:T(8,128)(2,1)S(1)} %all_to_all.20.mine_ref), channel_id=1, source_target_pairs={{0,16},{16,0},{1,17},{17,1},{2,18},{18,2},{3,19},{19,3},{4,20},{20... | collective-permute-start | bytes 1769480 | tf_op jit(solution)/shard_map/ppermute | solution.py:295
  25.2 0.0 copy-done.1
  25.3 0.0 copy-start.2
  25.3 3.4 %collective-permute-start.1 = (bf16[1,256,512]{2,1,0:T(8,128)(2,1)S(1)}, bf16[1,256,512]{2,1,0:T(8,128)(2,1)S(1)}, u32[]{:S(2)}, u32[]{:S(2)}) collective-permute-start(bf16[1,256,512]{2,1,0:T(8,128)(2,1)S(1)} %get-tuple-element.18), channel_id=1, source_target_pairs={{16,32},{48,64},{80,96},{112,128},{144,160},{176,192},{208,224},{2... | collective-permute-start | bytes 786440 | tf_op jit(solution)/shard_map/ppermute | solution.py:300
  28.7 1.9 %collective-permute-start = (bf16[1,256,512]{2,1,0:T(8,128)(2,1)S(1)}, bf16[1,256,512]{2,1,0:T(8,128)(2,1)S(1)}, u32[]{:S(2)}, u32[]{:S(2)}) collective-permute-start(bf16[1,256,512]{2,1,0:T(8,128)(2,1)S(1)} %get-tuple-element.19), channel_id=1, source_target_pairs={{0,16},{16,0},{1,17},{17,1},{2,18},{18,2},{3,19},{19,3},{4,20},{20... | collective-permute-start | bytes 786440 | tf_op jit(solution)/shard_map/ppermute | solution.py:295
  30.6 1.6 %stage.1 = (bf16[4,256,512]{2,1,0:T(8,128)(2,1)S(1)}, bf16[4,256,512]{2,1,0:T(8,128)(2,1)S(1)}) custom-call(bf16[4,256,512]{2,1,0:T(8,128)(2,1)} %feat_hbm.1, bf16[4,256,512]{2,1,0:T(8,128)(2,1)} %cot_hbm.1), custom_call_target="tpu_custom_call" | custom-call | flops 1048576 | bytes 4194304 | tf_op jit(solution)/shard_map/stage/pallas_call | solution.py:239
  32.2 0.0 copy-done.2
  32.2 0.1 dynamic-slice_subtract_fusion.limits_ref
  32.3 0.7 collective-permute-done.1.outer_ref
  33.0 0.0 collective-permute-done.inner_ref
  33.0 0.0 collective-permute-done.2.theirs_ref
  33.0 6.4 %grad.1 = (bf16[4,256,512]{2,1,0:T(8,128)(2,1)}, bf16[1,256,512]{2,1,0:T(8,128)(2,1)S(1)}, f32[16,9,16,128]{3,2,1,0:T(8,128)S(1)}, bf16[24,9,16,128]{3,2,1,0:T(8,128)(2,1)S(1)}) custom-call(s32[4]{0:T(128)S(1)} %dynamic-slice_subtract_fusion.limits_ref, s32[1]{0:T(128)} %bitcast.core_ref, bf16[1,256,512]{2,1,0:T(8,128)(2,1)S(1)} %collective-permute-done.inner_ref, ...), custom_call_target="tpu_custom_call" | custom-call | flops 4831838208 | bytes 8388608 | tf_op jit(solution)/shard_map/grad/pallas_call | solution.py:255
  39.4 1.9 %collective-permute-start.3 = (bf16[24,9,16,128]{3,2,1,0:T(8,128)(2,1)S(1)}, bf16[24,9,16,128]{3,2,1,0:T(8,128)(2,1)S(1)}, u32[]{:S(2)}, u32[]{:S(2)}) collective-permute-start(bf16[24,9,16,128]{3,2,1,0:T(8,128)(2,1)S(1)} %get-tuple-element.13), channel_id=1, source_target_pairs={{0,16},{16,0},{1,17},{17,1},{2,18},{18,2},{3,19},{19,3},{4,20},{20... | collective-permute-start | bytes 2654216 | tf_op jit(solution)/shard_map/ppermute | solution.py:295
  41.3 2.4 %collective-permute-done.3 = bf16[24,9,16,128]{3,2,1,0:T(8,128)(2,1)S(1)} collective-permute-done((bf16[24,9,16,128]{3,2,1,0:T(8,128)(2,1)S(1)}, bf16[24,9,16,128]{3,2,1,0:T(8,128)(2,1)S(1)}, u32[]{:S(2)}, u32[]{:S(2)}) %collective-permute-start.3) | collective-permute-done | bytes 884768 | tf_op jit(solution)/shard_map/ppermute | solution.py:295
  43.8 0.1 add_convert_fusion
  43.9 14.5 %all_to_all.21 = bf16[16,9,16,128]{3,2,1,0:T(8,128)(2,1)S(1)} all-to-all(bf16[16,9,16,128]{3,2,1,0:T(8,128)(2,1)S(1)} %add_convert_fusion), channel_id=1, replica_groups=mesh['z_far'=4,'z_near'=4,'core'=2,'ch_0'=4,'ch_1'=4] {'ch_0','ch_1'}, dimensions={0} | all-to-all | bytes 1179648 | tf_op jit(solution)/shard_map/all_to_all | solution.py:308
  58.4 0.0 copy-start
  58.4 0.1 convert_reduce_fusion
  58.5 12.2 %all_to_all.22.parts_ref = bf16[4,9,16,128]{3,2,1,0:T(8,128)(2,1)S(1)} all-to-all(bf16[4,9,16,128]{3,2,1,0:T(8,128)(2,1)S(1)} %broadcast_in_dim.2), channel_id=1, replica_groups=mesh['z_far'=4,'z_near'=4,'core'=2,'ch_0'=4,'ch_1'=4] {'z_near'}, dimensions={0} | all-to-all | bytes 294912 | tf_op jit(solution)/shard_map/all_to_all | solution.py:308
  70.7 0.7 sum.1
  71.4 12.1 %all-to-all-start.3 = ((bf16[4,9,16,128]{3,2,1,0:T(8,128)(2,1)}), bf16[4,9,16,128]{3,2,1,0:T(8,128)(2,1)S(1)}, u32[]{:S(2)}, u32[]{:S(2)}) async-start(bf16[4,9,16,128]{3,2,1,0:T(8,128)(2,1)} %sum.1), calls=%async_computation.3 | async-start | bytes 294912 | tf_op jit(solution)/shard_map/all_to_all | solution.py:308
  83.5 5.5 %collective-permute-start.4 = (bf16[1,256,512]{2,1,0:T(8,128)(2,1)S(1)}, bf16[1,256,512]{2,1,0:T(8,128)(2,1)S(1)}, u32[]{:S(2)}, u32[]{:S(2)}) collective-permute-start(bf16[1,256,512]{2,1,0:T(8,128)(2,1)S(1)} %get-tuple-element.16), channel_id=1, source_target_pairs={{16,32},{48,64},{80,96},{112,128},{144,160},{176,192},{208,224},{2... | collective-permute-start | bytes 786440 | tf_op jit(solution)/shard_map/ppermute | solution.py:300
  89.0 6.8 %all-to-all-done.3 = bf16[4,9,16,128]{3,2,1,0:T(8,128)(2,1)S(1)} async-done(((bf16[4,9,16,128]{3,2,1,0:T(8,128)(2,1)}), bf16[4,9,16,128]{3,2,1,0:T(8,128)(2,1)S(1)}, u32[]{:S(2)}, u32[]{:S(2)}) %all-to-all-start.3) | async-done | bytes 147488 | tf_op jit(solution)/shard_map/all_to_all | solution.py:308
  95.8 6.4 %collective-permute-start.5 = (f32[9,16,128]{2,1,0:T(8,128)S(1)}, f32[9,16,128]{2,1,0:T(8,128)S(1)}, u32[]{:S(2)}, u32[]{:S(2)}) collective-permute-start(f32[9,16,128]{2,1,0:T(8,128)S(1)} %convert_reduce_fusion.1.mine_ref), channel_id=1, source_target_pairs={{0,16},{16,0},{1,17},{17,1},{2,18},{18,2},{3,19},{19,3},{4,20},{20... | collective-permute-start | bytes 221192 | tf_op jit(solution)/shard_map/ppermute | solution.py:295
  102.1 0.0 collective-permute-done.4.outer_ref
  102.1 0.0 copy-done
  102.2 4.1 %input.1 = bf16[4,256,512]{2,1,0:T(8,128)(2,1)} custom-call(s32[1]{0:T(128)} %bitcast.core_ref, bf16[8,9,16,128]{3,2,1,0:T(8,128)(2,1)S(1)} %slice.9.got_ref, bf16[4,256,512]{2,1,0:T(8,128)(2,1)S(1)} %copy-done, bf16[1,256,512]{2,1,0:T(8,128)(2,1)S(1)} %collective-permute-done.4.outer_ref, bf16[16,9,16,128]{3,2,1,0:T(8,128)(2,1)S(1)} %all_to_all.20.mine_ref, ...), custom_call_target="tpu_custom_call" | custom-call | flops 2415919104 | bytes 4194304 | tf_op jit(solution)/shard_map/input/pallas_call | solution.py:279
  106.2 0.0 collective-permute-done.5.theirs_ref
  106.3 0.7 join.1
  (4 shorter events, 0.1 us)
Async XLA Ops:
  0.6 24.6 %copy-start.1 = (bf16[4,256,512]{2,1,0:T(8,128)(2,1)S(1)}, bf16[4,256,512]{2,1,0:T(8,128)(2,1)}, u32[]{:S(2)}) copy-start(bf16[4,256,512]{2,1,0:T(8,128)(2,1)} %feat_hbm.1) | copy-start | bytes 3145732
  19.8 13.2 %collective-permute-start.2 = (bf16[16,9,16,128]{3,2,1,0:T(8,128)(2,1)S(1)}, bf16[16,9,16,128]{3,2,1,0:T(8,128)(2,1)S(1)}, u32[]{:S(2)}, u32[]{:S(2)}) collective-permute-start(bf16[16,9,16,128]{3,2,1,0:T(8,128)(2,1)S(1)} %all_to_all.20.mine_ref), channel_id=1, source_target_pairs={{0,16},{16,0},{1,17},{17,1},{2,18},{18,2},{3,19},{19,3},{4,20},{20... | collective-permute-start | bytes 1769480 | tf_op jit(solution)/shard_map/ppermute | solution.py:295
  25.3 6.9 %copy-start.2 = (s32[64]{0:T(128)S(1)}, s32[64]{0:T(128)}, u32[]{:S(2)}) copy-start(s32[64]{0:T(128)} %param.7) | copy-start | bytes 772
  25.3 7.7 %collective-permute-start.1 = (bf16[1,256,512]{2,1,0:T(8,128)(2,1)S(1)}, bf16[1,256,512]{2,1,0:T(8,128)(2,1)S(1)}, u32[]{:S(2)}, u32[]{:S(2)}) collective-permute-start(bf16[1,256,512]{2,1,0:T(8,128)(2,1)S(1)} %get-tuple-element.18), channel_id=1, source_target_pairs={{16,32},{48,64},{80,96},{112,128},{144,160},{176,192},{208,224},{2... | collective-permute-start | bytes 786440 | tf_op jit(solution)/shard_map/ppermute | solution.py:300
  28.7 4.3 %collective-permute-start = (bf16[1,256,512]{2,1,0:T(8,128)(2,1)S(1)}, bf16[1,256,512]{2,1,0:T(8,128)(2,1)S(1)}, u32[]{:S(2)}, u32[]{:S(2)}) collective-permute-start(bf16[1,256,512]{2,1,0:T(8,128)(2,1)S(1)} %get-tuple-element.19), channel_id=1, source_target_pairs={{0,16},{16,0},{1,17},{17,1},{2,18},{18,2},{3,19},{19,3},{4,20},{20... | collective-permute-start | bytes 786440 | tf_op jit(solution)/shard_map/ppermute | solution.py:295
  39.4 4.3 %collective-permute-start.3 = (bf16[24,9,16,128]{3,2,1,0:T(8,128)(2,1)S(1)}, bf16[24,9,16,128]{3,2,1,0:T(8,128)(2,1)S(1)}, u32[]{:S(2)}, u32[]{:S(2)}) collective-permute-start(bf16[24,9,16,128]{3,2,1,0:T(8,128)(2,1)S(1)} %get-tuple-element.13), channel_id=1, source_target_pairs={{0,16},{16,0},{1,17},{17,1},{2,18},{18,2},{3,19},{19,3},{4,20},{20... | collective-permute-start | bytes 2654216 | tf_op jit(solution)/shard_map/ppermute | solution.py:295
  58.4 43.8 %copy-start = (bf16[4,256,512]{2,1,0:T(8,128)(2,1)S(1)}, bf16[4,256,512]{2,1,0:T(8,128)(2,1)}, u32[]{:S(2)}) copy-start(bf16[4,256,512]{2,1,0:T(8,128)(2,1)} %get-tuple-element.15.grad_ref) | copy-start | bytes 3145732
  71.4 24.3 %all-to-all-start.3 = ((bf16[4,9,16,128]{3,2,1,0:T(8,128)(2,1)}), bf16[4,9,16,128]{3,2,1,0:T(8,128)(2,1)S(1)}, u32[]{:S(2)}, u32[]{:S(2)}) async-start(bf16[4,9,16,128]{3,2,1,0:T(8,128)(2,1)} %sum.1), calls=%async_computation.3 | async-start | bytes 294912 | tf_op jit(solution)/shard_map/all_to_all | solution.py:308
  83.5 18.6 %collective-permute-start.4 = (bf16[1,256,512]{2,1,0:T(8,128)(2,1)S(1)}, bf16[1,256,512]{2,1,0:T(8,128)(2,1)S(1)}, u32[]{:S(2)}, u32[]{:S(2)}) collective-permute-start(bf16[1,256,512]{2,1,0:T(8,128)(2,1)S(1)} %get-tuple-element.16), channel_id=1, source_target_pairs={{16,32},{48,64},{80,96},{112,128},{144,160},{176,192},{208,224},{2... | collective-permute-start | bytes 786440 | tf_op jit(solution)/shard_map/ppermute | solution.py:300
  95.8 10.5 %collective-permute-start.5 = (f32[9,16,128]{2,1,0:T(8,128)S(1)}, f32[9,16,128]{2,1,0:T(8,128)S(1)}, u32[]{:S(2)}, u32[]{:S(2)}) collective-permute-start(f32[9,16,128]{2,1,0:T(8,128)S(1)} %convert_reduce_fusion.1.mine_ref), channel_id=1, source_target_pairs={{0,16},{16,0},{1,17},{17,1},{2,18},{18,2},{3,19},{19,3},{4,20},{20... | collective-permute-start | bytes 221192 | tf_op jit(solution)/shard_map/ppermute | solution.py:295
